TPU v7x, 256 devices: a whole 4x4x8 slice. The times are simulated.
256 devices in a mesh: gx: 8 (over z), gy: 32 (over y, x, core).
Axes of the slice: x: 4, y: 4, z: 8, core: 2. Of those that a mesh axis runs over, the one named last changes fastest.
Arguments:
- rhs: float32 [8, 32, 1, 3, 200, 128], P('gx', 'gy'), may hold values from -25 to 25
- stiff_inverse: bfloat16 [8, 32, 1, 1200, 1200], P('gx', 'gy'), may hold values from -2 to 6, as said below
- schur: bfloat16 [8, 32, 1, 1200, 1200], P('gx', 'gy'), may hold values from -2 to 6, as said below
- phi: bfloat16 [8, 32, 1, 24, 1200], P('gx', 'gy'), may hold values from -0.1875 to 0.1875
- coarse_inverse: float32 [1536, 1536], P(('gx', 'gy')), may hold values from -2 to 6, as said below
- incidence: int32 [8, 32, 1, 8], P('gx', 'gy'), may hold values from 0 to 511, as said below
- pairing: int32 [8, 32, 1, 3, 200], P('gx', 'gy'), may hold values from 0 to 199, as said below
Outputs:
- multipliers: float32 [8, 32, 1, 3, 200, 128], P('gx', 'gy')
- reduction: float32 [128], replicated
Inputs may be any that keep to these rules, and one draw needn't show every extreme that they name: `stiff_inverse`: each block is symmetric positive definite. `schur`: each block is symmetric positive definite. `coarse_inverse`: symmetric positive definite. `incidence`: the corners of the subdomain grid, periodic in the first two dimensions, under an arbitrary numbering of the 512 nodes: corner c of subdomain (x, y, z) is the grid point (x + c % 2, y + (c // 2) % 2, z + c // 4), and subdomains that share a grid point name the same node. `pairing`: each row over the last dimension is a permutation of 0 to 199.
All inputs are finite; a program needn't handle non-finite values.
Results may differ from a plain program's by a relative error of at most 0.0027.
Values sent between devices are 32-bit elements; how exact they have to be, the bound alone decides.
No kernel may reach another device: no remote copies, remote signals or barrier semaphores. Data moves between devices by JAX's collectives and lax.ppermute only.
A program may use at most 64 MiB of HBM per device.

v0:
```python
import functools

import jax
import jax.numpy as jnp
import numpy as np
from jax import lax
from jax.experimental import pallas as pl
from jax.experimental.pallas import tpu as pltpu
from jax.sharding import Mesh
from jax.sharding import PartitionSpec as P

GY = ("gy_0", "gy_1", "gy_2")
GX_GY = ("gx", "gy_0", "gy_1", "gy_2")
EXACT = lax.Precision.HIGHEST
GX, GYN = 8, 32
CHUNK = 16
NODES = 2 * GX * GYN
E_LANE, ID_LANE = 120, 121
F32, BF16 = jnp.float32, jnp.bfloat16


def corner_lanes():
    lanes = np.full((GX, 128), -1, np.int32)
    shifts = [(0, 0), (1, 0), (-1, 0), (0, 1), (0, -1)]
    for x in range(GX):
        for t, (dx, dy) in enumerate(shifts):
            for c in range(8):
                for i in range(3):
                    node_x = (x + dx + c % 2) % GX
                    j = 1 + dy + (c // 2) % 2
                    lanes[x, t * 24 + 3 * c + i] = j * 64 + i * 16 + node_x * 2 + c // 4
        lanes[x, E_LANE] = 48
        lanes[x, ID_LANE] = 112 + 2 * x
        lanes[x, ID_LANE + 1] = 113 + 2 * x
    return lanes


def in_three(a):
    high = a.astype(BF16)
    rest = a - high.astype(F32)
    middle = rest.astype(BF16)
    low = (rest - middle.astype(F32)).astype(BF16)
    return jnp.concatenate([high, middle, low], axis=0)


def added_up(stacked):
    rows = stacked.shape[0] // 3
    return stacked[:rows] + (stacked[rows : 2 * rows] + stacked[2 * rows :])


def dot(a, b):
    return lax.dot_general(a, b, (((1,), (0,)), ((), ())), preferred_element_type=F32)


def dot_rows(a, b):
    return lax.dot_general(a, b, (((1,), (1,)), ((), ())), preferred_element_type=F32)


def moved_lanes(a, start, to):
    by = (to - start) % 128
    return a if by == 0 else pltpu.roll(a, by, 1)


def lane_group(shape):
    return lax.broadcasted_iota(jnp.int32, shape, 1) // 16


def spread_kernel(got_ref, lanes_ref, out_ref):
    total = jnp.zeros((3 * CHUNK, 256), F32)
    for x in range(GX):
        total += dot(in_three(got_ref[x, 0:CHUNK, :]), lanes_ref[x])
    out_ref[...] = jnp.broadcast_to(added_up(total)[None], out_ref.shape)


def assembled_loads(me, got_ref, loads_ref):
    group = lane_group((CHUNK, 128))
    tiles = [[None] * 4 for _ in range(3)]
    energy = jnp.zeros((CHUNK, 128), F32)

    def left(k):
        return got_ref[lax.rem(me + (k + 31) % GYN, GYN), :, 0:128]

    def right(k):
        return got_ref[lax.rem(me + (k + 31) % GYN, GYN), :, 128:256]

    for k in range(GYN):
        low = right(k - 1) + left(k + 1)
        high = left(k) + right(k - 2)
        load = low + pltpu.roll(high, 64, 1)
        energy += left(k)
        for i in range(3):
            piece = jnp.where(group == k % 8, moved_lanes(load, i * 16, (k % 8) * 16), 0.0)
            old = tiles[i][k // 8]
            tiles[i][k // 8] = piece if old is None else old + piece
    for i in range(3):
        for q in range(4):
            loads_ref[:, i * 512 + q * 128 : i * 512 + (q + 1) * 128] = tiles[i][q]
    return energy


def own_rows(loads_ref, high_ref, low_ref):
    total = jnp.zeros((CHUNK, 48), F32)
    for i in range(3):
        a = loads_ref[:, i * 512 : (i + 1) * 512]
        high = a.astype(BF16)
        low = (a - high.astype(F32)).astype(BF16)
        both = dot_rows(jnp.concatenate([high, low], axis=0), high_ref[i * 48 : (i + 1) * 48, :])
        total += both[:CHUNK] + both[CHUNK:] + dot_rows(high, low_ref[i * 48 : (i + 1) * 48, :])
    return total


def send_rows(rows, energy, sums_ref, out_ref, energy_ref):
    wide = jnp.concatenate([rows, jnp.zeros((CHUNK, 80), F32)], axis=1)
    tile = wide[0:8] + pltpu.roll(wide[8:16], 48, 1)
    row = lax.broadcasted_iota(jnp.int32, (8, 128), 0)
    group = lane_group((8, 128))
    for n in range(2):
        spread_row = jnp.broadcast_to(sums_ref[n : n + 1, :], (8, 128))
        for r in range(8):
            here = (row == r) & (group == 6 + n)
            tile = jnp.where(here, moved_lanes(spread_row, r * 16, 96 + n * 16), tile)
    out_ref[...] = jnp.broadcast_to(tile[None], (GYN, 8, 128))
    energy_ref[...] = energy


def rows_of_sums(tile):
    row = lax.broadcasted_iota(jnp.int32, (8, 128), 0)
    group = lane_group((8, 128))
    out = jnp.zeros((8, 128), F32)
    for n in range(2):
        for r in range(8):
            whole = jnp.broadcast_to(tile[r : r + 1, :], (8, 128))
            out = jnp.where((row == n) & (group == r), moved_lanes(whole, 96 + n * 16, r * 16), out)
    return out


def first_solve_kernel(
    me_ref, got_ref, rows_ref, sums_ref, out_ref, loads_ref, energy_ref, high_ref, low_ref, place_ref, held
):
    me = me_ref[0]
    energy = assembled_loads(me, got_ref, loads_ref)
    group = lane_group((8, 128))
    ids = []
    for q in range(4):
        tile = jnp.zeros((8, 128), F32)
        for n in range(8):
            left = got_ref[lax.rem(me + (q * 8 + n + 31) % GYN, GYN), 0:8, 0:128]
            tile += jnp.where(group == n, moved_lanes(left, 112, n * 16), 0.0)
        ids.append(tile[0:1])
    ids = jnp.concatenate(ids, axis=1).astype(jnp.int32)
    row = lax.broadcasted_iota(jnp.int32, (NODES, NODES), 0)
    by_id = jnp.where(row == ids, 1.0, 0.0).astype(BF16)
    place = (ids % 64 // 2) * 16 + (ids // 64) * 2 + ids % 2
    place_ref[...] = jnp.where(row == place, 1.0, 0.0).astype(BF16)
    for x in range(GX):
        for q in range(4):
            for column in range(3):
                for i in range(3):
                    start = CHUNK + q * 24 + column * 8 + i * 2
                    at = column * 48 + i * 16 + x * 2
                    held[at : at + 2, q * 128 : (q + 1) * 128] = rows_ref[x, start : start + 2, :]
    ordered = added_up(dot(in_three(held[...]), by_id))
    high = ordered.astype(BF16)
    high_ref[...] = high
    low_ref[...] = (ordered - high.astype(F32)).astype(BF16)
    rows = own_rows(loads_ref, high_ref, low_ref)
    send_rows(rows, energy, sums_ref, out_ref, energy_ref)


def next_solve_kernel(me_ref, got_ref, high_ref, low_ref, sums_ref, out_ref, loads_ref, energy_ref):
    energy = assembled_loads(me_ref[0], got_ref, loads_ref)
    rows = own_rows(loads_ref, high_ref, low_ref)
    send_rows(rows, energy, sums_ref, out_ref, energy_ref)


def lane_sum(a, b_ref, shape):
    total = jnp.zeros((CHUNK, 1), F32)
    for i in range(3):
        total += jnp.sum(a[:, i * 512 : (i + 1) * 512] * b_ref[i * CHUNK : (i + 1) * CHUNK, :], axis=1, keepdims=True)
    return jnp.broadcast_to(total, shape)


def pick_kernel(got_ref, loads_ref, energy_ref, place_ref, lanes_ref, *rest):
    before_ref = rest[0] if len(rest) == 3 else None
    out_ref, grid_ref = rest[-2:]
    group = lane_group((CHUNK, 128))
    tiles = [[None] * 4 for _ in range(3)]
    sums = jnp.zeros((8, 128), F32)
    for k in range(GYN):
        rows = got_ref[k]
        sums += rows
        for i in range(3):
            to = (k % 8) * 16
            both = [moved_lanes(rows, i * 16, to), moved_lanes(rows, 48 + i * 16, to)]
            piece = jnp.where(group == k % 8, jnp.concatenate(both, axis=0), 0.0)
            old = tiles[i][k // 8]
            tiles[i][k // 8] = piece if old is None else old + piece
    solution = jnp.concatenate([jnp.concatenate(tiles[i], axis=1) for i in range(3)], axis=0)
    grid_ref[...] = added_up(dot(in_three(solution), place_ref[...]))
    loads = loads_ref[...]
    shape = (CHUNK, 128)
    product = lane_sum(loads, grid_ref, shape)
    mixed = product if before_ref is None else lane_sum(loads, before_ref, shape)
    lane = lax.broadcasted_iota(jnp.int32, shape, 1)
    halves = []
    for half in range(2):
        tile = jnp.zeros(shape, F32)
        for n in range(2):
            for i in range(3):
                at = n * 64 + i * 16
                near = grid_ref[i * CHUNK : (i + 1) * CHUNK, 0:128]
                tile = jnp.where(group == at // 16, moved_lanes(near, (half * 2 + n) * 16, at), tile)
        if half == 0:
            tile = jnp.where(lane == 48, energy_ref[...], tile)
            tile = jnp.where(lane >= 112, jnp.where(lane % 2 == 0, product, mixed), tile)
        halves.append(tile)
    near = in_three(jnp.concatenate(halves, axis=1))
    sums = rows_of_sums(sums)
    for x in range(GX):
        out_ref[x, 0:CHUNK, :] = added_up(dot_rows(near, lanes_ref[x]))
        out_ref[x, CHUNK : CHUNK + 8, :] = sums


def wide_three(a):
    high = a.astype(BF16)
    rest = a - high.astype(F32)
    middle = rest.astype(BF16)
    low = (rest - middle.astype(F32)).astype(BF16)
    return jnp.concatenate([high, middle, low], axis=1)


def wide_sum(a):
    width = a.shape[1] // 3
    return a[:, :width] + (a[:, width : 2 * width] + a[:, 2 * width :])


def dot_columns(a, b):
    return lax.dot_general(a, b, (((0,), (0,)), ((), ())), preferred_element_type=F32)


def faces_of(ref, n, face):
    return ref[n * face : (n + 1) * face, :]


def send_faces(values_ref, table_ref, outs, face):
    up_x, up_y, low_x, low_y = outs
    up_x[...] = wide_sum(dot(table_ref[0], wide_three(faces_of(values_ref, 1, face))))
    up_y[...] = wide_sum(dot(table_ref[1], wide_three(faces_of(values_ref, 3, face))))
    low_x[...] = faces_of(values_ref, 0, face)
    low_y[...] = faces_of(values_ref, 2, face)


def jump_faces(values_ref, received, table_ref, face):
    below_x, below_y, above_x, above_y = received
    up = [wide_sum(dot_columns(table_ref[a], wide_three(ref[...]))) for a, ref in ((0, above_x), (1, above_y))]
    own = [faces_of(values_ref, n, face) for n in range(6)]
    return [
        own[0] - below_x[...], own[1] - up[0], own[2] - below_y[...], own[3] - up[1], 0.0 * own[4], 0.0 * own[5]
    ]


def column_sum(a, b):
    return jnp.sum(a * b, axis=0, keepdims=True)


def write_rows(ref, rows):
    ref[...] = jnp.concatenate([*rows, jnp.zeros((8 - len(rows), rows[0].shape[1]), F32)], axis=0)


def loads_of(solved_ref, reach_ref, energy, ids, face):
    loads = jnp.zeros((128, 3 * 128), F32)
    for n in range(4):
        loads += dot(reach_ref[n], wide_three(faces_of(solved_ref, n, face)))
    loads = 0.5 * wide_sum(loads)
    row = lax.broadcasted_iota(jnp.int32, (128, 128), 0)
    loads = jnp.where(row == E_LANE, energy, loads)
    if ids is not None:
        number = jnp.where(row == ID_LANE, ids[0], jnp.where(row == ID_LANE + 1, ids[1], 0))
        loads = loads + number.astype(F32)
    return loads.T


def corner_faces(corners, reach_ref):
    pieces = wide_three(corners)
    return [wide_sum(dot_columns(reach_ref[n], pieces)) for n in range(4)]


def coupling_of(phi_ref, n, face):
    return phi_ref[...].astype(F32)[:, n * face : (n + 1) * face]


def start_kernel(rhs_ref, pairing_ref, phi_ref, plus_x, plus_y, minus_x, minus_y, table_ref):
    face = rhs_ref.shape[1]
    row = lax.broadcasted_iota(jnp.int32, (face, face), 0)
    for a, (plus, minus) in enumerate(((plus_x, minus_x), (plus_y, minus_y))):
        table = jnp.where(row == pairing_ref[a : a + 1, :], 1.0, 0.0).astype(BF16)
        table_ref[a] = table
        plus[0:face, :] = wide_sum(dot(table, wide_three(rhs_ref[a])))
        moved = dot_rows(coupling_of(phi_ref, 2 * a + 1, face).astype(BF16), table)
        moved = jnp.concatenate([moved, jnp.zeros((24, 256 - face), F32)], axis=1)
        plus[face : face + 24, :] = moved[:, :128]
        plus[face + 24 : face + 48, :] = moved[:, 128:]
        minus[...] = coupling_of(phi_ref, 2 * a, face)


def first_kernel(
    ids_ref, rhs_ref, below_x, below_y, above_x, above_y, phi_ref, table_ref, matrix_ref, rows_ref,
    half_ref, solved_ref, reach_ref, up_x, up_y, low_x, low_y, out_ref,
):
    face = rhs_ref.shape[1]
    none = jnp.zeros((face, 128), F32)
    half = [
        -0.5 * below_x[0:face, :], 0.5 * rhs_ref[0], -0.5 * below_y[0:face, :], 0.5 * rhs_ref[1], none, 0.0 * rhs_ref[2]
    ]
    for n in range(6):
        half_ref[n * face : (n + 1) * face, :] = half[n]
    solved_ref[...] = dot(matrix_ref[...], half_ref[...].astype(BF16))
    send_faces(solved_ref, table_ref, (up_x, up_y, low_x, low_y), face)

    def near(n, slot, other):
        parts = [coupling_of(phi_ref, n, face)] + [jnp.zeros((24, face), F32)] * 4 + [jnp.zeros((8, face), F32)]
        parts[slot] = -other
        reach_ref[n] = jnp.concatenate(parts, axis=0).astype(BF16)

    for a, (below, above) in enumerate(((below_x, above_x), (below_y, above_y))):
        near(2 * a + 1, 1 + 2 * a, dot(above[...].astype(BF16), table_ref[a]))
        under = jnp.concatenate([below[face : face + 24, :], below[face + 24 : face + 48, :]], axis=1)
        near(2 * a, 2 + 2 * a, under[:, :face])
    energy = column_sum(half_ref[...], solved_ref[...])
    loads = loads_of(solved_ref, reach_ref, energy, (ids_ref[0], ids_ref[4]), face)
    for x in range(GX):
        out_ref[x, 0:CHUNK, :] = loads[x * CHUNK : (x + 1) * CHUNK]
        out_ref[x, CHUNK : CHUNK + 96, :] = rows_ref[...]


def stretch_kernel(
    solved_ref, below_x, below_y, above_x, above_y, table_ref, matrix_ref, *rest
):
    face = below_x.shape[0]
    old = rest[:2] if len(rest) == 9 else None
    field_ref, stretched_ref, up_x, up_y, low_x, low_y, sums_ref = rest[-7:]
    jumped = jump_faces(solved_ref, (below_x, below_y, above_x, above_y), table_ref, face)
    for n in range(6):
        field_ref[n * face : (n + 1) * face, :] = 0.5 * jumped[n]
    stretched_ref[...] = dot(matrix_ref[...], field_ref[...].astype(BF16))
    send_faces(stretched_ref, table_ref, (up_x, up_y, low_x, low_y), face)
    rows = [column_sum(field_ref[...], stretched_ref[...])]
    if old is not None:
        old_field, old_stretched = old
        rows.append(
            column_sum(field_ref[...], old_stretched[...]) + column_sum(old_field[...], stretched_ref[...])
        )
    write_rows(sums_ref, rows)


def returned(got_ref):
    corners = jnp.concatenate([got_ref[x, 0:CHUNK, :] for x in range(GX)], axis=0).T
    sums = got_ref[0, CHUNK:, :]
    for x in range(1, GX):
        sums += got_ref[x, CHUNK:, :]
    return corners, sums


def turn_kernel(
    got_ref, half_ref, field_ref, stretched_ref, below_x, below_y, above_x, above_y, table_ref, reach_ref, matrix_ref,
    next_ref, solved_ref, image_ref, corners_ref, scalars_ref, up_x, up_y, low_x, low_y, out_ref,
):
    face = below_x.shape[0]
    corners, sums = returned(got_ref)
    corners_ref[...] = corners
    energy = corners[E_LANE : E_LANE + 1]
    curvature = sums[0:1] + corners[E_LANE + 1 : E_LANE + 2]
    alpha = energy / curvature
    write_rows(scalars_ref, [energy, curvature, alpha])
    jumped = jump_faces(stretched_ref, (below_x, below_y, above_x, above_y), table_ref, face)
    coarse = corner_faces(corners, reach_ref)
    for n in range(6):
        at = slice(n * face, (n + 1) * face)
        image = jumped[n] + coarse[n] if n < 4 else jumped[n]
        image_ref[at, :] = image
        next_ref[at, :] = half_ref[at, :] - (0.5 * alpha) * image
    solved_ref[...] = dot(matrix_ref[...], next_ref[...].astype(BF16))
    send_faces(solved_ref, table_ref, (up_x, up_y, low_x, low_y), face)
    energy = column_sum(next_ref[...], solved_ref[...])
    loads = loads_of(solved_ref, reach_ref, energy, None, face)
    for x in range(GX):
        out_ref[x] = loads[x * CHUNK : (x + 1) * CHUNK]


def last_kernel(
    got_ref, half_ref, field_ref, fresh_ref, stretched_ref, below_x, below_y, above_x, above_y, image_ref,
    corners_ref, scalars_ref, table_ref, reach_ref, matrix_ref, multipliers_ref, out_ref, held_ref,
):
    face = below_x.shape[0]
    corners, sums = returned(got_ref)
    start, curvature, alpha = scalars_ref[0:1], scalars_ref[1:2], scalars_ref[2:3]
    energy = corners[E_LANE : E_LANE + 1]
    ratio = energy / start
    mixed = sums[1:2] + 2.0 * corners[E_LANE + 2 : E_LANE + 3]
    curvature = sums[0:1] + corners[E_LANE + 1 : E_LANE + 2] + ratio * mixed + ratio * ratio * curvature
    step = energy / curvature
    jumped = jump_faces(stretched_ref, (below_x, below_y, above_x, above_y), table_ref, face)
    coarse = corner_faces(corners, reach_ref)
    for n in range(6):
        at = slice(n * face, (n + 1) * face)
        image = jumped[n] + coarse[n] if n < 4 else jumped[n]
        held_ref[at, :] = half_ref[at, :] - (0.5 * step) * (image + ratio * image_ref[at, :])
    for a in range(3):
        at = slice((2 * a + 1) * face, (2 * a + 2) * face)
        first = field_ref[at, :]
        multipliers_ref[a] = alpha * first + step * (fresh_ref[at, :] + ratio * first)
    solved = dot(matrix_ref[...], held_ref[...].astype(BF16))
    out_ref[...] = jnp.broadcast_to(column_sum(held_ref[...], solved)[None], out_ref.shape)


def pass_on_kernel(got_ref, out_ref):
    total = jnp.sum(got_ref[...], axis=0)
    out_ref[...] = jnp.broadcast_to(total[None], out_ref.shape)


def finish_kernel(got_ref, scalars_ref, out_ref):
    out_ref[...] = (jnp.sum(got_ref[...], axis=0) / jnp.broadcast_to(scalars_ref[0:1], (8, 128)))[0:1]


def call(kernel, outs, smem=0, scratch=(), flops=2_000_000):
    vmem = pl.BlockSpec(memory_space=pltpu.VMEM)

    def run(*operands, after=()):
        many = len(operands)

        def body(*refs):
            kernel(*refs[:many], *refs[many + len(after) :])

        specs = [pl.BlockSpec(memory_space=pltpu.SMEM)] * smem + [vmem] * (many - smem)
        return pl.pallas_call(
            body,
            name=kernel.__name__,
            out_shape=[jax.ShapeDtypeStruct(s, d) for s, d in outs],
            in_specs=specs + [pl.BlockSpec(memory_space=pl.ANY)] * len(after),
            out_specs=[vmem] * len(outs),
            scratch_shapes=list(scratch),
            cost_estimate=pl.CostEstimate(flops=flops, bytes_accessed=1_000_000, transcendentals=0),
        )(*operands, *after)

    return run


SENT = [((GYN, 8, 128), F32), ((CHUNK, 3 * NODES), F32), ((CHUNK, 128), F32)]
spread = call(spread_kernel, [((GYN, CHUNK, 256), F32)])
first_solve = call(
    first_solve_kernel,
    SENT + [((144, NODES), BF16), ((144, NODES), BF16), ((NODES, NODES), BF16)],
    smem=1,
    scratch=[pltpu.VMEM((144, NODES), F32)],
)
next_solve = call(next_solve_kernel, SENT, smem=1)
pick = call(pick_kernel, [((GX, CHUNK + 8, 128), F32), ((3 * CHUNK, NODES), F32)])


def passed_along(array, axis, by):
    peers = lax.axis_size(axis)
    return lax.ppermute(array, axis, [(i, (i + by) % peers) for i in range(peers)])


def passed_both_ways(up_x, up_y, low_x, low_y):
    return (
        passed_along(up_x, "gx", 1),
        passed_along(up_y, GY, 1),
        passed_along(low_x, "gx", -1),
        passed_along(low_y, GY, -1),
    )


def exchanged(array, axis):
    return lax.all_to_all(array, axis, split_axis=0, concat_axis=0, tiled=True)


def local(rhs, stiff_inverse, schur, phi, coarse_inverse, incidence, pairing):
    face = rhs.shape[4]
    interface = 6 * face
    rhs = rhs[0, 0, 0]
    stiffness = stiff_inverse[0, 0, 0]
    schur_block = schur[0, 0, 0]
    pairing = pairing[0, 0, 0]
    coupling = phi[0, 0, 0]
    me = lax.axis_index(GY).astype(jnp.int32).reshape(1)
    lanes = (jnp.asarray(corner_lanes())[:, :, None] == jnp.arange(256)[None, None, :]).astype(BF16)
    mine = coarse_inverse.reshape(2, 3, 4, 128, 3)
    mine = jnp.transpose(mine, (2, 4, 1, 0, 3)).reshape(12, 6, 128)
    mine = jnp.concatenate([mine, jnp.zeros((12, 2, 128), F32)], axis=1).reshape(96, 128)

    whole, faces = ((interface, 128), F32), [((face, 128), F32)] * 4
    big = 2 * interface * interface * 128
    *sent, table = call(
        start_kernel, [((face + 48, 128), F32)] * 2 + [((24, face), F32)] * 2 + [((2, face, face), BF16)]
    )(rhs, pairing, coupling)
    received = passed_both_ways(*sent)
    half, solved, reach, *sent, message = call(
        first_kernel,
        [whole, whole, ((4, 128, face), BF16), *faces, ((GX, CHUNK + 96, 128), F32)],
        smem=1,
        flops=big,
    )(incidence[0, 0, 0], rhs, *received, coupling, table, schur_block, mine)
    received = passed_both_ways(*sent)
    first_rows = exchanged(message, "gx")
    (sent,) = spread(first_rows, lanes, after=received)
    field, stretched, *faces_sent, sums = call(stretch_kernel, [whole, whole, *faces, ((8, 128), F32)], flops=big)(
        solved, *received, table, stiffness
    )
    received = passed_both_ways(*faces_sent)
    arrived = exchanged(sent, GY)
    sent, loads, energy, high, low, place = first_solve(me, arrived, first_rows, sums)
    back, grid = pick(exchanged(sent, GY), loads, energy, place, lanes, after=received)
    back = exchanged(back, "gx")
    half, solved, image, corners, scalars, *sent, message = call(
        turn_kernel,
        [whole, whole, whole, ((128, 128), F32), ((8, 128), F32), *faces, ((GX, CHUNK, 128), F32)],
        flops=big,
    )(back, half, field, stretched, *received, table, reach, schur_block)

    received = passed_both_ways(*sent)
    (sent,) = spread(exchanged(message, "gx"), lanes, after=received)
    fresh, fresh_stretched, *faces_sent, sums = call(
        stretch_kernel, [whole, whole, *faces, ((8, 128), F32)], flops=big
    )(solved, *received, table, stiffness, field, stretched)
    received = passed_both_ways(*faces_sent)
    sent, loads, energy = next_solve(me, exchanged(sent, GY), high, low, sums)
    back, _ = pick(exchanged(sent, GY), loads, energy, place, lanes, grid, after=received)
    back = exchanged(back, "gx")
    multipliers, energy = call(
        last_kernel,
        [((3, face, 128), F32), ((GX, 8, 128), F32)],
        scratch=[pltpu.VMEM((interface, 128), F32)],
        flops=big,
    )(
        back, half, field, fresh, fresh_stretched, *received, image, corners, scalars, table, reach, schur_block
    )
    (energy,) = call(pass_on_kernel, [((GYN, 8, 128), F32)])(exchanged(energy, "gx"))
    (reduction,) = call(finish_kernel, [((1, 128), F32)])(exchanged(energy, GY), scalars)
    return (multipliers[None, None, None], reduction[0])


def solution(mesh):
    finer = Mesh(mesh.devices.reshape(mesh.shape["gx"], 4, 4, 2), ("gx", "gy_0", "gy_1", "gy_2"))
    in_specs = (
        P("gx", GY, None, None, None, None),
        P("gx", GY, None, None, None),
        P("gx", GY, None, None, None),
        P("gx", GY, None, None, None),
        P(GX_GY, None),
        P("gx", GY, None, None),
        P("gx", GY, None, None, None),
    )
    out_specs = (P("gx", GY, None, None, None, None), P())
    return jax.shard_map(local, mesh=finer, in_specs=in_specs, out_specs=out_specs, check_vma=False)
```

profile of v0, /device:TPU:1, one launch (start us, length us, event | category | flops | bytes accessed | tf_op | source)
XLA Modules:
  0.0 213.0 jit_solution(5974679542932677104)
XLA Ops:
  0.6 1.3 copy.14
  1.9 2.0 start_kernel.1
  3.9 2.5 %collective-permute-start = (f32[248,128]{1,0:T(8,128)}, f32[248,128]{1,0:T(8,128)S(1)}, u32[]{:S(2)}, u32[]{:S(2)}) collective-permute-start(f32[248,128]{1,0:T(8,128)} %get-tuple-element.53), channel_id=1, source_target_pairs={{0,32},{32,64},{64,96},{96,128},{128,160},{160,192},{192,224},{224... | collective-permute-start | bytes 380936 | tf_op jit(solution)/shard_map/ppermute | solution.py:462
  6.3 2.0 collective-permute-start.1
  8.4 3.7 %collective-permute-start.2 = (f32[24,200]{1,0:T(8,128)}, f32[24,200]{1,0:T(8,128)S(1)}, u32[]{:S(2)}, u32[]{:S(2)}) collective-permute-start(f32[24,200]{1,0:T(8,128)} %get-tuple-element.55), channel_id=1, source_target_pairs={{0,224},{32,0},{64,32},{96,64},{128,96},{160,128},{192,160},{224,1... | collective-permute-start | bytes 57608 | tf_op jit(solution)/shard_map/ppermute | solution.py:462
  12.1 2.2 %reshape.18 = f32[2,3,4,128,3]{4,3,2,1,0:T(8,128)S(1)} reshape(f32[6,1536]{1,0:T(8,128)} %param.12) | data formatting | bytes 73728 | tf_op jit(solution)/shard_map/reshape | solution.py:488
  14.3 0.5 copy.11
  14.8 0.6 pad_bitcast_fusion.refs_9_
  15.5 0.5 copy-done.24
  16.2 5.0 %first_kernel.1 = (f32[1200,128]{1,0:T(8,128)}, f32[1200,128]{1,0:T(8,128)}, bf16[4,128,200]{2,1,0:T(8,128)(2,1)}, f32[200,128]{1,0:T(8,128)}, f32[200,128]{1,0:...) custom-call(s32[8]{0:T(128)} %bitcast.25, f32[3,200,128]{2,1,0:T(8,128)} %bitcast.21, ...), custom_call_target="tpu_custom_call" | custom-call | flops 368640000 | bytes 1000000 | tf_op jit(solution)/shard_map/first_kernel/pallas_call | solution.py:435
  21.2 5.9 %all-to-all-start = ((f32[8,112,128]{2,1,0:T(8,128)}), f32[8,112,128]{2,1,0:T(8,128)S(1)}, u32[]{:S(2)}, u32[]{:S(2)}) async-start(f32[8,112,128]{2,1,0:T(8,128)} %get-tuple-element.58), calls=%async_computation | async-start | bytes 917504 | tf_op jit(solution)/shard_map/all_to_all | solution.py:475
  27.1 1.5 collective-permute-start.4
  28.5 2.2 %collective-permute-start.5 = (f32[200,128]{1,0:T(8,128)}, f32[200,128]{1,0:T(8,128)S(1)}, u32[]{:S(2)}, u32[]{:S(2)}) collective-permute-start(f32[200,128]{1,0:T(8,128)} %get-tuple-element.60), channel_id=1, source_target_pairs={{0,1},{1,2},{2,3},{3,4},{4,5},{5,6},{6,7},{7,8},{8,9},{9,10},{10,1... | collective-permute-start | bytes 307208 | tf_op jit(solution)/shard_map/ppermute | solution.py:462
  30.8 1.0 collective-permute-start.6
  31.7 2.6 %collective-permute-start.7 = (f32[200,128]{1,0:T(8,128)}, f32[200,128]{1,0:T(8,128)S(1)}, u32[]{:S(2)}, u32[]{:S(2)}) collective-permute-start(f32[200,128]{1,0:T(8,128)} %get-tuple-element.62), channel_id=1, source_target_pairs={{0,31},{1,0},{2,1},{3,2},{4,3},{5,4},{6,5},{7,6},{8,7},{9,8},{10,9... | collective-permute-start | bytes 307208 | tf_op jit(solution)/shard_map/ppermute | solution.py:462
  34.3 1.0 fusion.refs_1_.refs_4_
  35.3 3.0 %collective-permute-done.4.refs_2_.refs_1_ = f32[200,128]{1,0:T(8,128)S(1)} collective-permute-done((f32[200,128]{1,0:T(8,128)}, f32[200,128]{1,0:T(8,128)S(1)}, u32[]{:S(2)}, u32[]{:S(2)}) %collective-permute-start.4) | collective-permute-done | bytes 102432 | tf_op jit(solution)/shard_map/ppermute | solution.py:462
  38.4 0.6 copy-done.13
  39.1 0.8 copy-done
  39.9 2.3 %spread_kernel.2 = f32[32,16,256]{2,1,0:T(8,128)} custom-call(f32[8,112,128]{2,1,0:T(8,128)} %copy-done, bf16[8,128,256]{2,1,0:T(8,128)(2,1)} %fusion.refs_1_.refs_4_, f32[200,128]{1,0:T(8,128)} %copy-done.13, f32[200,128]{1,0:T(8,128)} %copy-done.14, f32[200,128]{1,0:T(8,128)} %copy-done.15, f32[200,128]{1,0:T(8,128)} %copy-done.16), custom_call_target="tpu_custom_call" | custom-call | flops 2000000 | bytes 1000000 | tf_op jit(solution)/shard_map/spread_kernel/pallas_call | solution.py:435
  42.1 12.9 %all-to-all-start.1 = ((f32[32,16,256]{2,1,0:T(8,128)}), f32[32,16,256]{2,1,0:T(8,128)S(1)}, u32[]{:S(2)}, u32[]{:S(2)}) async-start(f32[32,16,256]{2,1,0:T(8,128)} %spread_kernel.2), calls=%async_computation.1 | async-start | bytes 1048576 | tf_op jit(solution)/shard_map/all_to_all | solution.py:475
  55.1 4.7 %stretch_kernel.2 = (f32[1200,128]{1,0:T(8,128)}, f32[1200,128]{1,0:T(8,128)}, f32[200,128]{1,0:T(8,128)}, f32[200,128]{1,0:T(8,128)}, f32[200,128]{1,0:T(8,128)}, /*index=5*/f32[200,128]{1,0:T(8,128)}, f32[8,128]{1,0:T(8,128)}) custom-call(f32[1200,128]{1,0:T(8,128)} %get-tuple-element.63.refs_0_, f32[200,128]{1,0:T(8,128)} %copy-done.13, ...), custom_call_target="tpu_custom_call" | custom-call | flops 368640000 | bytes 1000000 | tf_op jit(solution)/shard_map/stretch_kernel/pallas_call | solution.py:435
  59.7 6.8 %all-to-all-done.1.refs_1_ = f32[32,16,256]{2,1,0:T(8,128)S(1)} async-done(((f32[32,16,256]{2,1,0:T(8,128)}), f32[32,16,256]{2,1,0:T(8,128)S(1)}, u32[]{:S(2)}, u32[]{:S(2)}) %all-to-all-start.1) | async-done | bytes 524320 | tf_op jit(solution)/shard_map/all_to_all | solution.py:475
  66.5 0.8 copy-done.1
  67.3 3.0 %first_solve_kernel.1 = (f32[32,8,128]{2,1,0:T(8,128)}, f32[16,1536]{1,0:T(8,128)}, f32[16,128]{1,0:T(8,128)}, bf16[144,512]{1,0:T(8,128)(2,1)}, bf16[144,512]{1,0:T(8,128)(2,1)}, /*index=5*/bf16[512,512]{1,0:T(8,128)(2,1)}) custom-call(s32[1]{0:T(128)} %bitcast.refs_0_, f32[32,16,256]{2,1,0:T(8,128)} %copy-done.1, f32[8,112,128]{2,1,0:T(8,128)} %copy-done, ...), custom_call_target="tpu_custom_call" | custom-call | flops 2000000 | bytes 1000000 | tf_op jit(solution)/shard_map/first_solve_kernel/pallas_call | solution.py:435
  70.3 3.9 %all-to-all-start.2 = ((f32[32,8,128]{2,1,0:T(8,128)}), f32[32,8,128]{2,1,0:T(8,128)S(1)}, u32[]{:S(2)}, u32[]{:S(2)}) async-start(f32[32,8,128]{2,1,0:T(8,128)} %get-tuple-element.65), calls=%async_computation.2 | async-start | bytes 262144 | tf_op jit(solution)/shard_map/all_to_all | solution.py:475
  74.4 1.9 collective-permute-start.9
  76.3 2.5 %collective-permute-start.10 = (f32[200,128]{1,0:T(8,128)}, f32[200,128]{1,0:T(8,128)S(1)}, u32[]{:S(2)}, u32[]{:S(2)}) collective-permute-start(f32[200,128]{1,0:T(8,128)} %get-tuple-element.71), channel_id=1, source_target_pairs={{0,224},{32,0},{64,32},{96,64},{128,96},{160,128},{192,160},{224,1... | collective-permute-start | bytes 307208 | tf_op jit(solution)/shard_map/ppermute | solution.py:462
  78.9 0.9 collective-permute-done.8.refs_5_.refs_4_
  79.8 1.3 collective-permute-done.10.refs_7_.refs_6_
  81.1 2.1 collective-permute-done.11.refs_8_.refs_7_
  83.2 0.6 copy-done.10
  83.8 2.7 %pick_kernel.2 = (f32[8,24,128]{2,1,0:T(8,128)}, f32[48,512]{1,0:T(8,128)}) custom-call(f32[32,8,128]{2,1,0:T(8,128)} %copy-done.4, f32[16,1536]{1,0:T(8,128)} %get-tuple-element.66.refs_1_, f32[16,128]{1,0:T(8,128)} %get-tuple-element.67.refs_2_, bf16[512,512]{1,0:T(8,128)(2,1)} %get-tuple-element.68.refs_3_, bf16[8,128,256]{2,1,0:T(8,128)(2,1)} %fusion.refs_1_.refs_4_, ...), custom_call_target="tpu_custom_call" | custom-call | flops 2000000 | bytes 1000000 | tf_op jit(solution)/shard_map/pick_kernel/pallas_call | solution.py:435
  86.6 12.3 %all_to_all.50.refs_0_ = f32[8,24,128]{2,1,0:T(8,128)} all-to-all(f32[8,24,128]{2,1,0:T(8,128)} %get-tuple-element.73), channel_id=1, replica_groups=mesh['gx'=8,'gy_0'=4,'gy_1'=4,'gy_2'=2] {'gx'}, dimensions={0} | all-to-all | bytes 196608 | tf_op jit(solution)/shard_map/all_to_all | solution.py:475
  98.9 5.7 %turn_kernel.1 = (f32[1200,128]{1,0:T(8,128)}, f32[1200,128]{1,0:T(8,128)}, f32[1200,128]{1,0:T(8,128)}, f32[128,128]{1,0:T(8,128)}, f32[8,128]{1,0:T(8,128)}, /...) custom-call(f32[8,24,128]{2,1,0:T(8,128)} %all_to_all.50.refs_0_, ...), custom_call_target="tpu_custom_call" | custom-call | flops 368640000 | bytes 1000000 | tf_op jit(solution)/shard_map/turn_kernel/pallas_call | solution.py:435
  104.5 3.3 %all-to-all-start.4 = ((f32[8,16,128]{2,1,0:T(8,128)}), f32[8,16,128]{2,1,0:T(8,128)S(1)}, u32[]{:S(2)}, u32[]{:S(2)}) async-start(f32[8,16,128]{2,1,0:T(8,128)} %get-tuple-element.78), calls=%async_computation.4 | async-start | bytes 131072 | tf_op jit(solution)/shard_map/all_to_all | solution.py:475
  107.9 1.4 collective-permute-start.12
  109.3 2.5 %collective-permute-start.13 = (f32[200,128]{1,0:T(8,128)}, f32[200,128]{1,0:T(8,128)S(1)}, u32[]{:S(2)}, u32[]{:S(2)}) collective-permute-start(f32[200,128]{1,0:T(8,128)} %get-tuple-element.80), channel_id=1, source_target_pairs={{0,1},{1,2},{2,3},{3,4},{4,5},{5,6},{6,7},{7,8},{8,9},{9,10},{10,1... | collective-permute-start | bytes 307208 | tf_op jit(solution)/shard_map/ppermute | solution.py:462
  111.8 1.1 collective-permute-start.14
  112.9 1.4 collective-permute-start.15
  114.3 1.7 collective-permute-done.14.refs_4_.refs_3_
  116.0 1.5 collective-permute-done.15.refs_5_.refs_4_
  117.5 0.6 copy-done.12
  118.2 0.6 copy-done.21
  118.8 2.2 %spread_kernel.3 = f32[32,16,256]{2,1,0:T(8,128)} custom-call(f32[8,16,128]{2,1,0:T(8,128)} %copy-done.21, bf16[8,128,256]{2,1,0:T(8,128)(2,1)} %fusion.refs_1_.refs_4_, f32[200,128]{1,0:T(8,128)} %copy-done.7, f32[200,128]{1,0:T(8,128)} %copy-done.9, f32[200,128]{1,0:T(8,128)} %copy-done.11, f32[200,128]{1,0:T(8,128)} %copy-done.12), custom_call_target="tpu_custom_call" | custom-call | flops 2000000 | bytes 1000000 | tf_op jit(solution)/shard_map/spread_kernel/pallas_call | solution.py:435
  120.9 10.7 %all-to-all-start.5 = ((f32[32,16,256]{2,1,0:T(8,128)}), f32[32,16,256]{2,1,0:T(8,128)S(1)}, u32[]{:S(2)}, u32[]{:S(2)}) async-start(f32[32,16,256]{2,1,0:T(8,128)} %spread_kernel.3), calls=%async_computation.5 | async-start | bytes 1048576 | tf_op jit(solution)/shard_map/all_to_all | solution.py:475
  131.6 4.9 %stretch_kernel.3 = (f32[1200,128]{1,0:T(8,128)}, f32[1200,128]{1,0:T(8,128)}, f32[200,128]{1,0:T(8,128)}, f32[200,128]{1,0:T(8,128)}, f32[200,128]{1,0:T(8,128)}, /*index=5*/f32[200,128]{1,0:T(8,128)}, f32[8,128]{1,0:T(8,128)}) custom-call(f32[1200,128]{1,0:T(8,128)} %get-tuple-element.85.refs_0_, f32[200,128]{1,0:T(8,128)} %copy-done.7, ...), custom_call_target="tpu_custom_call" | custom-call | flops 368640000 | bytes 1000000 | tf_op jit(solution)/shard_map/stretch_kernel/pallas_call | solution.py:435
  136.5 6.5 %all-to-all-done.5.refs_1_ = f32[32,16,256]{2,1,0:T(8,128)S(1)} async-done(((f32[32,16,256]{2,1,0:T(8,128)}), f32[32,16,256]{2,1,0:T(8,128)S(1)}, u32[]{:S(2)}, u32[]{:S(2)}) %all-to-all-start.5) | async-done | bytes 524320 | tf_op jit(solution)/shard_map/all_to_all | solution.py:475
  143.0 0.8 copy-done.2
  143.8 2.4 %next_solve_kernel.1 = (f32[32,8,128]{2,1,0:T(8,128)}, f32[16,1536]{1,0:T(8,128)}, f32[16,128]{1,0:T(8,128)}) custom-call(s32[1]{0:T(128)} %bitcast.refs_0_, f32[32,16,256]{2,1,0:T(8,128)} %copy-done.2, bf16[144,512]{1,0:T(8,128)(2,1)} %get-tuple-element.83.refs_2_, bf16[144,512]{1,0:T(8,128)(2,1)} %get-tuple-element.84.refs_3_, ...), custom_call_target="tpu_custom_call" | custom-call | flops 2000000 | bytes 1000000 | tf_op jit(solution)/shard_map/next_solve_kernel/pallas_call | solution.py:435
  146.2 3.9 %all-to-all-start.6 = ((f32[32,8,128]{2,1,0:T(8,128)}), f32[32,8,128]{2,1,0:T(8,128)S(1)}, u32[]{:S(2)}, u32[]{:S(2)}) async-start(f32[32,8,128]{2,1,0:T(8,128)} %get-tuple-element.87), calls=%async_computation.6 | async-start | bytes 262144 | tf_op jit(solution)/shard_map/all_to_all | solution.py:475
  150.5 1.9 collective-permute-start.17
  152.4 2.3 %collective-permute-start.18 = (f32[200,128]{1,0:T(8,128)}, f32[200,128]{1,0:T(8,128)S(1)}, u32[]{:S(2)}, u32[]{:S(2)}) collective-permute-start(f32[200,128]{1,0:T(8,128)} %get-tuple-element.93), channel_id=1, source_target_pairs={{0,224},{32,0},{64,32},{96,64},{128,96},{160,128},{192,160},{224,1... | collective-permute-start | bytes 307208 | tf_op jit(solution)/shard_map/ppermute | solution.py:462
  154.7 0.9 collective-permute-done.16.refs_6_.refs_5_
  155.7 1.3 collective-permute-done.18.refs_8_.refs_7_
  156.9 2.1 collective-permute-done.19.refs_9_.refs_8_
  159.1 0.6 copy-done.20
  159.7 2.7 %pick_kernel.3 = (f32[8,24,128]{2,1,0:T(8,128)}, f32[48,512]{1,0:T(8,128)}) custom-call(f32[32,8,128]{2,1,0:T(8,128)} %copy-done.3, f32[16,1536]{1,0:T(8,128)} %get-tuple-element.88.refs_1_, f32[16,128]{1,0:T(8,128)} %get-tuple-element.89.refs_2_, bf16[512,512]{1,0:T(8,128)(2,1)} %get-tuple-element.68.refs_3_, bf16[8,128,256]{2,1,0:T(8,128)(2,1)} %fusion.refs_1_.refs_4_, ...), custom_call_target="tpu_custom_call" | custom-call | flops 2000000 | bytes 1000000 | tf_op jit(solution)/shard_map/pick_kernel/pallas_call | solution.py:435
  162.5 14.5 %all_to_all.51.refs_0_ = f32[8,24,128]{2,1,0:T(8,128)} all-to-all(f32[8,24,128]{2,1,0:T(8,128)} %get-tuple-element.95), channel_id=1, replica_groups=mesh['gx'=8,'gy_0'=4,'gy_1'=4,'gy_2'=2] {'gx'}, dimensions={0} | all-to-all | bytes 196608 | tf_op jit(solution)/shard_map/all_to_all | solution.py:475
  176.9 5.2 %last_kernel.1 = (f32[3,200,128]{2,1,0:T(8,128)}, f32[8,8,128]{2,1,0:T(8,128)}) custom-call(f32[8,24,128]{2,1,0:T(8,128)} %all_to_all.51.refs_0_, f32[1200,128]{1,0:T(8,128)} %get-tuple-element.96.refs_1_, f32[1200,128]{1,0:T(8,128)} %get-tuple-element.75.refs_2_.refs_7_, f32[1200,128]{1,0:T(8,128)} %get-tuple-element.97.refs_3_, ...), custom_call_target="tpu_custom_call" | custom-call | flops 368640000 | bytes 1000000 | tf_op jit(solution)/shard_map/last_kernel/pallas_call | solution.py:435
  182.1 10.8 %all_to_all.52.refs_0_ = f32[8,8,128]{2,1,0:T(8,128)} all-to-all(f32[8,8,128]{2,1,0:T(8,128)} %get-tuple-element.103), channel_id=1, replica_groups=mesh['gx'=8,'gy_0'=4,'gy_1'=4,'gy_2'=2] {'gx'}, dimensions={0} | all-to-all | bytes 65536 | tf_op jit(solution)/shard_map/all_to_all | solution.py:475
  192.9 1.4 pass_on_kernel.1
  194.3 17.2 %all_to_all.53.refs_0_ = f32[32,8,128]{2,1,0:T(8,128)} all-to-all(f32[32,8,128]{2,1,0:T(8,128)} %pass_on_kernel.1), channel_id=1, replica_groups=mesh['gx'=8,'gy_0'=4,'gy_1'=4,'gy_2'=2] {'gy_0','gy_1','gy_2'}, dimensions={0} | all-to-all | bytes 262144 | tf_op jit(solution)/shard_map/all_to_all | solution.py:475
  211.6 1.5 finish_kernel.1
  (66 shorter events, 1.2 us)
Async XLA Ops:
  3.9 11.6 %collective-permute-start = (f32[248,128]{1,0:T(8,128)}, f32[248,128]{1,0:T(8,128)S(1)}, u32[]{:S(2)}, u32[]{:S(2)}) collective-permute-start(f32[248,128]{1,0:T(8,128)} %get-tuple-element.53), channel_id=1, source_target_pairs={{0,32},{32,64},{64,96},{96,128},{128,160},{160,192},{192,224},{224... | collective-permute-start | bytes 380936 | tf_op jit(solution)/shard_map/ppermute | solution.py:462
  6.3 9.2 %collective-permute-start.1 = (f32[248,128]{1,0:T(8,128)}, f32[248,128]{1,0:T(8,128)S(1)}, u32[]{:S(2)}, u32[]{:S(2)}) collective-permute-start(f32[248,128]{1,0:T(8,128)} %get-tuple-element.54), channel_id=1, source_target_pairs={{0,1},{1,2},{2,3},{3,4},{4,5},{5,6},{6,7},{7,8},{8,9},{9,10},{10,1... | collective-permute-start | bytes 380936 | tf_op jit(solution)/shard_map/ppermute | solution.py:462
  8.4 7.1 %collective-permute-start.2 = (f32[24,200]{1,0:T(8,128)}, f32[24,200]{1,0:T(8,128)S(1)}, u32[]{:S(2)}, u32[]{:S(2)}) collective-permute-start(f32[24,200]{1,0:T(8,128)} %get-tuple-element.55), channel_id=1, source_target_pairs={{0,224},{32,0},{64,32},{96,64},{128,96},{160,128},{192,160},{224,1... | collective-permute-start | bytes 57608 | tf_op jit(solution)/shard_map/ppermute | solution.py:462
  12.1 3.5 %collective-permute-start.3 = (f32[24,200]{1,0:T(8,128)}, f32[24,200]{1,0:T(8,128)S(1)}, u32[]{:S(2)}, u32[]{:S(2)}) collective-permute-start(f32[24,200]{1,0:T(8,128)} %get-tuple-element.56), channel_id=1, source_target_pairs={{0,31},{1,0},{2,1},{3,2},{4,3},{5,4},{6,5},{7,6},{8,7},{9,8},{10,9... | collective-permute-start | bytes 57608 | tf_op jit(solution)/shard_map/ppermute | solution.py:462
  14.3 20.0 %copy-start.26 = (s32[8,128]{1,0:T(8,128)S(1)}, s32[8,128]{1,0:T(8,128)}, u32[]{:S(2)}) copy-start(s32[8,128]{1,0:T(8,128)} %constant.19.clone) | copy-start | bytes 12292
  15.4 0.6 copy-start.24
  15.5 0.6 copy-start.25
  15.5 0.7 copy-start.22
  15.5 0.7 copy-start.23
  21.2 17.2 %all-to-all-start = ((f32[8,112,128]{2,1,0:T(8,128)}), f32[8,112,128]{2,1,0:T(8,128)S(1)}, u32[]{:S(2)}, u32[]{:S(2)}) async-start(f32[8,112,128]{2,1,0:T(8,128)} %get-tuple-element.58), calls=%async_computation | async-start | bytes 917504 | tf_op jit(solution)/shard_map/all_to_all | solution.py:475
  27.1 11.3 %collective-permute-start.4 = (f32[200,128]{1,0:T(8,128)}, f32[200,128]{1,0:T(8,128)S(1)}, u32[]{:S(2)}, u32[]{:S(2)}) collective-permute-start(f32[200,128]{1,0:T(8,128)} %get-tuple-element.59), channel_id=1, source_target_pairs={{0,32},{32,64},{64,96},{96,128},{128,160},{160,192},{192,224},{224... | collective-permute-start | bytes 307208 | tf_op jit(solution)/shard_map/ppermute | solution.py:462
  28.5 9.8 %collective-permute-start.5 = (f32[200,128]{1,0:T(8,128)}, f32[200,128]{1,0:T(8,128)S(1)}, u32[]{:S(2)}, u32[]{:S(2)}) collective-permute-start(f32[200,128]{1,0:T(8,128)} %get-tuple-element.60), channel_id=1, source_target_pairs={{0,1},{1,2},{2,3},{3,4},{4,5},{5,6},{6,7},{7,8},{8,9},{9,10},{10,1... | collective-permute-start | bytes 307208 | tf_op jit(solution)/shard_map/ppermute | solution.py:462
  30.8 7.6 %collective-permute-start.6 = (f32[200,128]{1,0:T(8,128)}, f32[200,128]{1,0:T(8,128)S(1)}, u32[]{:S(2)}, u32[]{:S(2)}) collective-permute-start(f32[200,128]{1,0:T(8,128)} %get-tuple-element.61), channel_id=1, source_target_pairs={{0,224},{32,0},{64,32},{96,64},{128,96},{160,128},{192,160},{224,1... | collective-permute-start | bytes 307208 | tf_op jit(solution)/shard_map/ppermute | solution.py:462
  31.7 6.7 %collective-permute-start.7 = (f32[200,128]{1,0:T(8,128)}, f32[200,128]{1,0:T(8,128)S(1)}, u32[]{:S(2)}, u32[]{:S(2)}) collective-permute-start(f32[200,128]{1,0:T(8,128)} %get-tuple-element.62), channel_id=1, source_target_pairs={{0,31},{1,0},{2,1},{3,2},{4,3},{5,4},{6,5},{7,6},{8,7},{9,8},{10,9... | collective-permute-start | bytes 307208 | tf_op jit(solution)/shard_map/ppermute | solution.py:462
  38.4 0.6 copy-start.13
  38.4 0.7 copy-start.14
  38.4 0.7 copy-start.15
  38.4 0.7 copy-start.16
  39.1 0.8 copy-start
  42.1 24.4 %all-to-all-start.1 = ((f32[32,16,256]{2,1,0:T(8,128)}), f32[32,16,256]{2,1,0:T(8,128)S(1)}, u32[]{:S(2)}, u32[]{:S(2)}) async-start(f32[32,16,256]{2,1,0:T(8,128)} %spread_kernel.2), calls=%async_computation.1 | async-start | bytes 1048576 | tf_op jit(solution)/shard_map/all_to_all | solution.py:475
  66.5 0.8 copy-start.1
  70.3 12.9 %all-to-all-start.2 = ((f32[32,8,128]{2,1,0:T(8,128)}), f32[32,8,128]{2,1,0:T(8,128)S(1)}, u32[]{:S(2)}, u32[]{:S(2)}) async-start(f32[32,8,128]{2,1,0:T(8,128)} %get-tuple-element.65), calls=%async_computation.2 | async-start | bytes 262144 | tf_op jit(solution)/shard_map/all_to_all | solution.py:475
  74.2 5.6 %collective-permute-start.8 = (f32[200,128]{1,0:T(8,128)}, f32[200,128]{1,0:T(8,128)S(1)}, u32[]{:S(2)}, u32[]{:S(2)}) collective-permute-start(f32[200,128]{1,0:T(8,128)} %get-tuple-element.69), channel_id=1, source_target_pairs={{0,32},{32,64},{64,96},{96,128},{128,160},{160,192},{192,224},{224... | collective-permute-start | bytes 307208 | tf_op jit(solution)/shard_map/ppermute | solution.py:462
  74.4 5.4 %collective-permute-start.9 = (f32[200,128]{1,0:T(8,128)}, f32[200,128]{1,0:T(8,128)S(1)}, u32[]{:S(2)}, u32[]{:S(2)}) collective-permute-start(f32[200,128]{1,0:T(8,128)} %get-tuple-element.70), channel_id=1, source_target_pairs={{0,1},{1,2},{2,3},{3,4},{4,5},{5,6},{6,7},{7,8},{8,9},{9,10},{10,1... | collective-permute-start | bytes 307208 | tf_op jit(solution)/shard_map/ppermute | solution.py:462
  76.3 4.7 %collective-permute-start.10 = (f32[200,128]{1,0:T(8,128)}, f32[200,128]{1,0:T(8,128)S(1)}, u32[]{:S(2)}, u32[]{:S(2)}) collective-permute-start(f32[200,128]{1,0:T(8,128)} %get-tuple-element.71), channel_id=1, source_target_pairs={{0,224},{32,0},{64,32},{96,64},{128,96},{160,128},{192,160},{224,1... | collective-permute-start | bytes 307208 | tf_op jit(solution)/shard_map/ppermute | solution.py:462
  78.9 4.3 %collective-permute-start.11 = (f32[200,128]{1,0:T(8,128)}, f32[200,128]{1,0:T(8,128)S(1)}, u32[]{:S(2)}, u32[]{:S(2)}) collective-permute-start(f32[200,128]{1,0:T(8,128)} %get-tuple-element.72), channel_id=1, source_target_pairs={{0,31},{1,0},{2,1},{3,2},{4,3},{5,4},{6,5},{7,6},{8,7},{9,8},{10,9... | collective-permute-start | bytes 307208 | tf_op jit(solution)/shard_map/ppermute | solution.py:462
  79.8 3.4 %copy-start.5 = (f32[200,128]{1,0:T(8,128)}, f32[200,128]{1,0:T(8,128)S(1)}, u32[]{:S(2)}) copy-start(f32[200,128]{1,0:T(8,128)S(1)} %collective-permute-done.8.refs_5_.refs_4_) | copy-start | bytes 307204
  79.8 3.4 %copy-start.6 = (f32[200,128]{1,0:T(8,128)}, f32[200,128]{1,0:T(8,128)S(1)}, u32[]{:S(2)}) copy-start(f32[200,128]{1,0:T(8,128)S(1)} %collective-permute-done.9.refs_6_.refs_5_) | copy-start | bytes 307204
  81.0 2.1 copy-start.8
  83.2 0.6 copy-start.10
  83.2 0.7 copy-start.4
  104.5 13.0 %all-to-all-start.4 = ((f32[8,16,128]{2,1,0:T(8,128)}), f32[8,16,128]{2,1,0:T(8,128)S(1)}, u32[]{:S(2)}, u32[]{:S(2)}) async-start(f32[8,16,128]{2,1,0:T(8,128)} %get-tuple-element.78), calls=%async_computation.4 | async-start | bytes 131072 | tf_op jit(solution)/shard_map/all_to_all | solution.py:475
  107.9 6.4 %collective-permute-start.12 = (f32[200,128]{1,0:T(8,128)}, f32[200,128]{1,0:T(8,128)S(1)}, u32[]{:S(2)}, u32[]{:S(2)}) collective-permute-start(f32[200,128]{1,0:T(8,128)} %get-tuple-element.79), channel_id=1, source_target_pairs={{0,32},{32,64},{64,96},{96,128},{128,160},{160,192},{192,224},{224... | collective-permute-start | bytes 307208 | tf_op jit(solution)/shard_map/ppermute | solution.py:462
  109.3 5.1 %collective-permute-start.13 = (f32[200,128]{1,0:T(8,128)}, f32[200,128]{1,0:T(8,128)S(1)}, u32[]{:S(2)}, u32[]{:S(2)}) collective-permute-start(f32[200,128]{1,0:T(8,128)} %get-tuple-element.80), channel_id=1, source_target_pairs={{0,1},{1,2},{2,3},{3,4},{4,5},{5,6},{6,7},{7,8},{8,9},{9,10},{10,1... | collective-permute-start | bytes 307208 | tf_op jit(solution)/shard_map/ppermute | solution.py:462
  111.8 4.2 %collective-permute-start.14 = (f32[200,128]{1,0:T(8,128)}, f32[200,128]{1,0:T(8,128)S(1)}, u32[]{:S(2)}, u32[]{:S(2)}) collective-permute-start(f32[200,128]{1,0:T(8,128)} %get-tuple-element.81), channel_id=1, source_target_pairs={{0,224},{32,0},{64,32},{96,64},{128,96},{160,128},{192,160},{224,1... | collective-permute-start | bytes 307208 | tf_op jit(solution)/shard_map/ppermute | solution.py:462
  112.9 4.6 %collective-permute-start.15 = (f32[200,128]{1,0:T(8,128)}, f32[200,128]{1,0:T(8,128)S(1)}, u32[]{:S(2)}, u32[]{:S(2)}) collective-permute-start(f32[200,128]{1,0:T(8,128)} %get-tuple-element.82), channel_id=1, source_target_pairs={{0,31},{1,0},{2,1},{3,2},{4,3},{5,4},{6,5},{7,6},{8,7},{9,8},{10,9... | collective-permute-start | bytes 307208 | tf_op jit(solution)/shard_map/ppermute | solution.py:462
  114.3 3.2 %copy-start.7 = (f32[200,128]{1,0:T(8,128)}, f32[200,128]{1,0:T(8,128)S(1)}, u32[]{:S(2)}) copy-start(f32[200,128]{1,0:T(8,128)S(1)} %collective-permute-done.12.refs_2_.refs_1_) | copy-start | bytes 307204
  114.3 3.2 %copy-start.9 = (f32[200,128]{1,0:T(8,128)}, f32[200,128]{1,0:T(8,128)S(1)}, u32[]{:S(2)}) copy-start(f32[200,128]{1,0:T(8,128)S(1)} %collective-permute-done.13.refs_3_.refs_2_) | copy-start | bytes 307204
  116.0 1.5 copy-start.11
  117.5 0.6 copy-start.12
  118.2 0.6 copy-start.21
  120.9 22.1 %all-to-all-start.5 = ((f32[32,16,256]{2,1,0:T(8,128)}), f32[32,16,256]{2,1,0:T(8,128)S(1)}, u32[]{:S(2)}, u32[]{:S(2)}) async-start(f32[32,16,256]{2,1,0:T(8,128)} %spread_kernel.3), calls=%async_computation.5 | async-start | bytes 1048576 | tf_op jit(solution)/shard_map/all_to_all | solution.py:475
  143.0 0.8 copy-start.2
  146.2 12.9 %all-to-all-start.6 = ((f32[32,8,128]{2,1,0:T(8,128)}), f32[32,8,128]{2,1,0:T(8,128)S(1)}, u32[]{:S(2)}, u32[]{:S(2)}) async-start(f32[32,8,128]{2,1,0:T(8,128)} %get-tuple-element.87), calls=%async_computation.6 | async-start | bytes 262144 | tf_op jit(solution)/shard_map/all_to_all | solution.py:475
  150.1 5.6 %collective-permute-start.16 = (f32[200,128]{1,0:T(8,128)}, f32[200,128]{1,0:T(8,128)S(1)}, u32[]{:S(2)}, u32[]{:S(2)}) collective-permute-start(f32[200,128]{1,0:T(8,128)} %get-tuple-element.91), channel_id=1, source_target_pairs={{0,32},{32,64},{64,96},{96,128},{128,160},{160,192},{192,224},{224... | collective-permute-start | bytes 307208 | tf_op jit(solution)/shard_map/ppermute | solution.py:462
  150.5 5.2 %collective-permute-start.17 = (f32[200,128]{1,0:T(8,128)}, f32[200,128]{1,0:T(8,128)S(1)}, u32[]{:S(2)}, u32[]{:S(2)}) collective-permute-start(f32[200,128]{1,0:T(8,128)} %get-tuple-element.92), channel_id=1, source_target_pairs={{0,1},{1,2},{2,3},{3,4},{4,5},{5,6},{6,7},{7,8},{8,9},{9,10},{10,1... | collective-permute-start | bytes 307208 | tf_op jit(solution)/shard_map/ppermute | solution.py:462
  152.4 4.5 %collective-permute-start.18 = (f32[200,128]{1,0:T(8,128)}, f32[200,128]{1,0:T(8,128)S(1)}, u32[]{:S(2)}, u32[]{:S(2)}) collective-permute-start(f32[200,128]{1,0:T(8,128)} %get-tuple-element.93), channel_id=1, source_target_pairs={{0,224},{32,0},{64,32},{96,64},{128,96},{160,128},{192,160},{224,1... | collective-permute-start | bytes 307208 | tf_op jit(solution)/shard_map/ppermute | solution.py:462
  154.7 4.3 %collective-permute-start.19 = (f32[200,128]{1,0:T(8,128)}, f32[200,128]{1,0:T(8,128)S(1)}, u32[]{:S(2)}, u32[]{:S(2)}) collective-permute-start(f32[200,128]{1,0:T(8,128)} %get-tuple-element.94), channel_id=1, source_target_pairs={{0,31},{1,0},{2,1},{3,2},{4,3},{5,4},{6,5},{7,6},{8,7},{9,8},{10,9... | collective-permute-start | bytes 307208 | tf_op jit(solution)/shard_map/ppermute | solution.py:462
  155.7 3.4 %copy-start.17 = (f32[200,128]{1,0:T(8,128)}, f32[200,128]{1,0:T(8,128)S(1)}, u32[]{:S(2)}) copy-start(f32[200,128]{1,0:T(8,128)S(1)} %collective-permute-done.16.refs_6_.refs_5_) | copy-start | bytes 307204
  155.7 3.4 %copy-start.18 = (f32[200,128]{1,0:T(8,128)}, f32[200,128]{1,0:T(8,128)S(1)}, u32[]{:S(2)}) copy-start(f32[200,128]{1,0:T(8,128)S(1)} %collective-permute-done.17.refs_7_.refs_6_) | copy-start | bytes 307204
  156.9 2.1 copy-start.19
  159.0 0.7 copy-start.20
  159.0 0.7 copy-start.3
where the time goes:
time: 214 us; the launch traced here: 213 us
  starting transfers between devices  71.8 us (34%)
  blocking collectives  54.8 us (26%)
  Pallas kernels  45.5 us (21%)
  waiting for transfers between devices  28.1 us (13%)
  local copies, waits for them, and re-layouts  11 us (5%)
    all_to_all x4, blocking collectives, exchanged(): return lax.all_to_all(array, axis, split_axis=0, concat_axis=0, tiled=True)  54.8 us
    pallas_call x14, Pallas kernels, run(): pl.pallas_call(body, name=kernel.__name__, out_shape=[jax.ShapeDtypeStruc...  45.5 us
    all_to_all x6, starting transfers between devices, exchanged(): return lax.all_to_all(array, axis, split_axis=0, concat_axis=0, tiled=True)  40.6 us
    ppermute x20, starting transfers between devices, passed_along(): lax.ppermute(array, axis, [(i, (i + by) % peers) for i in range(peers)])  31.2 us
    ppermute x20, waiting for transfers between devices, passed_along(): lax.ppermute(array, axis, [(i, (i + by) % peers) for i in range(peers)])  14.9 us
    all_to_all x6, waiting for transfers between devices, exchanged(): return lax.all_to_all(array, axis, split_axis=0, concat_axis=0, tiled=True)  13.3 us
    unnamed x55, local copies, waits for them, and re-layouts  7.63 us
  transfers between devices with their start and end apart: 26, of which 12 were waited for; matrix products, arithmetic and copies ran while one was open for 2% of the time, Pallas kernels for 4%

commit v1 on v0

--- a/solution.py
+++ b/solution.py
@@ -20,32 +20,30 @@
 
 
 def corner_lanes():
-    lanes = np.full((GX, 128), -1, np.int32)
+    lanes = np.full(128, -1, np.int32)
     shifts = [(0, 0), (1, 0), (-1, 0), (0, 1), (0, -1)]
-    for x in range(GX):
-        for t, (dx, dy) in enumerate(shifts):
-            for c in range(8):
-                for i in range(3):
-                    node_x = (x + dx + c % 2) % GX
-                    j = 1 + dy + (c // 2) % 2
-                    lanes[x, t * 24 + 3 * c + i] = j * 64 + i * 16 + node_x * 2 + c // 4
-        lanes[x, E_LANE] = 48
-        lanes[x, ID_LANE] = 112 + 2 * x
-        lanes[x, ID_LANE + 1] = 113 + 2 * x
+    for t, (dx, dy) in enumerate(shifts):
+        for c in range(8):
+            for i in range(3):
+                j = 1 + dy + (c // 2) % 2
+                lanes[t * 24 + 3 * c + i] = j * 64 + i * 16 + (dx + c % 2) % GX * 2 + c // 4
+    lanes[E_LANE], lanes[ID_LANE], lanes[ID_LANE + 1] = 48, 112, 113
     return lanes
 
 
-def in_three(a):
+def halves_of(a, axis):
     high = a.astype(BF16)
-    rest = a - high.astype(F32)
-    middle = rest.astype(BF16)
-    low = (rest - middle.astype(F32)).astype(BF16)
-    return jnp.concatenate([high, middle, low], axis=0)
+    low = (a - high.astype(F32)).astype(BF16)
+    return jnp.concatenate([high, low], axis=axis)
+
+
+def in_two(a):
+    return halves_of(a, 0)
 
 
 def added_up(stacked):
-    rows = stacked.shape[0] // 3
-    return stacked[:rows] + (stacked[rows : 2 * rows] + stacked[2 * rows :])
+    rows = stacked.shape[0] // 2
+    return stacked[:rows] + stacked[rows:]
 
 
 def dot(a, b):
@@ -65,11 +63,24 @@
     return lax.broadcasted_iota(jnp.int32, shape, 1) // 16
 
 
+def rolled_groups(a, by):
+    by %= 16
+    if by == 0:
+        return a
+    lane = lax.broadcasted_iota(jnp.int32, (a.shape[0], 128), 1) % 16
+    tiles = [a[:, n : n + 128] for n in range(0, a.shape[1], 128)]
+    return jnp.concatenate(
+        [jnp.where(lane >= by, pltpu.roll(t, by, 1), pltpu.roll(t, 112 + by, 1)) for t in tiles], axis=1
+    )
+
+
 def spread_kernel(got_ref, lanes_ref, out_ref):
-    total = jnp.zeros((3 * CHUNK, 256), F32)
-    for x in range(GX):
-        total += dot(in_three(got_ref[x, 0:CHUNK, :]), lanes_ref[x])
-    out_ref[...] = jnp.broadcast_to(added_up(total)[None], out_ref.shape)
+    loads = jnp.concatenate([got_ref[x, 0:CHUNK, :] for x in range(GX)], axis=0)
+    placed = added_up(dot(in_two(loads), lanes_ref[...]))
+    total = placed[0:CHUNK]
+    for x in range(1, GX):
+        total += rolled_groups(placed[x * CHUNK : (x + 1) * CHUNK], 2 * x)
+    out_ref[...] = jnp.broadcast_to(total[None], out_ref.shape)
 
 
 def assembled_loads(me, got_ref, loads_ref):
@@ -95,7 +106,8 @@
     for i in range(3):
         for q in range(4):
             loads_ref[:, i * 512 + q * 128 : i * 512 + (q + 1) * 128] = tiles[i][q]
-    return energy
+    energy = jnp.sum(jnp.where(group == 3, energy, 0.0), axis=1, keepdims=True)
+    return jnp.broadcast_to(energy, (CHUNK, 128))
 
 
 def own_rows(loads_ref, high_ref, low_ref):
@@ -156,10 +168,10 @@
         for q in range(4):
             for column in range(3):
                 for i in range(3):
-                    start = CHUNK + q * 24 + column * 8 + i * 2
+                    start = CHUNK + q * 18 + column * 6 + i * 2
                     at = column * 48 + i * 16 + x * 2
                     held[at : at + 2, q * 128 : (q + 1) * 128] = rows_ref[x, start : start + 2, :]
-    ordered = added_up(dot(in_three(held[...]), by_id))
+    ordered = added_up(dot(in_two(held[...]), by_id))
     high = ordered.astype(BF16)
     high_ref[...] = high
     low_ref[...] = (ordered - high.astype(F32)).astype(BF16)
@@ -196,7 +208,7 @@
             old = tiles[i][k // 8]
             tiles[i][k // 8] = piece if old is None else old + piece
     solution = jnp.concatenate([jnp.concatenate(tiles[i], axis=1) for i in range(3)], axis=0)
-    grid_ref[...] = added_up(dot(in_three(solution), place_ref[...]))
+    grid_ref[...] = added_up(dot(in_two(solution), place_ref[...]))
     loads = loads_ref[...]
     shape = (CHUNK, 128)
     product = lane_sum(loads, grid_ref, shape)
@@ -211,27 +223,25 @@
                 near = grid_ref[i * CHUNK : (i + 1) * CHUNK, 0:128]
                 tile = jnp.where(group == at // 16, moved_lanes(near, (half * 2 + n) * 16, at), tile)
         if half == 0:
-            tile = jnp.where(lane == 48, energy_ref[...], tile)
+            tile = jnp.where(group == 3, energy_ref[...], tile)
             tile = jnp.where(lane >= 112, jnp.where(lane % 2 == 0, product, mixed), tile)
         halves.append(tile)
-    near = in_three(jnp.concatenate(halves, axis=1))
+    near = jnp.concatenate(halves, axis=1)
+    near = jnp.concatenate([rolled_groups(near, -2 * x) for x in range(GX)], axis=0)
+    picked = added_up(dot_rows(in_two(near), lanes_ref[...]))
     sums = rows_of_sums(sums)
     for x in range(GX):
-        out_ref[x, 0:CHUNK, :] = added_up(dot_rows(near, lanes_ref[x]))
+        out_ref[x, 0:CHUNK, :] = picked[x * CHUNK : (x + 1) * CHUNK]
         out_ref[x, CHUNK : CHUNK + 8, :] = sums
 
 
-def wide_three(a):
-    high = a.astype(BF16)
-    rest = a - high.astype(F32)
-    middle = rest.astype(BF16)
-    low = (rest - middle.astype(F32)).astype(BF16)
-    return jnp.concatenate([high, middle, low], axis=1)
+def wide_two(a):
+    return halves_of(a, 1)
 
 
 def wide_sum(a):
-    width = a.shape[1] // 3
-    return a[:, :width] + (a[:, width : 2 * width] + a[:, 2 * width :])
+    width = a.shape[1] // 2
+    return a[:, :width] + a[:, width:]
 
 
 def dot_columns(a, b):
@@ -244,15 +254,15 @@
 
 def send_faces(values_ref, table_ref, outs, face):
     up_x, up_y, low_x, low_y = outs
-    up_x[...] = wide_sum(dot(table_ref[0], wide_three(faces_of(values_ref, 1, face))))
-    up_y[...] = wide_sum(dot(table_ref[1], wide_three(faces_of(values_ref, 3, face))))
+    up_x[...] = wide_sum(dot(table_ref[0], wide_two(faces_of(values_ref, 1, face))))
+    up_y[...] = wide_sum(dot(table_ref[1], wide_two(faces_of(values_ref, 3, face))))
     low_x[...] = faces_of(values_ref, 0, face)
     low_y[...] = faces_of(values_ref, 2, face)
 
 
 def jump_faces(values_ref, received, table_ref, face):
     below_x, below_y, above_x, above_y = received
-    up = [wide_sum(dot_columns(table_ref[a], wide_three(ref[...]))) for a, ref in ((0, above_x), (1, above_y))]
+    up = [wide_sum(dot_columns(table_ref[a], wide_two(ref[...]))) for a, ref in ((0, above_x), (1, above_y))]
     own = [faces_of(values_ref, n, face) for n in range(6)]
     return [
         own[0] - below_x[...], own[1] - up[0], own[2] - below_y[...], own[3] - up[1], 0.0 * own[4], 0.0 * own[5]
@@ -268,9 +278,9 @@
 
 
 def loads_of(solved_ref, reach_ref, energy, ids, face):
-    loads = jnp.zeros((128, 3 * 128), F32)
+    loads = jnp.zeros((128, 2 * 128), F32)
     for n in range(4):
-        loads += dot(reach_ref[n], wide_three(faces_of(solved_ref, n, face)))
+        loads += dot(reach_ref[n], wide_two(faces_of(solved_ref, n, face)))
     loads = 0.5 * wide_sum(loads)
     row = lax.broadcasted_iota(jnp.int32, (128, 128), 0)
     loads = jnp.where(row == E_LANE, energy, loads)
@@ -281,7 +291,7 @@
 
 
 def corner_faces(corners, reach_ref):
-    pieces = wide_three(corners)
+    pieces = wide_two(corners)
     return [wide_sum(dot_columns(reach_ref[n], pieces)) for n in range(4)]
 
 
@@ -295,7 +305,7 @@
     for a, (plus, minus) in enumerate(((plus_x, minus_x), (plus_y, minus_y))):
         table = jnp.where(row == pairing_ref[a : a + 1, :], 1.0, 0.0).astype(BF16)
         table_ref[a] = table
-        plus[0:face, :] = wide_sum(dot(table, wide_three(rhs_ref[a])))
+        plus[0:face, :] = wide_sum(dot(table, wide_two(rhs_ref[a])))
         moved = dot_rows(coupling_of(phi_ref, 2 * a + 1, face).astype(BF16), table)
         moved = jnp.concatenate([moved, jnp.zeros((24, 256 - face), F32)], axis=1)
         plus[face : face + 24, :] = moved[:, :128]
@@ -330,18 +340,20 @@
     loads = loads_of(solved_ref, reach_ref, energy, (ids_ref[0], ids_ref[4]), face)
     for x in range(GX):
         out_ref[x, 0:CHUNK, :] = loads[x * CHUNK : (x + 1) * CHUNK]
-        out_ref[x, CHUNK : CHUNK + 96, :] = rows_ref[...]
+        out_ref[x, CHUNK : CHUNK + 72, :] = rows_ref[...]
 
 
 def stretch_kernel(
     solved_ref, below_x, below_y, above_x, above_y, table_ref, matrix_ref, *rest
 ):
     face = below_x.shape[0]
-    old = rest[:2] if len(rest) == 9 else None
-    field_ref, stretched_ref, up_x, up_y, low_x, low_y, sums_ref = rest[-7:]
+    old = rest[:2] if len(rest) == 10 else None
+    field_ref, stretched_ref, upper_ref, up_x, up_y, low_x, low_y, sums_ref = rest[-8:]
     jumped = jump_faces(solved_ref, (below_x, below_y, above_x, above_y), table_ref, face)
     for n in range(6):
         field_ref[n * face : (n + 1) * face, :] = 0.5 * jumped[n]
+        if n % 2 == 1:
+            upper_ref[n // 2] = 0.5 * jumped[n]
     stretched_ref[...] = dot(matrix_ref[...], field_ref[...].astype(BF16))
     send_faces(stretched_ref, table_ref, (up_x, up_y, low_x, low_y), face)
     rows = [column_sum(field_ref[...], stretched_ref[...])]
@@ -362,7 +374,7 @@
 
 
 def turn_kernel(
-    got_ref, half_ref, field_ref, stretched_ref, below_x, below_y, above_x, above_y, table_ref, reach_ref, matrix_ref,
+    got_ref, half_ref, stretched_ref, below_x, below_y, above_x, above_y, table_ref, reach_ref, matrix_ref,
     next_ref, solved_ref, image_ref, corners_ref, scalars_ref, up_x, up_y, low_x, low_y, out_ref,
 ):
     face = below_x.shape[0]
@@ -388,7 +400,7 @@
 
 
 def last_kernel(
-    got_ref, half_ref, field_ref, fresh_ref, stretched_ref, below_x, below_y, above_x, above_y, image_ref,
+    got_ref, half_ref, upper_ref, fresh_ref, stretched_ref, below_x, below_y, above_x, above_y, image_ref,
     corners_ref, scalars_ref, table_ref, reach_ref, matrix_ref, multipliers_ref, out_ref, held_ref,
 ):
     face = below_x.shape[0]
@@ -406,20 +418,10 @@
         image = jumped[n] + coarse[n] if n < 4 else jumped[n]
         held_ref[at, :] = half_ref[at, :] - (0.5 * step) * (image + ratio * image_ref[at, :])
     for a in range(3):
-        at = slice((2 * a + 1) * face, (2 * a + 2) * face)
-        first = field_ref[at, :]
-        multipliers_ref[a] = alpha * first + step * (fresh_ref[at, :] + ratio * first)
+        first = upper_ref[a]
+        multipliers_ref[a] = alpha * first + step * (fresh_ref[a] + ratio * first)
     solved = dot(matrix_ref[...], held_ref[...].astype(BF16))
-    out_ref[...] = jnp.broadcast_to(column_sum(held_ref[...], solved)[None], out_ref.shape)
-
-
-def pass_on_kernel(got_ref, out_ref):
-    total = jnp.sum(got_ref[...], axis=0)
-    out_ref[...] = jnp.broadcast_to(total[None], out_ref.shape)
-
-
-def finish_kernel(got_ref, scalars_ref, out_ref):
-    out_ref[...] = (jnp.sum(got_ref[...], axis=0) / jnp.broadcast_to(scalars_ref[0:1], (8, 128)))[0:1]
+    out_ref[...] = column_sum(held_ref[...], solved)
 
 
 def call(kernel, outs, smem=0, scratch=(), flops=2_000_000):
@@ -484,12 +486,11 @@
     pairing = pairing[0, 0, 0]
     coupling = phi[0, 0, 0]
     me = lax.axis_index(GY).astype(jnp.int32).reshape(1)
-    lanes = (jnp.asarray(corner_lanes())[:, :, None] == jnp.arange(256)[None, None, :]).astype(BF16)
+    lanes = (jnp.asarray(corner_lanes())[:, None] == jnp.arange(256)[None, :]).astype(BF16)
     mine = coarse_inverse.reshape(2, 3, 4, 128, 3)
-    mine = jnp.transpose(mine, (2, 4, 1, 0, 3)).reshape(12, 6, 128)
-    mine = jnp.concatenate([mine, jnp.zeros((12, 2, 128), F32)], axis=1).reshape(96, 128)
-
-    whole, faces = ((interface, 128), F32), [((face, 128), F32)] * 4
+    mine = jnp.transpose(mine, (2, 4, 1, 0, 3)).reshape(72, 128)
+
+    whole, upper, faces = ((interface, 128), F32), ((3, face, 128), F32), [((face, 128), F32)] * 4
     big = 2 * interface * interface * 128
     *sent, table = call(
         start_kernel, [((face + 48, 128), F32)] * 2 + [((24, face), F32)] * 2 + [((2, face, face), BF16)]
@@ -497,14 +498,14 @@
     received = passed_both_ways(*sent)
     half, solved, reach, *sent, message = call(
         first_kernel,
-        [whole, whole, ((4, 128, face), BF16), *faces, ((GX, CHUNK + 96, 128), F32)],
+        [whole, whole, ((4, 128, face), BF16), *faces, ((GX, CHUNK + 72, 128), F32)],
         smem=1,
         flops=big,
     )(incidence[0, 0, 0], rhs, *received, coupling, table, schur_block, mine)
     received = passed_both_ways(*sent)
     first_rows = exchanged(message, "gx")
     (sent,) = spread(first_rows, lanes, after=received)
-    field, stretched, *faces_sent, sums = call(stretch_kernel, [whole, whole, *faces, ((8, 128), F32)], flops=big)(
+    field, stretched, direction, *faces_sent, sums = call(stretch_kernel, [whole, whole, upper, *faces, ((8, 128), F32)], flops=big)(
         solved, *received, table, stiffness
     )
     received = passed_both_ways(*faces_sent)
@@ -516,12 +517,12 @@
         turn_kernel,
         [whole, whole, whole, ((128, 128), F32), ((8, 128), F32), *faces, ((GX, CHUNK, 128), F32)],
         flops=big,
-    )(back, half, field, stretched, *received, table, reach, schur_block)
+    )(back, half, stretched, *received, table, reach, schur_block)
 
     received = passed_both_ways(*sent)
     (sent,) = spread(exchanged(message, "gx"), lanes, after=received)
-    fresh, fresh_stretched, *faces_sent, sums = call(
-        stretch_kernel, [whole, whole, *faces, ((8, 128), F32)], flops=big
+    _, fresh_stretched, fresh, *faces_sent, sums = call(
+        stretch_kernel, [whole, whole, upper, *faces, ((8, 128), F32)], flops=big
     )(solved, *received, table, stiffness, field, stretched)
     received = passed_both_ways(*faces_sent)
     sent, loads, energy = next_solve(me, exchanged(sent, GY), high, low, sums)
@@ -529,15 +530,14 @@
     back = exchanged(back, "gx")
     multipliers, energy = call(
         last_kernel,
-        [((3, face, 128), F32), ((GX, 8, 128), F32)],
+        [((3, face, 128), F32), ((1, 128), F32)],
         scratch=[pltpu.VMEM((interface, 128), F32)],
         flops=big,
     )(
-        back, half, field, fresh, fresh_stretched, *received, image, corners, scalars, table, reach, schur_block
+        back, half, direction, fresh, fresh_stretched, *received, image, corners, scalars, table, reach, schur_block
     )
-    (energy,) = call(pass_on_kernel, [((GYN, 8, 128), F32)])(exchanged(energy, "gx"))
-    (reduction,) = call(finish_kernel, [((1, 128), F32)])(exchanged(energy, GY), scalars)
-    return (multipliers[None, None, None], reduction[0])
+    energy = jnp.sum(exchanged(jnp.broadcast_to(energy, (GX * GYN, 1, 128)), GX_GY), axis=(0, 1))
+    return (multipliers[None, None, None], energy / scalars[0])
 
 
 def solution(mesh):

time: 214 us -> 205 us (0.958)
  blocking collectives: 54.8 us -> 49.7 us
  Pallas kernels: 45.5 us -> 40.7 us
    all_to_all x4 -> x3, blocking collectives: 54.8 us -> 49.7 us  [exchanged(): return lax.all_to_all(array, axis, split_axis=0, concat_axis=0, tiled=True)]
    pallas_call x14 -> x12, Pallas kernels: 45.5 us -> 40.7 us  [run(): pl.pallas_call(body, name=kernel.__name__, out_shape=[jax.ShapeDtypeStruc...]
  transfers between devices with their start and end apart: 26 -> 26, of which waited for: 12 -> 14; matrix products, arithmetic and copies ran while one was open for 2% -> 2% of each run, Pallas kernels for 4% -> 5%
where the time goes in v1:
time: 205 us; the launch traced here: 204 us
  starting transfers between devices  71.5 us (35%)
  blocking collectives  49.7 us (24%)
  Pallas kernels  40.7 us (20%)
  waiting for transfers between devices  28 us (14%)
  local copies, waits for them, and re-layouts  10.9 us (5%)
    all_to_all x3, blocking collectives, exchanged(): return lax.all_to_all(array, axis, split_axis=0, concat_axis=0, tiled=True)  49.7 us
    pallas_call x12, Pallas kernels, run(): pl.pallas_call(body, name=kernel.__name__, out_shape=[jax.ShapeDtypeStruc...  40.7 us
    all_to_all x6, starting transfers between devices, exchanged(): return lax.all_to_all(array, axis, split_axis=0, concat_axis=0, tiled=True)  39.8 us
    ppermute x20, starting transfers between devices, passed_along(): lax.ppermute(array, axis, [(i, (i + by) % peers) for i in range(peers)])  31.7 us
    all_to_all x6, waiting for transfers between devices, exchanged(): return lax.all_to_all(array, axis, split_axis=0, concat_axis=0, tiled=True)  14.8 us
    ppermute x20, waiting for transfers between devices, passed_along(): lax.ppermute(array, axis, [(i, (i + by) % peers) for i in range(peers)])  13.2 us
    unnamed x55, local copies, waits for them, and re-layouts  6.9 us
  transfers between devices with their start and end apart: 26, of which 14 were waited for; matrix products, arithmetic and copies ran while one was open for 2% of the time, Pallas kernels for 5%

profile of v1, /device:TPU:1, one launch (start us, length us, event | category | flops | bytes accessed | tf_op | source)
XLA Modules:
  0.0 203.6 jit_solution(6182996886914940325)
XLA Ops:
  0.6 1.3 copy.17
  1.9 1.9 start_kernel.1
  3.8 2.5 %collective-permute-start = (f32[248,128]{1,0:T(8,128)}, f32[248,128]{1,0:T(8,128)S(1)}, u32[]{:S(2)}, u32[]{:S(2)}) collective-permute-start(f32[248,128]{1,0:T(8,128)} %get-tuple-element.54), channel_id=1, source_target_pairs={{0,32},{32,64},{64,96},{96,128},{128,160},{160,192},{192,224},{224... | collective-permute-start | bytes 380936 | tf_op jit(solution)/shard_map/ppermute | solution.py:464
  6.3 2.1 %collective-permute-start.1 = (f32[248,128]{1,0:T(8,128)}, f32[248,128]{1,0:T(8,128)S(1)}, u32[]{:S(2)}, u32[]{:S(2)}) collective-permute-start(f32[248,128]{1,0:T(8,128)} %get-tuple-element.55), channel_id=1, source_target_pairs={{0,1},{1,2},{2,3},{3,4},{4,5},{5,6},{6,7},{7,8},{8,9},{9,10},{10,1... | collective-permute-start | bytes 380936 | tf_op jit(solution)/shard_map/ppermute | solution.py:464
  8.4 3.7 %collective-permute-start.2 = (f32[24,200]{1,0:T(8,128)}, f32[24,200]{1,0:T(8,128)S(1)}, u32[]{:S(2)}, u32[]{:S(2)}) collective-permute-start(f32[24,200]{1,0:T(8,128)} %get-tuple-element.56), channel_id=1, source_target_pairs={{0,224},{32,0},{64,32},{96,64},{128,96},{160,128},{192,160},{224,1... | collective-permute-start | bytes 57608 | tf_op jit(solution)/shard_map/ppermute | solution.py:464
  12.0 2.2 %reshape.16 = f32[2,3,4,128,3]{4,3,2,1,0:T(8,128)S(1)} reshape(f32[6,1536]{1,0:T(8,128)} %param.12) | data formatting | bytes 73728 | tf_op jit(solution)/shard_map/reshape | solution.py:490
  14.3 1.1 copy.13
  15.5 0.5 copy-done.24
  16.2 4.5 %first_kernel.1 = (f32[1200,128]{1,0:T(8,128)}, f32[1200,128]{1,0:T(8,128)}, bf16[4,128,200]{2,1,0:T(8,128)(2,1)}, f32[200,128]{1,0:T(8,128)}, f32[200,128]{1,0:...) custom-call(s32[8]{0:T(128)} %bitcast.29, f32[3,200,128]{2,1,0:T(8,128)} %bitcast.23, ...), custom_call_target="tpu_custom_call" | custom-call | flops 368640000 | bytes 1000000 | tf_op jit(solution)/shard_map/first_kernel/pallas_call | solution.py:437
  20.7 5.9 %all-to-all-start = ((f32[8,88,128]{2,1,0:T(8,128)}), f32[8,88,128]{2,1,0:T(8,128)S(1)}, u32[]{:S(2)}, u32[]{:S(2)}) async-start(f32[8,88,128]{2,1,0:T(8,128)} %get-tuple-element.59), calls=%async_computation | async-start | bytes 720896 | tf_op jit(solution)/shard_map/all_to_all | solution.py:477
  26.6 1.5 collective-permute-start.4
  28.0 2.2 %collective-permute-start.5 = (f32[200,128]{1,0:T(8,128)}, f32[200,128]{1,0:T(8,128)S(1)}, u32[]{:S(2)}, u32[]{:S(2)}) collective-permute-start(f32[200,128]{1,0:T(8,128)} %get-tuple-element.61), channel_id=1, source_target_pairs={{0,1},{1,2},{2,3},{3,4},{4,5},{5,6},{6,7},{7,8},{8,9},{9,10},{10,1... | collective-permute-start | bytes 307208 | tf_op jit(solution)/shard_map/ppermute | solution.py:464
  30.2 1.0 collective-permute-start.6
  31.2 2.6 %collective-permute-start.7 = (f32[200,128]{1,0:T(8,128)}, f32[200,128]{1,0:T(8,128)S(1)}, u32[]{:S(2)}, u32[]{:S(2)}) collective-permute-start(f32[200,128]{1,0:T(8,128)} %get-tuple-element.63), channel_id=1, source_target_pairs={{0,31},{1,0},{2,1},{3,2},{4,3},{5,4},{6,5},{7,6},{8,7},{9,8},{10,9... | collective-permute-start | bytes 307208 | tf_op jit(solution)/shard_map/ppermute | solution.py:464
  33.8 0.7 fusion.refs_1_.refs_4_
  34.5 0.6 collective-permute-done.4.refs_2_.refs_1_
  35.0 0.8 collective-permute-done.6.refs_4_.refs_3_
  35.8 1.4 all-to-all-done.refs_0_.refs_2_
  37.2 0.7 copy-done
  37.9 2.1 %spread_kernel.2 = f32[32,16,256]{2,1,0:T(8,128)} custom-call(f32[8,88,128]{2,1,0:T(8,128)} %copy-done, bf16[128,256]{1,0:T(8,128)(2,1)} %fusion.refs_1_.refs_4_, f32[200,128]{1,0:T(8,128)} %copy-done.13, f32[200,128]{1,0:T(8,128)} %copy-done.14, f32[200,128]{1,0:T(8,128)} %copy-done.15, f32[200,128]{1,0:T(8,128)} %copy-done.16), custom_call_target="tpu_custom_call" | custom-call | flops 2000000 | bytes 1000000 | tf_op jit(solution)/shard_map/spread_kernel/pallas_call | solution.py:437
  40.0 12.2 %all-to-all-start.1 = ((f32[32,16,256]{2,1,0:T(8,128)}), f32[32,16,256]{2,1,0:T(8,128)S(1)}, u32[]{:S(2)}, u32[]{:S(2)}) async-start(f32[32,16,256]{2,1,0:T(8,128)} %spread_kernel.2), calls=%async_computation.1 | async-start | bytes 1048576 | tf_op jit(solution)/shard_map/all_to_all | solution.py:477
  52.2 4.6 %stretch_kernel.2 = (f32[1200,128]{1,0:T(8,128)}, f32[1200,128]{1,0:T(8,128)}, f32[3,200,128]{2,1,0:T(8,128)}, f32[200,128]{1,0:T(8,128)}, f32[200,128]{1,0:T(8,...) custom-call(f32[1200,128]{1,0:T(8,128)} %get-tuple-element.64.refs_0_, f32[200,128]{1,0:T(8,128)} %copy-done.13, ...), custom_call_target="tpu_custom_call" | custom-call | flops 368640000 | bytes 1000000 | tf_op jit(solution)/shard_map/stretch_kernel/pallas_call | solution.py:437
  56.8 6.8 %all-to-all-done.1.refs_1_ = f32[32,16,256]{2,1,0:T(8,128)S(1)} async-done(((f32[32,16,256]{2,1,0:T(8,128)}), f32[32,16,256]{2,1,0:T(8,128)S(1)}, u32[]{:S(2)}, u32[]{:S(2)}) %all-to-all-start.1) | async-done | bytes 524320 | tf_op jit(solution)/shard_map/all_to_all | solution.py:477
  63.7 0.8 copy-done.1
  64.4 3.0 %first_solve_kernel.1 = (f32[32,8,128]{2,1,0:T(8,128)}, f32[16,1536]{1,0:T(8,128)}, f32[16,128]{1,0:T(8,128)}, bf16[144,512]{1,0:T(8,128)(2,1)}, bf16[144,512]{1,0:T(8,128)(2,1)}, /*index=5*/bf16[512,512]{1,0:T(8,128)(2,1)}) custom-call(s32[1]{0:T(128)} %bitcast.refs_0_, f32[32,16,256]{2,1,0:T(8,128)} %copy-done.1, f32[8,88,128]{2,1,0:T(8,128)} %copy-done, ...), custom_call_target="tpu_custom_call" | custom-call | flops 2000000 | bytes 1000000 | tf_op jit(solution)/shard_map/first_solve_kernel/pallas_call | solution.py:437
  67.4 3.9 %all-to-all-start.2 = ((f32[32,8,128]{2,1,0:T(8,128)}), f32[32,8,128]{2,1,0:T(8,128)S(1)}, u32[]{:S(2)}, u32[]{:S(2)}) async-start(f32[32,8,128]{2,1,0:T(8,128)} %get-tuple-element.66), calls=%async_computation.2 | async-start | bytes 262144 | tf_op jit(solution)/shard_map/all_to_all | solution.py:477
  71.3 0.5 collective-permute-start.8
  71.8 1.9 collective-permute-start.9
  73.7 2.5 %collective-permute-start.10 = (f32[200,128]{1,0:T(8,128)}, f32[200,128]{1,0:T(8,128)S(1)}, u32[]{:S(2)}, u32[]{:S(2)}) collective-permute-start(f32[200,128]{1,0:T(8,128)} %get-tuple-element.72), channel_id=1, source_target_pairs={{0,224},{32,0},{64,32},{96,64},{128,96},{160,128},{192,160},{224,1... | collective-permute-start | bytes 307208 | tf_op jit(solution)/shard_map/ppermute | solution.py:464
  76.2 0.9 collective-permute-done.8.refs_5_.refs_3_
  77.1 1.3 collective-permute-done.10.refs_7_.refs_5_
  78.4 2.1 %collective-permute-done.11.refs_8_.refs_6_ = f32[200,128]{1,0:T(8,128)S(1)} collective-permute-done((f32[200,128]{1,0:T(8,128)}, f32[200,128]{1,0:T(8,128)S(1)}, u32[]{:S(2)}, u32[]{:S(2)}) %collective-permute-start.11) | collective-permute-done | bytes 102432 | tf_op jit(solution)/shard_map/ppermute | solution.py:464
  80.5 0.6 copy-done.8
  81.2 2.5 %pick_kernel.2 = (f32[8,24,128]{2,1,0:T(8,128)}, f32[48,512]{1,0:T(8,128)}) custom-call(f32[32,8,128]{2,1,0:T(8,128)} %copy-done.3, f32[16,1536]{1,0:T(8,128)} %get-tuple-element.67.refs_1_, f32[16,128]{1,0:T(8,128)} %get-tuple-element.68.refs_2_, bf16[512,512]{1,0:T(8,128)(2,1)} %get-tuple-element.69.refs_3_, bf16[128,256]{1,0:T(8,128)(2,1)} %fusion.refs_1_.refs_4_, ...), custom_call_target="tpu_custom_call" | custom-call | flops 2000000 | bytes 1000000 | tf_op jit(solution)/shard_map/pick_kernel/pallas_call | solution.py:437
  83.7 13.4 %all_to_all.45.refs_0_ = f32[8,24,128]{2,1,0:T(8,128)} all-to-all(f32[8,24,128]{2,1,0:T(8,128)} %get-tuple-element.74), channel_id=1, replica_groups=mesh['gx'=8,'gy_0'=4,'gy_1'=4,'gy_2'=2] {'gx'}, dimensions={0} | all-to-all | bytes 196608 | tf_op jit(solution)/shard_map/all_to_all | solution.py:477
  97.1 5.3 %turn_kernel.1 = (f32[1200,128]{1,0:T(8,128)}, f32[1200,128]{1,0:T(8,128)}, f32[1200,128]{1,0:T(8,128)}, f32[128,128]{1,0:T(8,128)}, f32[8,128]{1,0:T(8,128)}, /...) custom-call(f32[8,24,128]{2,1,0:T(8,128)} %all_to_all.45.refs_0_, ...), custom_call_target="tpu_custom_call" | custom-call | flops 368640000 | bytes 1000000 | tf_op jit(solution)/shard_map/turn_kernel/pallas_call | solution.py:437
  102.4 3.3 %all-to-all-start.4 = ((f32[8,16,128]{2,1,0:T(8,128)}), f32[8,16,128]{2,1,0:T(8,128)S(1)}, u32[]{:S(2)}, u32[]{:S(2)}) async-start(f32[8,16,128]{2,1,0:T(8,128)} %get-tuple-element.78), calls=%async_computation.4 | async-start | bytes 131072 | tf_op jit(solution)/shard_map/all_to_all | solution.py:477
  105.8 1.4 collective-permute-start.12
  107.2 2.9 %collective-permute-start.13 = (f32[200,128]{1,0:T(8,128)}, f32[200,128]{1,0:T(8,128)S(1)}, u32[]{:S(2)}, u32[]{:S(2)}) collective-permute-start(f32[200,128]{1,0:T(8,128)} %get-tuple-element.80), channel_id=1, source_target_pairs={{0,1},{1,2},{2,3},{3,4},{4,5},{5,6},{6,7},{7,8},{8,9},{9,10},{10,1... | collective-permute-start | bytes 307208 | tf_op jit(solution)/shard_map/ppermute | solution.py:464
  110.1 1.1 collective-permute-start.14
  111.2 1.4 collective-permute-start.15
  112.6 1.6 collective-permute-done.14.refs_4_.refs_3_
  114.3 1.5 collective-permute-done.15.refs_5_.refs_4_
  115.8 0.6 copy-done.12
  116.4 0.6 copy-done.21
  117.0 2.0 spread_kernel.3
  119.0 10.6 %all-to-all-start.5 = ((f32[32,16,256]{2,1,0:T(8,128)}), f32[32,16,256]{2,1,0:T(8,128)S(1)}, u32[]{:S(2)}, u32[]{:S(2)}) async-start(f32[32,16,256]{2,1,0:T(8,128)} %spread_kernel.3), calls=%async_computation.5 | async-start | bytes 1048576 | tf_op jit(solution)/shard_map/all_to_all | solution.py:477
  129.7 4.9 %stretch_kernel.3 = (f32[1200,128]{1,0:T(8,128)}, f32[1200,128]{1,0:T(8,128)}, f32[3,200,128]{2,1,0:T(8,128)}, f32[200,128]{1,0:T(8,128)}, f32[200,128]{1,0:T(8,...) custom-call(f32[1200,128]{1,0:T(8,128)} %get-tuple-element.85.refs_0_, f32[200,128]{1,0:T(8,128)} %copy-done.9, ...), custom_call_target="tpu_custom_call" | custom-call | flops 368640000 | bytes 1000000 | tf_op jit(solution)/shard_map/stretch_kernel/pallas_call | solution.py:437
  134.5 6.6 %all-to-all-done.5.refs_1_ = f32[32,16,256]{2,1,0:T(8,128)S(1)} async-done(((f32[32,16,256]{2,1,0:T(8,128)}), f32[32,16,256]{2,1,0:T(8,128)S(1)}, u32[]{:S(2)}, u32[]{:S(2)}) %all-to-all-start.5) | async-done | bytes 524320 | tf_op jit(solution)/shard_map/all_to_all | solution.py:477
  141.1 0.8 copy-done.2
  141.9 2.4 %next_solve_kernel.1 = (f32[32,8,128]{2,1,0:T(8,128)}, f32[16,1536]{1,0:T(8,128)}, f32[16,128]{1,0:T(8,128)}) custom-call(s32[1]{0:T(128)} %bitcast.refs_0_, f32[32,16,256]{2,1,0:T(8,128)} %copy-done.2, bf16[144,512]{1,0:T(8,128)(2,1)} %get-tuple-element.83.refs_2_, bf16[144,512]{1,0:T(8,128)(2,1)} %get-tuple-element.84.refs_3_, ...), custom_call_target="tpu_custom_call" | custom-call | flops 2000000 | bytes 1000000 | tf_op jit(solution)/shard_map/next_solve_kernel/pallas_call | solution.py:437
  144.3 3.9 %all-to-all-start.6 = ((f32[32,8,128]{2,1,0:T(8,128)}), f32[32,8,128]{2,1,0:T(8,128)S(1)}, u32[]{:S(2)}, u32[]{:S(2)}) async-start(f32[32,8,128]{2,1,0:T(8,128)} %get-tuple-element.88), calls=%async_computation.6 | async-start | bytes 262144 | tf_op jit(solution)/shard_map/all_to_all | solution.py:477
  148.6 1.9 collective-permute-start.17
  150.5 2.3 %collective-permute-start.18 = (f32[200,128]{1,0:T(8,128)}, f32[200,128]{1,0:T(8,128)S(1)}, u32[]{:S(2)}, u32[]{:S(2)}) collective-permute-start(f32[200,128]{1,0:T(8,128)} %get-tuple-element.94), channel_id=1, source_target_pairs={{0,224},{32,0},{64,32},{96,64},{128,96},{160,128},{192,160},{224,1... | collective-permute-start | bytes 307208 | tf_op jit(solution)/shard_map/ppermute | solution.py:464
  152.9 0.9 collective-permute-done.16.refs_6_.refs_5_
  153.8 1.3 collective-permute-done.18.refs_8_.refs_7_
  155.1 2.1 %collective-permute-done.19.refs_9_.refs_8_ = f32[200,128]{1,0:T(8,128)S(1)} collective-permute-done((f32[200,128]{1,0:T(8,128)}, f32[200,128]{1,0:T(8,128)S(1)}, u32[]{:S(2)}, u32[]{:S(2)}) %collective-permute-start.19) | collective-permute-done | bytes 102432 | tf_op jit(solution)/shard_map/ppermute | solution.py:464
  157.2 0.6 copy-done.20
  157.8 2.6 %pick_kernel.3 = (f32[8,24,128]{2,1,0:T(8,128)}, f32[48,512]{1,0:T(8,128)}) custom-call(f32[32,8,128]{2,1,0:T(8,128)} %copy-done.4, f32[16,1536]{1,0:T(8,128)} %get-tuple-element.89.refs_1_, f32[16,128]{1,0:T(8,128)} %get-tuple-element.90.refs_2_, bf16[512,512]{1,0:T(8,128)(2,1)} %get-tuple-element.69.refs_3_, bf16[128,256]{1,0:T(8,128)(2,1)} %fusion.refs_1_.refs_4_, ...), custom_call_target="tpu_custom_call" | custom-call | flops 2000000 | bytes 1000000 | tf_op jit(solution)/shard_map/pick_kernel/pallas_call | solution.py:437
  160.5 14.5 %all_to_all.46.refs_0_ = f32[8,24,128]{2,1,0:T(8,128)} all-to-all(f32[8,24,128]{2,1,0:T(8,128)} %get-tuple-element.96), channel_id=1, replica_groups=mesh['gx'=8,'gy_0'=4,'gy_1'=4,'gy_2'=2] {'gx'}, dimensions={0} | all-to-all | bytes 196608 | tf_op jit(solution)/shard_map/all_to_all | solution.py:477
  174.9 4.9 %last_kernel.1 = (f32[3,200,128]{2,1,0:T(8,128)}, f32[1,128]{1,0:T(1,128)}) custom-call(f32[8,24,128]{2,1,0:T(8,128)} %all_to_all.46.refs_0_, f32[1200,128]{1,0:T(8,128)} %get-tuple-element.97.refs_1_, f32[3,200,128]{2,1,0:T(8,128)} %get-tuple-element.98.refs_2_, f32[3,200,128]{2,1,0:T(8,128)} %get-tuple-element.99.refs_3_, ...), custom_call_target="tpu_custom_call" | custom-call | flops 368640000 | bytes 1000000 | tf_op jit(solution)/shard_map/last_kernel/pallas_call | solution.py:437
  179.8 0.7 broadcast_in_dim.9
  180.5 21.8 %all_to_all.47 = f32[256,1,128]{2,1,0:T(1,128)S(1)} all-to-all(f32[256,1,128]{2,1,0:T(1,128)S(1)} %broadcast_in_dim.9), channel_id=1, replica_groups=mesh['gx'=8,'gy_0'=4,'gy_1'=4,'gy_2'=2] {'gx','gy_0','gy_1','gy_2'}, dimensions={0} | all-to-all | bytes 262144 | tf_op jit(solution)/shard_map/all_to_all | solution.py:477
  202.4 1.2 bitcast_divide_fusion
  (64 shorter events, 1.0 us)
Async XLA Ops:
  3.8 11.6 %collective-permute-start = (f32[248,128]{1,0:T(8,128)}, f32[248,128]{1,0:T(8,128)S(1)}, u32[]{:S(2)}, u32[]{:S(2)}) collective-permute-start(f32[248,128]{1,0:T(8,128)} %get-tuple-element.54), channel_id=1, source_target_pairs={{0,32},{32,64},{64,96},{96,128},{128,160},{160,192},{192,224},{224... | collective-permute-start | bytes 380936 | tf_op jit(solution)/shard_map/ppermute | solution.py:464
  6.3 9.2 %collective-permute-start.1 = (f32[248,128]{1,0:T(8,128)}, f32[248,128]{1,0:T(8,128)S(1)}, u32[]{:S(2)}, u32[]{:S(2)}) collective-permute-start(f32[248,128]{1,0:T(8,128)} %get-tuple-element.55), channel_id=1, source_target_pairs={{0,1},{1,2},{2,3},{3,4},{4,5},{5,6},{6,7},{7,8},{8,9},{9,10},{10,1... | collective-permute-start | bytes 380936 | tf_op jit(solution)/shard_map/ppermute | solution.py:464
  8.4 7.0 %collective-permute-start.2 = (f32[24,200]{1,0:T(8,128)}, f32[24,200]{1,0:T(8,128)S(1)}, u32[]{:S(2)}, u32[]{:S(2)}) collective-permute-start(f32[24,200]{1,0:T(8,128)} %get-tuple-element.56), channel_id=1, source_target_pairs={{0,224},{32,0},{64,32},{96,64},{128,96},{160,128},{192,160},{224,1... | collective-permute-start | bytes 57608 | tf_op jit(solution)/shard_map/ppermute | solution.py:464
  12.0 3.5 %collective-permute-start.3 = (f32[24,200]{1,0:T(8,128)}, f32[24,200]{1,0:T(8,128)S(1)}, u32[]{:S(2)}, u32[]{:S(2)}) collective-permute-start(f32[24,200]{1,0:T(8,128)} %get-tuple-element.57), channel_id=1, source_target_pairs={{0,31},{1,0},{2,1},{3,2},{4,3},{5,4},{6,5},{7,6},{8,7},{9,8},{10,9... | collective-permute-start | bytes 57608 | tf_op jit(solution)/shard_map/ppermute | solution.py:464
  14.3 19.5 %copy-start.26 = (s32[128]{0:T(128)S(1)}, s32[128]{0:T(128)}, u32[]{:S(2)}) copy-start(s32[128]{0:T(128)} %constant.19.clone) | copy-start | bytes 1540
  15.4 0.6 copy-start.24
  15.5 0.6 copy-start.25
  15.5 0.7 copy-start.22
  15.5 0.7 copy-start.23
  20.7 16.4 %all-to-all-start = ((f32[8,88,128]{2,1,0:T(8,128)}), f32[8,88,128]{2,1,0:T(8,128)S(1)}, u32[]{:S(2)}, u32[]{:S(2)}) async-start(f32[8,88,128]{2,1,0:T(8,128)} %get-tuple-element.59), calls=%async_computation | async-start | bytes 720896 | tf_op jit(solution)/shard_map/all_to_all | solution.py:477
  26.6 8.5 %collective-permute-start.4 = (f32[200,128]{1,0:T(8,128)}, f32[200,128]{1,0:T(8,128)S(1)}, u32[]{:S(2)}, u32[]{:S(2)}) collective-permute-start(f32[200,128]{1,0:T(8,128)} %get-tuple-element.60), channel_id=1, source_target_pairs={{0,32},{32,64},{64,96},{96,128},{128,160},{160,192},{192,224},{224... | collective-permute-start | bytes 307208 | tf_op jit(solution)/shard_map/ppermute | solution.py:464
  28.0 7.0 %collective-permute-start.5 = (f32[200,128]{1,0:T(8,128)}, f32[200,128]{1,0:T(8,128)S(1)}, u32[]{:S(2)}, u32[]{:S(2)}) collective-permute-start(f32[200,128]{1,0:T(8,128)} %get-tuple-element.61), channel_id=1, source_target_pairs={{0,1},{1,2},{2,3},{3,4},{4,5},{5,6},{6,7},{7,8},{8,9},{9,10},{10,1... | collective-permute-start | bytes 307208 | tf_op jit(solution)/shard_map/ppermute | solution.py:464
  30.2 5.6 %collective-permute-start.6 = (f32[200,128]{1,0:T(8,128)}, f32[200,128]{1,0:T(8,128)S(1)}, u32[]{:S(2)}, u32[]{:S(2)}) collective-permute-start(f32[200,128]{1,0:T(8,128)} %get-tuple-element.62), channel_id=1, source_target_pairs={{0,224},{32,0},{64,32},{96,64},{128,96},{160,128},{192,160},{224,1... | collective-permute-start | bytes 307208 | tf_op jit(solution)/shard_map/ppermute | solution.py:464
  31.2 4.6 %collective-permute-start.7 = (f32[200,128]{1,0:T(8,128)}, f32[200,128]{1,0:T(8,128)S(1)}, u32[]{:S(2)}, u32[]{:S(2)}) collective-permute-start(f32[200,128]{1,0:T(8,128)} %get-tuple-element.63), channel_id=1, source_target_pairs={{0,31},{1,0},{2,1},{3,2},{4,3},{5,4},{6,5},{7,6},{8,7},{9,8},{10,9... | collective-permute-start | bytes 307208 | tf_op jit(solution)/shard_map/ppermute | solution.py:464
  35.0 2.1 %copy-start.13 = (f32[200,128]{1,0:T(8,128)}, f32[200,128]{1,0:T(8,128)S(1)}, u32[]{:S(2)}) copy-start(f32[200,128]{1,0:T(8,128)S(1)} %collective-permute-done.4.refs_2_.refs_1_) | copy-start | bytes 307204
  35.0 2.1 %copy-start.14 = (f32[200,128]{1,0:T(8,128)}, f32[200,128]{1,0:T(8,128)S(1)}, u32[]{:S(2)}) copy-start(f32[200,128]{1,0:T(8,128)S(1)} %collective-permute-done.5.refs_3_.refs_2_) | copy-start | bytes 307204
  35.8 1.4 copy-start.15
  35.8 1.4 copy-start.16
  37.2 0.7 copy-start
  40.0 23.6 %all-to-all-start.1 = ((f32[32,16,256]{2,1,0:T(8,128)}), f32[32,16,256]{2,1,0:T(8,128)S(1)}, u32[]{:S(2)}, u32[]{:S(2)}) async-start(f32[32,16,256]{2,1,0:T(8,128)} %spread_kernel.2), calls=%async_computation.1 | async-start | bytes 1048576 | tf_op jit(solution)/shard_map/all_to_all | solution.py:477
  63.7 0.8 copy-start.1
  67.4 13.1 %all-to-all-start.2 = ((f32[32,8,128]{2,1,0:T(8,128)}), f32[32,8,128]{2,1,0:T(8,128)S(1)}, u32[]{:S(2)}, u32[]{:S(2)}) async-start(f32[32,8,128]{2,1,0:T(8,128)} %get-tuple-element.66), calls=%async_computation.2 | async-start | bytes 262144 | tf_op jit(solution)/shard_map/all_to_all | solution.py:477
  71.3 5.8 %collective-permute-start.8 = (f32[200,128]{1,0:T(8,128)}, f32[200,128]{1,0:T(8,128)S(1)}, u32[]{:S(2)}, u32[]{:S(2)}) collective-permute-start(f32[200,128]{1,0:T(8,128)} %get-tuple-element.70), channel_id=1, source_target_pairs={{0,32},{32,64},{64,96},{96,128},{128,160},{160,192},{192,224},{224... | collective-permute-start | bytes 307208 | tf_op jit(solution)/shard_map/ppermute | solution.py:464
  71.8 5.3 %collective-permute-start.9 = (f32[200,128]{1,0:T(8,128)}, f32[200,128]{1,0:T(8,128)S(1)}, u32[]{:S(2)}, u32[]{:S(2)}) collective-permute-start(f32[200,128]{1,0:T(8,128)} %get-tuple-element.71), channel_id=1, source_target_pairs={{0,1},{1,2},{2,3},{3,4},{4,5},{5,6},{6,7},{7,8},{8,9},{9,10},{10,1... | collective-permute-start | bytes 307208 | tf_op jit(solution)/shard_map/ppermute | solution.py:464
  73.7 4.7 %collective-permute-start.10 = (f32[200,128]{1,0:T(8,128)}, f32[200,128]{1,0:T(8,128)S(1)}, u32[]{:S(2)}, u32[]{:S(2)}) collective-permute-start(f32[200,128]{1,0:T(8,128)} %get-tuple-element.72), channel_id=1, source_target_pairs={{0,224},{32,0},{64,32},{96,64},{128,96},{160,128},{192,160},{224,1... | collective-permute-start | bytes 307208 | tf_op jit(solution)/shard_map/ppermute | solution.py:464
  76.2 4.3 %collective-permute-start.11 = (f32[200,128]{1,0:T(8,128)}, f32[200,128]{1,0:T(8,128)S(1)}, u32[]{:S(2)}, u32[]{:S(2)}) collective-permute-start(f32[200,128]{1,0:T(8,128)} %get-tuple-element.73), channel_id=1, source_target_pairs={{0,31},{1,0},{2,1},{3,2},{4,3},{5,4},{6,5},{7,6},{8,7},{9,8},{10,9... | collective-permute-start | bytes 307208 | tf_op jit(solution)/shard_map/ppermute | solution.py:464
  77.1 3.4 %copy-start.5 = (f32[200,128]{1,0:T(8,128)}, f32[200,128]{1,0:T(8,128)S(1)}, u32[]{:S(2)}) copy-start(f32[200,128]{1,0:T(8,128)S(1)} %collective-permute-done.8.refs_5_.refs_3_) | copy-start | bytes 307204
  77.1 3.4 %copy-start.6 = (f32[200,128]{1,0:T(8,128)}, f32[200,128]{1,0:T(8,128)S(1)}, u32[]{:S(2)}) copy-start(f32[200,128]{1,0:T(8,128)S(1)} %collective-permute-done.9.refs_6_.refs_4_) | copy-start | bytes 307204
  78.4 2.1 %copy-start.7 = (f32[200,128]{1,0:T(8,128)}, f32[200,128]{1,0:T(8,128)S(1)}, u32[]{:S(2)}) copy-start(f32[200,128]{1,0:T(8,128)S(1)} %collective-permute-done.10.refs_7_.refs_5_) | copy-start | bytes 307204
  80.5 0.6 copy-start.8
  80.5 0.7 copy-start.3
  102.4 13.3 %all-to-all-start.4 = ((f32[8,16,128]{2,1,0:T(8,128)}), f32[8,16,128]{2,1,0:T(8,128)S(1)}, u32[]{:S(2)}, u32[]{:S(2)}) async-start(f32[8,16,128]{2,1,0:T(8,128)} %get-tuple-element.78), calls=%async_computation.4 | async-start | bytes 131072 | tf_op jit(solution)/shard_map/all_to_all | solution.py:477
  105.8 6.8 %collective-permute-start.12 = (f32[200,128]{1,0:T(8,128)}, f32[200,128]{1,0:T(8,128)S(1)}, u32[]{:S(2)}, u32[]{:S(2)}) collective-permute-start(f32[200,128]{1,0:T(8,128)} %get-tuple-element.79), channel_id=1, source_target_pairs={{0,32},{32,64},{64,96},{96,128},{128,160},{160,192},{192,224},{224... | collective-permute-start | bytes 307208 | tf_op jit(solution)/shard_map/ppermute | solution.py:464
  107.2 5.4 %collective-permute-start.13 = (f32[200,128]{1,0:T(8,128)}, f32[200,128]{1,0:T(8,128)S(1)}, u32[]{:S(2)}, u32[]{:S(2)}) collective-permute-start(f32[200,128]{1,0:T(8,128)} %get-tuple-element.80), channel_id=1, source_target_pairs={{0,1},{1,2},{2,3},{3,4},{4,5},{5,6},{6,7},{7,8},{8,9},{9,10},{10,1... | collective-permute-start | bytes 307208 | tf_op jit(solution)/shard_map/ppermute | solution.py:464
  110.1 4.2 %collective-permute-start.14 = (f32[200,128]{1,0:T(8,128)}, f32[200,128]{1,0:T(8,128)S(1)}, u32[]{:S(2)}, u32[]{:S(2)}) collective-permute-start(f32[200,128]{1,0:T(8,128)} %get-tuple-element.81), channel_id=1, source_target_pairs={{0,224},{32,0},{64,32},{96,64},{128,96},{160,128},{192,160},{224,1... | collective-permute-start | bytes 307208 | tf_op jit(solution)/shard_map/ppermute | solution.py:464
  111.2 4.6 %collective-permute-start.15 = (f32[200,128]{1,0:T(8,128)}, f32[200,128]{1,0:T(8,128)S(1)}, u32[]{:S(2)}, u32[]{:S(2)}) collective-permute-start(f32[200,128]{1,0:T(8,128)} %get-tuple-element.82), channel_id=1, source_target_pairs={{0,31},{1,0},{2,1},{3,2},{4,3},{5,4},{6,5},{7,6},{8,7},{9,8},{10,9... | collective-permute-start | bytes 307208 | tf_op jit(solution)/shard_map/ppermute | solution.py:464
  112.6 3.2 %copy-start.9 = (f32[200,128]{1,0:T(8,128)}, f32[200,128]{1,0:T(8,128)S(1)}, u32[]{:S(2)}) copy-start(f32[200,128]{1,0:T(8,128)S(1)} %collective-permute-done.12.refs_2_.refs_1_) | copy-start | bytes 307204
  112.6 3.2 %copy-start.10 = (f32[200,128]{1,0:T(8,128)}, f32[200,128]{1,0:T(8,128)S(1)}, u32[]{:S(2)}) copy-start(f32[200,128]{1,0:T(8,128)S(1)} %collective-permute-done.13.refs_3_.refs_2_) | copy-start | bytes 307204
  114.3 1.5 copy-start.11
  115.8 0.6 copy-start.12
  116.4 0.6 copy-start.21
  119.0 22.1 %all-to-all-start.5 = ((f32[32,16,256]{2,1,0:T(8,128)}), f32[32,16,256]{2,1,0:T(8,128)S(1)}, u32[]{:S(2)}, u32[]{:S(2)}) async-start(f32[32,16,256]{2,1,0:T(8,128)} %spread_kernel.3), calls=%async_computation.5 | async-start | bytes 1048576 | tf_op jit(solution)/shard_map/all_to_all | solution.py:477
  141.1 0.8 copy-start.2
  144.3 12.9 %all-to-all-start.6 = ((f32[32,8,128]{2,1,0:T(8,128)}), f32[32,8,128]{2,1,0:T(8,128)S(1)}, u32[]{:S(2)}, u32[]{:S(2)}) async-start(f32[32,8,128]{2,1,0:T(8,128)} %get-tuple-element.88), calls=%async_computation.6 | async-start | bytes 262144 | tf_op jit(solution)/shard_map/all_to_all | solution.py:477
  148.2 5.6 %collective-permute-start.16 = (f32[200,128]{1,0:T(8,128)}, f32[200,128]{1,0:T(8,128)S(1)}, u32[]{:S(2)}, u32[]{:S(2)}) collective-permute-start(f32[200,128]{1,0:T(8,128)} %get-tuple-element.92), channel_id=1, source_target_pairs={{0,32},{32,64},{64,96},{96,128},{128,160},{160,192},{192,224},{224... | collective-permute-start | bytes 307208 | tf_op jit(solution)/shard_map/ppermute | solution.py:464
  148.6 5.2 %collective-permute-start.17 = (f32[200,128]{1,0:T(8,128)}, f32[200,128]{1,0:T(8,128)S(1)}, u32[]{:S(2)}, u32[]{:S(2)}) collective-permute-start(f32[200,128]{1,0:T(8,128)} %get-tuple-element.93), channel_id=1, source_target_pairs={{0,1},{1,2},{2,3},{3,4},{4,5},{5,6},{6,7},{7,8},{8,9},{9,10},{10,1... | collective-permute-start | bytes 307208 | tf_op jit(solution)/shard_map/ppermute | solution.py:464
  150.5 4.5 %collective-permute-start.18 = (f32[200,128]{1,0:T(8,128)}, f32[200,128]{1,0:T(8,128)S(1)}, u32[]{:S(2)}, u32[]{:S(2)}) collective-permute-start(f32[200,128]{1,0:T(8,128)} %get-tuple-element.94), channel_id=1, source_target_pairs={{0,224},{32,0},{64,32},{96,64},{128,96},{160,128},{192,160},{224,1... | collective-permute-start | bytes 307208 | tf_op jit(solution)/shard_map/ppermute | solution.py:464
  152.9 4.3 %collective-permute-start.19 = (f32[200,128]{1,0:T(8,128)}, f32[200,128]{1,0:T(8,128)S(1)}, u32[]{:S(2)}, u32[]{:S(2)}) collective-permute-start(f32[200,128]{1,0:T(8,128)} %get-tuple-element.95), channel_id=1, source_target_pairs={{0,31},{1,0},{2,1},{3,2},{4,3},{5,4},{6,5},{7,6},{8,7},{9,8},{10,9... | collective-permute-start | bytes 307208 | tf_op jit(solution)/shard_map/ppermute | solution.py:464
  153.8 3.4 %copy-start.17 = (f32[200,128]{1,0:T(8,128)}, f32[200,128]{1,0:T(8,128)S(1)}, u32[]{:S(2)}) copy-start(f32[200,128]{1,0:T(8,128)S(1)} %collective-permute-done.16.refs_6_.refs_5_) | copy-start | bytes 307204
  153.8 3.4 %copy-start.18 = (f32[200,128]{1,0:T(8,128)}, f32[200,128]{1,0:T(8,128)S(1)}, u32[]{:S(2)}) copy-start(f32[200,128]{1,0:T(8,128)S(1)} %collective-permute-done.17.refs_7_.refs_6_) | copy-start | bytes 307204
  155.0 2.1 %copy-start.19 = (f32[200,128]{1,0:T(8,128)}, f32[200,128]{1,0:T(8,128)S(1)}, u32[]{:S(2)}) copy-start(f32[200,128]{1,0:T(8,128)S(1)} %collective-permute-done.18.refs_8_.refs_7_) | copy-start | bytes 307204
  157.2 0.6 copy-start.20
  157.2 0.7 copy-start.4

commit v2 on v1

--- a/solution.py
+++ b/solution.py
@@ -15,6 +15,7 @@
 GX, GYN = 8, 32
 CHUNK = 16
 NODES = 2 * GX * GYN
+VMEM_LIMIT = 55_000_000
 E_LANE, ID_LANE = 120, 121
 F32, BF16 = jnp.float32, jnp.bfloat16
 
@@ -303,7 +304,7 @@
     face = rhs_ref.shape[1]
     row = lax.broadcasted_iota(jnp.int32, (face, face), 0)
     for a, (plus, minus) in enumerate(((plus_x, minus_x), (plus_y, minus_y))):
-        table = jnp.where(row == pairing_ref[a : a + 1, :], 1.0, 0.0).astype(BF16)
+        table = jnp.where(row == pairing_ref[a], 1.0, 0.0).astype(BF16)
         table_ref[a] = table
         plus[0:face, :] = wide_sum(dot(table, wide_two(rhs_ref[a])))
         moved = dot_rows(coupling_of(phi_ref, 2 * a + 1, face).astype(BF16), table)
@@ -313,9 +314,28 @@
         minus[...] = coupling_of(phi_ref, 2 * a, face)
 
 
+def rows_by_component(rows_ref, held_ref):
+    source = lax.broadcasted_iota(jnp.int32, (128, 384), 0)
+    target = lax.broadcasted_iota(jnp.int32, (128, 384), 1)
+    wanted = 3 * (target % 128) + target // 128
+    total = jnp.zeros((24, 384), F32)
+    for m in range(3):
+        chosen = jnp.where(wanted == 128 * m + source, 1.0, 0.0).astype(BF16)
+        part = [rows_ref[:, (3 * q + m) * 128 : (3 * q + m + 1) * 128] for q in range(4)]
+        part = jnp.concatenate(part, axis=0)
+        high = part.astype(BF16)
+        total += dot(high, chosen) + dot((part - high.astype(F32)).astype(BF16), chosen)
+    for q in range(4):
+        for column in range(3):
+            for i in range(3):
+                for b in range(2):
+                    at = q * 18 + column * 6 + i * 2 + b
+                    held_ref[at : at + 1, :] = total[q * 6 + b * 3 + i : q * 6 + b * 3 + i + 1, column * 128 : (column + 1) * 128]
+
+
 def first_kernel(
     ids_ref, rhs_ref, below_x, below_y, above_x, above_y, phi_ref, table_ref, matrix_ref, rows_ref,
-    half_ref, solved_ref, reach_ref, up_x, up_y, low_x, low_y, out_ref,
+    half_ref, solved_ref, reach_ref, up_x, up_y, low_x, low_y, out_ref, held_ref,
 ):
     face = rhs_ref.shape[1]
     none = jnp.zeros((face, 128), F32)
@@ -338,9 +358,10 @@
         near(2 * a, 2 + 2 * a, under[:, :face])
     energy = column_sum(half_ref[...], solved_ref[...])
     loads = loads_of(solved_ref, reach_ref, energy, (ids_ref[0], ids_ref[4]), face)
+    rows_by_component(rows_ref, held_ref)
     for x in range(GX):
         out_ref[x, 0:CHUNK, :] = loads[x * CHUNK : (x + 1) * CHUNK]
-        out_ref[x, CHUNK : CHUNK + 72, :] = rows_ref[...]
+        out_ref[x, CHUNK : CHUNK + 72, :] = held_ref[...]
 
 
 def stretch_kernel(
@@ -424,7 +445,7 @@
     out_ref[...] = column_sum(held_ref[...], solved)
 
 
-def call(kernel, outs, smem=0, scratch=(), flops=2_000_000):
+def call(kernel, outs, smem=0, scratch=(), flops=2_000_000, limit=VMEM_LIMIT):
     vmem = pl.BlockSpec(memory_space=pltpu.VMEM)
 
     def run(*operands, after=()):
@@ -441,6 +462,7 @@
             in_specs=specs + [pl.BlockSpec(memory_space=pl.ANY)] * len(after),
             out_specs=[vmem] * len(outs),
             scratch_shapes=list(scratch),
+            compiler_params=pltpu.CompilerParams(vmem_limit_bytes=limit),
             cost_estimate=pl.CostEstimate(flops=flops, bytes_accessed=1_000_000, transcendentals=0),
         )(*operands, *after)
 
@@ -483,25 +505,25 @@
     rhs = rhs[0, 0, 0]
     stiffness = stiff_inverse[0, 0, 0]
     schur_block = schur[0, 0, 0]
-    pairing = pairing[0, 0, 0]
+    pairing = pairing[0, 0, 0].reshape(3, 1, face)
     coupling = phi[0, 0, 0]
     me = lax.axis_index(GY).astype(jnp.int32).reshape(1)
     lanes = (jnp.asarray(corner_lanes())[:, None] == jnp.arange(256)[None, :]).astype(BF16)
-    mine = coarse_inverse.reshape(2, 3, 4, 128, 3)
-    mine = jnp.transpose(mine, (2, 4, 1, 0, 3)).reshape(72, 128)
-
     whole, upper, faces = ((interface, 128), F32), ((3, face, 128), F32), [((face, 128), F32)] * 4
     big = 2 * interface * interface * 128
     *sent, table = call(
-        start_kernel, [((face + 48, 128), F32)] * 2 + [((24, face), F32)] * 2 + [((2, face, face), BF16)]
+        start_kernel, [((face + 48, 128), F32)] * 2 + [((24, face), F32)] * 2 + [((2, face, face), BF16)],
+        limit=None,
     )(rhs, pairing, coupling)
     received = passed_both_ways(*sent)
     half, solved, reach, *sent, message = call(
         first_kernel,
         [whole, whole, ((4, 128, face), BF16), *faces, ((GX, CHUNK + 72, 128), F32)],
         smem=1,
+        scratch=[pltpu.VMEM((72, 128), F32)],
         flops=big,
-    )(incidence[0, 0, 0], rhs, *received, coupling, table, schur_block, mine)
+        limit=None,
+    )(incidence[0, 0, 0], rhs, *received, coupling, table, schur_block, coarse_inverse)
     received = passed_both_ways(*sent)
     first_rows = exchanged(message, "gx")
     (sent,) = spread(first_rows, lanes, after=received)

time: 205 us -> 186 us (0.907)
  local copies, waits for them, and re-layouts: 10.9 us -> 2.29 us
  Pallas kernels: 40.7 us -> 32.8 us
  waiting for transfers between devices: 28 us -> 34 us
  starting transfers between devices: 71.5 us -> 67.2 us
    pallas_call x12, Pallas kernels: 40.7 us -> 32.8 us  [run(): pl.pallas_call(body, name=kernel.__name__, out_shape=[jax.ShapeDtypeStruc...]
    ppermute x20, waiting for transfers between devices: 13.2 us -> 20.8 us  [passed_along(): lax.ppermute(array, axis, [(i, (i + by) % peers) for i in range(peers)])]
    unnamed x55 -> x18, local copies, waits for them, and re-layouts: 6.9 us -> 2.22 us
    all_to_all x6, starting transfers between devices: 39.8 us -> 37.6 us  [exchanged(): return lax.all_to_all(array, axis, split_axis=0, concat_axis=0, tiled=True)]
    reshape x1 -> x0, local copies, waits for them, and re-layouts: 2.23 us -> none  [local(): mine = coarse_inverse.reshape(2, 3, 4, 128, 3)]
  transfers between devices with their start and end apart: 26 -> 26, of which waited for: 14 -> 13; matrix products, arithmetic and copies ran while one was open for 2% -> 0% of each run, Pallas kernels for 5% -> 5%
where the time goes in v2:
time: 186 us
  starting transfers between devices  67.2 us (36%)
  blocking collectives  47.9 us (26%)
  waiting for transfers between devices  34 us (18%)
  Pallas kernels  32.8 us (18%)
  local copies, waits for them, and re-layouts  2.29 us (1%)
    all_to_all x3, blocking collectives, exchanged(): return lax.all_to_all(array, axis, split_axis=0, concat_axis=0, tiled=True)  47.9 us
    all_to_all x6, starting transfers between devices, exchanged(): return lax.all_to_all(array, axis, split_axis=0, concat_axis=0, tiled=True)  37.6 us
    pallas_call x12, Pallas kernels, run(): pl.pallas_call(body, name=kernel.__name__, out_shape=[jax.ShapeDtypeStruc...  32.8 us
    ppermute x20, starting transfers between devices, passed_along(): lax.ppermute(array, axis, [(i, (i + by) % peers) for i in range(peers)])  29.7 us
    ppermute x20, waiting for transfers between devices, passed_along(): lax.ppermute(array, axis, [(i, (i + by) % peers) for i in range(peers)])  20.8 us
    all_to_all x6, waiting for transfers between devices, exchanged(): return lax.all_to_all(array, axis, split_axis=0, concat_axis=0, tiled=True)  13.2 us
  transfers between devices with their start and end apart: 26, of which 13 were waited for; matrix products, arithmetic and copies ran while one was open for 0% of the time, Pallas kernels for 5%

profile of v2, /device:TPU:1, one launch (start us, length us, event | category | flops | bytes accessed | tf_op | source)
XLA Modules:
  0.0 185.7 jit_solution(15691646276950750851)
XLA Ops:
  0.6 0.0 copy-start.8
  0.6 2.0 %start_kernel.1 = (f32[248,128]{1,0:T(8,128)}, f32[248,128]{1,0:T(8,128)}, f32[24,200]{1,0:T(8,128)}, f32[24,200]{1,0:T(8,128)}, bf16[2,200,200]{2,1,0:T(8,128)(2,1)}) custom-call(f32[3,200,128]{2,1,0:T(8,128)} %bitcast.18, s32[3,1,200]{2,1,0:T(1,128)} %bitcast.23, bf16[24,1200]{1,0:T(8,128)(2,1)} %bitcast.21), custom_call_target="tpu_custom_call" | custom-call | flops 2000000 | bytes 1000000 | tf_op jit(solution)/shard_map/start_kernel/pallas_call | solution.py:458
  2.6 2.5 %collective-permute-start = (f32[248,128]{1,0:T(8,128)}, f32[248,128]{1,0:T(8,128)S(1)}, u32[]{:S(2)}, u32[]{:S(2)}) collective-permute-start(f32[248,128]{1,0:T(8,128)} %get-tuple-element.54), channel_id=1, source_target_pairs={{0,32},{32,64},{64,96},{96,128},{128,160},{160,192},{192,224},{224... | collective-permute-start | bytes 380936 | tf_op jit(solution)/shard_map/ppermute | solution.py:486
  5.1 2.1 %collective-permute-start.1 = (f32[248,128]{1,0:T(8,128)}, f32[248,128]{1,0:T(8,128)S(1)}, u32[]{:S(2)}, u32[]{:S(2)}) collective-permute-start(f32[248,128]{1,0:T(8,128)} %get-tuple-element.55), channel_id=1, source_target_pairs={{0,1},{1,2},{2,3},{3,4},{4,5},{5,6},{6,7},{7,8},{8,9},{9,10},{10,1... | collective-permute-start | bytes 380936 | tf_op jit(solution)/shard_map/ppermute | solution.py:486
  7.1 3.7 %collective-permute-start.2 = (f32[24,200]{1,0:T(8,128)}, f32[24,200]{1,0:T(8,128)S(1)}, u32[]{:S(2)}, u32[]{:S(2)}) collective-permute-start(f32[24,200]{1,0:T(8,128)} %get-tuple-element.56), channel_id=1, source_target_pairs={{0,224},{32,0},{64,32},{96,64},{128,96},{160,128},{192,160},{224,1... | collective-permute-start | bytes 57608 | tf_op jit(solution)/shard_map/ppermute | solution.py:486
  10.8 0.0 collective-permute-start.3
  10.8 1.2 collective-permute-done.2.refs_4_
  11.9 2.3 %collective-permute-done.3.refs_5_ = f32[24,200]{1,0:T(8,128)S(1)} collective-permute-done((f32[24,200]{1,0:T(8,128)}, f32[24,200]{1,0:T(8,128)S(1)}, u32[]{:S(2)}, u32[]{:S(2)}) %collective-permute-start.3) | collective-permute-done | bytes 19232 | tf_op jit(solution)/shard_map/ppermute | solution.py:486
  14.2 0.0 collective-permute-done.refs_2_
  14.3 0.6 copy-done.7
  14.8 0.0 copy-done.4
  14.9 0.1 copy-done.5
  14.9 4.8 %first_kernel.1 = (f32[1200,128]{1,0:T(8,128)}, f32[1200,128]{1,0:T(8,128)}, bf16[4,128,200]{2,1,0:T(8,128)(2,1)}, f32[200,128]{1,0:T(8,128)}, f32[200,128]{1,0:...) custom-call(s32[8]{0:T(128)} %bitcast.24, f32[3,200,128]{2,1,0:T(8,128)} %bitcast.19, ...), custom_call_target="tpu_custom_call" | custom-call | flops 368640000 | bytes 1000000 | tf_op jit(solution)/shard_map/first_kernel/pallas_call | solution.py:458
  19.8 5.9 %all-to-all-start = ((f32[8,88,128]{2,1,0:T(8,128)}), f32[8,88,128]{2,1,0:T(8,128)S(1)}, u32[]{:S(2)}, u32[]{:S(2)}) async-start(f32[8,88,128]{2,1,0:T(8,128)} %get-tuple-element.59), calls=%async_computation | async-start | bytes 720896 | tf_op jit(solution)/shard_map/all_to_all | solution.py:499
  25.7 1.5 collective-permute-start.4
  27.1 0.7 collective-permute-start.5
  27.8 1.0 collective-permute-start.6
  28.8 2.4 %collective-permute-start.7 = (f32[200,128]{1,0:T(8,128)}, f32[200,128]{1,0:T(8,128)S(1)}, u32[]{:S(2)}, u32[]{:S(2)}) collective-permute-start(f32[200,128]{1,0:T(8,128)} %get-tuple-element.63), channel_id=1, source_target_pairs={{0,31},{1,0},{2,1},{3,2},{4,3},{5,4},{6,5},{7,6},{8,7},{9,8},{10,9... | collective-permute-start | bytes 307208 | tf_op jit(solution)/shard_map/ppermute | solution.py:486
  31.2 0.1 fusion.refs_1_.refs_4_
  31.3 6.2 %collective-permute-done.4.refs_2_.refs_1_ = f32[200,128]{1,0:T(8,128)S(1)} collective-permute-done((f32[200,128]{1,0:T(8,128)}, f32[200,128]{1,0:T(8,128)S(1)}, u32[]{:S(2)}, u32[]{:S(2)}) %collective-permute-start.4) | collective-permute-done | bytes 102432 | tf_op jit(solution)/shard_map/ppermute | solution.py:486
  37.5 1.1 spread_kernel.2
  38.6 9.9 %all-to-all-start.1 = ((f32[32,16,256]{2,1,0:T(8,128)}), f32[32,16,256]{2,1,0:T(8,128)S(1)}, u32[]{:S(2)}, u32[]{:S(2)}) async-start(f32[32,16,256]{2,1,0:T(8,128)} %spread_kernel.2), calls=%async_computation.1 | async-start | bytes 1048576 | tf_op jit(solution)/shard_map/all_to_all | solution.py:499
  48.6 0.0 copy-start.1
  48.6 4.3 %stretch_kernel.2 = (f32[1200,128]{1,0:T(8,128)}, f32[1200,128]{1,0:T(8,128)}, f32[3,200,128]{2,1,0:T(8,128)S(1)}, f32[200,128]{1,0:T(8,128)S(1)}, f32[200,128]{...) custom-call(f32[1200,128]{1,0:T(8,128)} %get-tuple-element.64.refs_0_, ...), custom_call_target="tpu_custom_call" | custom-call | flops 368640000 | bytes 1000000 | tf_op jit(solution)/shard_map/stretch_kernel/pallas_call | solution.py:458
  52.9 7.1 %all-to-all-done.1.refs_1_ = f32[32,16,256]{2,1,0:T(8,128)S(1)} async-done(((f32[32,16,256]{2,1,0:T(8,128)}), f32[32,16,256]{2,1,0:T(8,128)S(1)}, u32[]{:S(2)}, u32[]{:S(2)}) %all-to-all-start.1) | async-done | bytes 524320 | tf_op jit(solution)/shard_map/all_to_all | solution.py:499
  60.0 0.8 copy-done.3
  60.8 2.8 %first_solve_kernel.1 = (f32[32,8,128]{2,1,0:T(8,128)}, f32[16,1536]{1,0:T(8,128)S(1)}, f32[16,128]{1,0:T(8,128)S(1)}, bf16[144,512]{1,0:T(8,128)(2,1)S(1)}, bf1...) custom-call(s32[1]{0:T(128)} %bitcast.refs_0_, f32[32,16,256]{2,1,0:T(8,128)} %copy-done.3, ...), custom_call_target="tpu_custom_call" | custom-call | flops 2000000 | bytes 1000000 | tf_op jit(solution)/shard_map/first_solve_kernel/pallas_call | solution.py:458
  63.5 3.9 %all-to-all-start.2 = ((f32[32,8,128]{2,1,0:T(8,128)}), f32[32,8,128]{2,1,0:T(8,128)S(1)}, u32[]{:S(2)}, u32[]{:S(2)}) async-start(f32[32,8,128]{2,1,0:T(8,128)} %get-tuple-element.66), calls=%async_computation.2 | async-start | bytes 262144 | tf_op jit(solution)/shard_map/all_to_all | solution.py:499
  67.4 0.4 collective-permute-start.8
  67.8 1.9 %collective-permute-start.9 = (f32[200,128]{1,0:T(8,128)S(1)}, f32[200,128]{1,0:T(8,128)S(1)}, u32[]{:S(2)}, u32[]{:S(2)}) collective-permute-start(f32[200,128]{1,0:T(8,128)S(1)} %get-tuple-element.71), channel_id=1, source_target_pairs={{0,1},{1,2},{2,3},{3,4},{4,5},{5,6},{6,7},{7,8},{8,9},{9,10},{10,1... | collective-permute-start | bytes 307208 | tf_op jit(solution)/shard_map/ppermute | solution.py:486
  69.7 2.4 %collective-permute-start.10 = (f32[200,128]{1,0:T(8,128)S(1)}, f32[200,128]{1,0:T(8,128)S(1)}, u32[]{:S(2)}, u32[]{:S(2)}) collective-permute-start(f32[200,128]{1,0:T(8,128)S(1)} %get-tuple-element.72), channel_id=1, source_target_pairs={{0,224},{32,0},{64,32},{96,64},{128,96},{160,128},{192,160},{224,1... | collective-permute-start | bytes 307208 | tf_op jit(solution)/shard_map/ppermute | solution.py:486
  72.1 0.7 collective-permute-done.8.refs_5_.refs_3_
  72.8 1.2 collective-permute-done.10.refs_7_.refs_5_
  74.0 2.2 %collective-permute-done.11.refs_8_.refs_6_ = f32[200,128]{1,0:T(8,128)S(1)} collective-permute-done((f32[200,128]{1,0:T(8,128)S(1)}, f32[200,128]{1,0:T(8,128)S(1)}, u32[]{:S(2)}, u32[]{:S(2)}) %collective-permute-start.11) | collective-permute-done | bytes 102432 | tf_op jit(solution)/shard_map/ppermute | solution.py:486
  76.2 0.8 pick_kernel.2
  77.0 11.9 %all_to_all.45.refs_0_ = f32[8,24,128]{2,1,0:T(8,128)S(1)} all-to-all(f32[8,24,128]{2,1,0:T(8,128)S(1)} %get-tuple-element.74), channel_id=1, replica_groups=mesh['gx'=8,'gy_0'=4,'gy_1'=4,'gy_2'=2] {'gx'}, dimensions={0} | all-to-all | bytes 196608 | tf_op jit(solution)/shard_map/all_to_all | solution.py:499
  88.9 4.9 %turn_kernel.1 = (f32[1200,128]{1,0:T(8,128)}, f32[1200,128]{1,0:T(8,128)}, f32[1200,128]{1,0:T(8,128)}, f32[128,128]{1,0:T(8,128)S(1)}, f32[8,128]{1,0:T(8,128)...) custom-call(f32[8,24,128]{2,1,0:T(8,128)S(1)} %all_to_all.45.refs_0_, ...), custom_call_target="tpu_custom_call" | custom-call | flops 368640000 | bytes 1000000 | tf_op jit(solution)/shard_map/turn_kernel/pallas_call | solution.py:458
  93.8 3.4 %all-to-all-start.4 = ((f32[8,16,128]{2,1,0:T(8,128)}), f32[8,16,128]{2,1,0:T(8,128)S(1)}, u32[]{:S(2)}, u32[]{:S(2)}) async-start(f32[8,16,128]{2,1,0:T(8,128)} %get-tuple-element.78), calls=%async_computation.4 | async-start | bytes 131072 | tf_op jit(solution)/shard_map/all_to_all | solution.py:499
  97.2 1.4 collective-permute-start.12
  98.5 2.7 %collective-permute-start.13 = (f32[200,128]{1,0:T(8,128)S(1)}, f32[200,128]{1,0:T(8,128)S(1)}, u32[]{:S(2)}, u32[]{:S(2)}) collective-permute-start(f32[200,128]{1,0:T(8,128)S(1)} %get-tuple-element.80), channel_id=1, source_target_pairs={{0,1},{1,2},{2,3},{3,4},{4,5},{5,6},{6,7},{7,8},{8,9},{9,10},{10,1... | collective-permute-start | bytes 307208 | tf_op jit(solution)/shard_map/ppermute | solution.py:486
  101.2 1.1 collective-permute-start.14
  102.3 1.4 collective-permute-start.15
  103.8 1.6 collective-permute-done.14.refs_4_.refs_3_
  105.3 1.4 collective-permute-done.15.refs_5_.refs_4_
  106.7 1.1 spread_kernel.3
  107.9 10.7 %all-to-all-start.5 = ((f32[32,16,256]{2,1,0:T(8,128)}), f32[32,16,256]{2,1,0:T(8,128)S(1)}, u32[]{:S(2)}, u32[]{:S(2)}) async-start(f32[32,16,256]{2,1,0:T(8,128)} %spread_kernel.3), calls=%async_computation.5 | async-start | bytes 1048576 | tf_op jit(solution)/shard_map/all_to_all | solution.py:499
  118.5 4.6 %stretch_kernel.3 = (f32[1200,128]{1,0:T(8,128)}, f32[1200,128]{1,0:T(8,128)}, f32[3,200,128]{2,1,0:T(8,128)S(1)}, f32[200,128]{1,0:T(8,128)S(1)}, f32[200,128]{...) custom-call(f32[1200,128]{1,0:T(8,128)} %get-tuple-element.85.refs_0_, ...), custom_call_target="tpu_custom_call" | custom-call | flops 368640000 | bytes 1000000 | tf_op jit(solution)/shard_map/stretch_kernel/pallas_call | solution.py:458
  123.1 0.7 copy-done.2
  123.8 6.1 %all-to-all-done.5.refs_1_ = f32[32,16,256]{2,1,0:T(8,128)S(1)} async-done(((f32[32,16,256]{2,1,0:T(8,128)}), f32[32,16,256]{2,1,0:T(8,128)S(1)}, u32[]{:S(2)}, u32[]{:S(2)}) %all-to-all-start.5) | async-done | bytes 524320 | tf_op jit(solution)/shard_map/all_to_all | solution.py:499
  130.0 1.2 next_solve_kernel.1
  131.2 3.9 %all-to-all-start.6 = ((f32[32,8,128]{2,1,0:T(8,128)}), f32[32,8,128]{2,1,0:T(8,128)S(1)}, u32[]{:S(2)}, u32[]{:S(2)}) async-start(f32[32,8,128]{2,1,0:T(8,128)} %get-tuple-element.88), calls=%async_computation.6 | async-start | bytes 262144 | tf_op jit(solution)/shard_map/all_to_all | solution.py:499
  135.1 0.4 collective-permute-start.16
  135.5 1.9 %collective-permute-start.17 = (f32[200,128]{1,0:T(8,128)S(1)}, f32[200,128]{1,0:T(8,128)S(1)}, u32[]{:S(2)}, u32[]{:S(2)}) collective-permute-start(f32[200,128]{1,0:T(8,128)S(1)} %get-tuple-element.93), channel_id=1, source_target_pairs={{0,1},{1,2},{2,3},{3,4},{4,5},{5,6},{6,7},{7,8},{8,9},{9,10},{10,1... | collective-permute-start | bytes 307208 | tf_op jit(solution)/shard_map/ppermute | solution.py:486
  137.5 2.3 %collective-permute-start.18 = (f32[200,128]{1,0:T(8,128)S(1)}, f32[200,128]{1,0:T(8,128)S(1)}, u32[]{:S(2)}, u32[]{:S(2)}) collective-permute-start(f32[200,128]{1,0:T(8,128)S(1)} %get-tuple-element.94), channel_id=1, source_target_pairs={{0,224},{32,0},{64,32},{96,64},{128,96},{160,128},{192,160},{224,1... | collective-permute-start | bytes 307208 | tf_op jit(solution)/shard_map/ppermute | solution.py:486
  139.8 0.0 collective-permute-start.19
  139.8 0.7 collective-permute-done.16.refs_6_.refs_5_
  140.5 1.2 collective-permute-done.18.refs_8_.refs_7_
  141.7 2.2 %collective-permute-done.19.refs_9_.refs_8_ = f32[200,128]{1,0:T(8,128)S(1)} collective-permute-done((f32[200,128]{1,0:T(8,128)S(1)}, f32[200,128]{1,0:T(8,128)S(1)}, u32[]{:S(2)}, u32[]{:S(2)}) %collective-permute-start.19) | collective-permute-done | bytes 102432 | tf_op jit(solution)/shard_map/ppermute | solution.py:486
  143.9 1.2 pick_kernel.3
  145.1 14.2 %all_to_all.46.refs_0_ = f32[8,24,128]{2,1,0:T(8,128)S(1)} all-to-all(f32[8,24,128]{2,1,0:T(8,128)S(1)} %get-tuple-element.96), channel_id=1, replica_groups=mesh['gx'=8,'gy_0'=4,'gy_1'=4,'gy_2'=2] {'gx'}, dimensions={0} | all-to-all | bytes 196608 | tf_op jit(solution)/shard_map/all_to_all | solution.py:499
  159.3 4.0 %last_kernel.1 = (f32[3,200,128]{2,1,0:T(8,128)}, f32[1,128]{1,0:T(1,128)S(1)}) custom-call(f32[8,24,128]{2,1,0:T(8,128)S(1)} %all_to_all.46.refs_0_, f32[1200,128]{1,0:T(8,128)} %get-tuple-element.97.refs_1_, f32[3,200,128]{2,1,0:T(8,128)S(1)} %get-tuple-element.98.refs_2_, f32[3,200,128]{2,1,0:T(8,128)} %copy-done.2, ...), custom_call_target="tpu_custom_call" | custom-call | flops 368640000 | bytes 1000000 | tf_op jit(solution)/shard_map/last_kernel/pallas_call | solution.py:458
  163.3 0.1 broadcast_in_dim.9
  163.4 21.7 %all_to_all.47 = f32[256,1,128]{2,1,0:T(1,128)S(1)} all-to-all(f32[256,1,128]{2,1,0:T(1,128)S(1)} %broadcast_in_dim.9), channel_id=1, replica_groups=mesh['gx'=8,'gy_0'=4,'gy_1'=4,'gy_2'=2] {'gx','gy_0','gy_1','gy_2'}, dimensions={0} | all-to-all | bytes 262144 | tf_op jit(solution)/shard_map/all_to_all | solution.py:499
  185.2 0.5 bitcast_divide_fusion
  (25 shorter events, 0.1 us)
Async XLA Ops:
  0.6 30.6 %copy-start.8 = (s32[128]{0:T(128)S(1)}, s32[128]{0:T(128)}, u32[]{:S(2)}) copy-start(s32[128]{0:T(128)} %constant.19.clone) | copy-start | bytes 1540
  2.6 11.6 %collective-permute-start = (f32[248,128]{1,0:T(8,128)}, f32[248,128]{1,0:T(8,128)S(1)}, u32[]{:S(2)}, u32[]{:S(2)}) collective-permute-start(f32[248,128]{1,0:T(8,128)} %get-tuple-element.54), channel_id=1, source_target_pairs={{0,32},{32,64},{64,96},{96,128},{128,160},{160,192},{192,224},{224... | collective-permute-start | bytes 380936 | tf_op jit(solution)/shard_map/ppermute | solution.py:486
  5.1 9.2 %collective-permute-start.1 = (f32[248,128]{1,0:T(8,128)}, f32[248,128]{1,0:T(8,128)S(1)}, u32[]{:S(2)}, u32[]{:S(2)}) collective-permute-start(f32[248,128]{1,0:T(8,128)} %get-tuple-element.55), channel_id=1, source_target_pairs={{0,1},{1,2},{2,3},{3,4},{4,5},{5,6},{6,7},{7,8},{8,9},{9,10},{10,1... | collective-permute-start | bytes 380936 | tf_op jit(solution)/shard_map/ppermute | solution.py:486
  7.1 4.8 %collective-permute-start.2 = (f32[24,200]{1,0:T(8,128)}, f32[24,200]{1,0:T(8,128)S(1)}, u32[]{:S(2)}, u32[]{:S(2)}) collective-permute-start(f32[24,200]{1,0:T(8,128)} %get-tuple-element.56), channel_id=1, source_target_pairs={{0,224},{32,0},{64,32},{96,64},{128,96},{160,128},{192,160},{224,1... | collective-permute-start | bytes 57608 | tf_op jit(solution)/shard_map/ppermute | solution.py:486
  10.8 3.5 %collective-permute-start.3 = (f32[24,200]{1,0:T(8,128)}, f32[24,200]{1,0:T(8,128)S(1)}, u32[]{:S(2)}, u32[]{:S(2)}) collective-permute-start(f32[24,200]{1,0:T(8,128)} %get-tuple-element.57), channel_id=1, source_target_pairs={{0,31},{1,0},{2,1},{3,2},{4,3},{5,4},{6,5},{7,6},{8,7},{9,8},{10,9... | collective-permute-start | bytes 57608 | tf_op jit(solution)/shard_map/ppermute | solution.py:486
  11.9 2.3 %copy-start.6 = (f32[24,200]{1,0:T(8,128)}, f32[24,200]{1,0:T(8,128)S(1)}, u32[]{:S(2)}) copy-start(f32[24,200]{1,0:T(8,128)S(1)} %collective-permute-done.2.refs_4_) | copy-start | bytes 57604
  14.2 0.6 copy-start.7
  14.2 0.6 copy-start.4
  14.3 0.7 copy-start.5
  14.9 33.6 %copy-start = (bf16[2,200,200]{2,1,0:T(8,128)(2,1)S(1)}, bf16[2,200,200]{2,1,0:T(8,128)(2,1)}, u32[]{:S(2)}) copy-start(bf16[2,200,200]{2,1,0:T(8,128)(2,1)} %get-tuple-element.58.refs_7_.refs_5_.refs_12_) | copy-start | bytes 480004
  19.8 17.7 %all-to-all-start = ((f32[8,88,128]{2,1,0:T(8,128)}), f32[8,88,128]{2,1,0:T(8,128)S(1)}, u32[]{:S(2)}, u32[]{:S(2)}) async-start(f32[8,88,128]{2,1,0:T(8,128)} %get-tuple-element.59), calls=%async_computation | async-start | bytes 720896 | tf_op jit(solution)/shard_map/all_to_all | solution.py:499
  25.7 11.8 %collective-permute-start.4 = (f32[200,128]{1,0:T(8,128)}, f32[200,128]{1,0:T(8,128)S(1)}, u32[]{:S(2)}, u32[]{:S(2)}) collective-permute-start(f32[200,128]{1,0:T(8,128)} %get-tuple-element.60), channel_id=1, source_target_pairs={{0,32},{32,64},{64,96},{96,128},{128,160},{160,192},{192,224},{224... | collective-permute-start | bytes 307208 | tf_op jit(solution)/shard_map/ppermute | solution.py:486
  27.1 10.4 %collective-permute-start.5 = (f32[200,128]{1,0:T(8,128)}, f32[200,128]{1,0:T(8,128)S(1)}, u32[]{:S(2)}, u32[]{:S(2)}) collective-permute-start(f32[200,128]{1,0:T(8,128)} %get-tuple-element.61), channel_id=1, source_target_pairs={{0,1},{1,2},{2,3},{3,4},{4,5},{5,6},{6,7},{7,8},{8,9},{9,10},{10,1... | collective-permute-start | bytes 307208 | tf_op jit(solution)/shard_map/ppermute | solution.py:486
  27.8 9.7 %collective-permute-start.6 = (f32[200,128]{1,0:T(8,128)}, f32[200,128]{1,0:T(8,128)S(1)}, u32[]{:S(2)}, u32[]{:S(2)}) collective-permute-start(f32[200,128]{1,0:T(8,128)} %get-tuple-element.62), channel_id=1, source_target_pairs={{0,224},{32,0},{64,32},{96,64},{128,96},{160,128},{192,160},{224,1... | collective-permute-start | bytes 307208 | tf_op jit(solution)/shard_map/ppermute | solution.py:486
  28.8 8.7 %collective-permute-start.7 = (f32[200,128]{1,0:T(8,128)}, f32[200,128]{1,0:T(8,128)S(1)}, u32[]{:S(2)}, u32[]{:S(2)}) collective-permute-start(f32[200,128]{1,0:T(8,128)} %get-tuple-element.63), channel_id=1, source_target_pairs={{0,31},{1,0},{2,1},{3,2},{4,3},{5,4},{6,5},{7,6},{8,7},{9,8},{10,9... | collective-permute-start | bytes 307208 | tf_op jit(solution)/shard_map/ppermute | solution.py:486
  38.6 21.4 %all-to-all-start.1 = ((f32[32,16,256]{2,1,0:T(8,128)}), f32[32,16,256]{2,1,0:T(8,128)S(1)}, u32[]{:S(2)}, u32[]{:S(2)}) async-start(f32[32,16,256]{2,1,0:T(8,128)} %spread_kernel.2), calls=%async_computation.1 | async-start | bytes 1048576 | tf_op jit(solution)/shard_map/all_to_all | solution.py:499
  48.6 40.4 %copy-start.1 = (bf16[4,128,200]{2,1,0:T(8,128)(2,1)S(1)}, bf16[4,128,200]{2,1,0:T(8,128)(2,1)}, u32[]{:S(2)}) copy-start(bf16[4,128,200]{2,1,0:T(8,128)(2,1)} %get-tuple-element.77.refs_8_.refs_13_) | copy-start | bytes 614404
  60.0 0.8 copy-start.3
  63.5 12.7 %all-to-all-start.2 = ((f32[32,8,128]{2,1,0:T(8,128)}), f32[32,8,128]{2,1,0:T(8,128)S(1)}, u32[]{:S(2)}, u32[]{:S(2)}) async-start(f32[32,8,128]{2,1,0:T(8,128)} %get-tuple-element.66), calls=%async_computation.2 | async-start | bytes 262144 | tf_op jit(solution)/shard_map/all_to_all | solution.py:499
  67.4 5.4 %collective-permute-start.8 = (f32[200,128]{1,0:T(8,128)S(1)}, f32[200,128]{1,0:T(8,128)S(1)}, u32[]{:S(2)}, u32[]{:S(2)}) collective-permute-start(f32[200,128]{1,0:T(8,128)S(1)} %get-tuple-element.70), channel_id=1, source_target_pairs={{0,32},{32,64},{64,96},{96,128},{128,160},{160,192},{192,224},{224... | collective-permute-start | bytes 307208 | tf_op jit(solution)/shard_map/ppermute | solution.py:486
  67.8 5.0 %collective-permute-start.9 = (f32[200,128]{1,0:T(8,128)S(1)}, f32[200,128]{1,0:T(8,128)S(1)}, u32[]{:S(2)}, u32[]{:S(2)}) collective-permute-start(f32[200,128]{1,0:T(8,128)S(1)} %get-tuple-element.71), channel_id=1, source_target_pairs={{0,1},{1,2},{2,3},{3,4},{4,5},{5,6},{6,7},{7,8},{8,9},{9,10},{10,1... | collective-permute-start | bytes 307208 | tf_op jit(solution)/shard_map/ppermute | solution.py:486
  69.7 4.3 %collective-permute-start.10 = (f32[200,128]{1,0:T(8,128)S(1)}, f32[200,128]{1,0:T(8,128)S(1)}, u32[]{:S(2)}, u32[]{:S(2)}) collective-permute-start(f32[200,128]{1,0:T(8,128)S(1)} %get-tuple-element.72), channel_id=1, source_target_pairs={{0,224},{32,0},{64,32},{96,64},{128,96},{160,128},{192,160},{224,1... | collective-permute-start | bytes 307208 | tf_op jit(solution)/shard_map/ppermute | solution.py:486
  72.1 4.1 %collective-permute-start.11 = (f32[200,128]{1,0:T(8,128)S(1)}, f32[200,128]{1,0:T(8,128)S(1)}, u32[]{:S(2)}, u32[]{:S(2)}) collective-permute-start(f32[200,128]{1,0:T(8,128)S(1)} %get-tuple-element.73), channel_id=1, source_target_pairs={{0,31},{1,0},{2,1},{3,2},{4,3},{5,4},{6,5},{7,6},{8,7},{9,8},{10,9... | collective-permute-start | bytes 307208 | tf_op jit(solution)/shard_map/ppermute | solution.py:486
  93.8 12.9 %all-to-all-start.4 = ((f32[8,16,128]{2,1,0:T(8,128)}), f32[8,16,128]{2,1,0:T(8,128)S(1)}, u32[]{:S(2)}, u32[]{:S(2)}) async-start(f32[8,16,128]{2,1,0:T(8,128)} %get-tuple-element.78), calls=%async_computation.4 | async-start | bytes 131072 | tf_op jit(solution)/shard_map/all_to_all | solution.py:499
  97.2 6.6 %collective-permute-start.12 = (f32[200,128]{1,0:T(8,128)S(1)}, f32[200,128]{1,0:T(8,128)S(1)}, u32[]{:S(2)}, u32[]{:S(2)}) collective-permute-start(f32[200,128]{1,0:T(8,128)S(1)} %get-tuple-element.79), channel_id=1, source_target_pairs={{0,32},{32,64},{64,96},{96,128},{128,160},{160,192},{192,224},{224... | collective-permute-start | bytes 307208 | tf_op jit(solution)/shard_map/ppermute | solution.py:486
  98.5 5.2 %collective-permute-start.13 = (f32[200,128]{1,0:T(8,128)S(1)}, f32[200,128]{1,0:T(8,128)S(1)}, u32[]{:S(2)}, u32[]{:S(2)}) collective-permute-start(f32[200,128]{1,0:T(8,128)S(1)} %get-tuple-element.80), channel_id=1, source_target_pairs={{0,1},{1,2},{2,3},{3,4},{4,5},{5,6},{6,7},{7,8},{8,9},{9,10},{10,1... | collective-permute-start | bytes 307208 | tf_op jit(solution)/shard_map/ppermute | solution.py:486
  101.2 4.1 %collective-permute-start.14 = (f32[200,128]{1,0:T(8,128)S(1)}, f32[200,128]{1,0:T(8,128)S(1)}, u32[]{:S(2)}, u32[]{:S(2)}) collective-permute-start(f32[200,128]{1,0:T(8,128)S(1)} %get-tuple-element.81), channel_id=1, source_target_pairs={{0,224},{32,0},{64,32},{96,64},{128,96},{160,128},{192,160},{224,1... | collective-permute-start | bytes 307208 | tf_op jit(solution)/shard_map/ppermute | solution.py:486
  102.3 4.4 %collective-permute-start.15 = (f32[200,128]{1,0:T(8,128)S(1)}, f32[200,128]{1,0:T(8,128)S(1)}, u32[]{:S(2)}, u32[]{:S(2)}) collective-permute-start(f32[200,128]{1,0:T(8,128)S(1)} %get-tuple-element.82), channel_id=1, source_target_pairs={{0,31},{1,0},{2,1},{3,2},{4,3},{5,4},{6,5},{7,6},{8,7},{9,8},{10,9... | collective-permute-start | bytes 307208 | tf_op jit(solution)/shard_map/ppermute | solution.py:486
  107.9 22.1 %all-to-all-start.5 = ((f32[32,16,256]{2,1,0:T(8,128)}), f32[32,16,256]{2,1,0:T(8,128)S(1)}, u32[]{:S(2)}, u32[]{:S(2)}) async-start(f32[32,16,256]{2,1,0:T(8,128)} %spread_kernel.3), calls=%async_computation.5 | async-start | bytes 1048576 | tf_op jit(solution)/shard_map/all_to_all | solution.py:499
  123.1 0.7 copy-start.2
  131.2 12.7 %all-to-all-start.6 = ((f32[32,8,128]{2,1,0:T(8,128)}), f32[32,8,128]{2,1,0:T(8,128)S(1)}, u32[]{:S(2)}, u32[]{:S(2)}) async-start(f32[32,8,128]{2,1,0:T(8,128)} %get-tuple-element.88), calls=%async_computation.6 | async-start | bytes 262144 | tf_op jit(solution)/shard_map/all_to_all | solution.py:499
  135.1 5.4 %collective-permute-start.16 = (f32[200,128]{1,0:T(8,128)S(1)}, f32[200,128]{1,0:T(8,128)S(1)}, u32[]{:S(2)}, u32[]{:S(2)}) collective-permute-start(f32[200,128]{1,0:T(8,128)S(1)} %get-tuple-element.92), channel_id=1, source_target_pairs={{0,32},{32,64},{64,96},{96,128},{128,160},{160,192},{192,224},{224... | collective-permute-start | bytes 307208 | tf_op jit(solution)/shard_map/ppermute | solution.py:486
  135.5 5.0 %collective-permute-start.17 = (f32[200,128]{1,0:T(8,128)S(1)}, f32[200,128]{1,0:T(8,128)S(1)}, u32[]{:S(2)}, u32[]{:S(2)}) collective-permute-start(f32[200,128]{1,0:T(8,128)S(1)} %get-tuple-element.93), channel_id=1, source_target_pairs={{0,1},{1,2},{2,3},{3,4},{4,5},{5,6},{6,7},{7,8},{8,9},{9,10},{10,1... | collective-permute-start | bytes 307208 | tf_op jit(solution)/shard_map/ppermute | solution.py:486
  137.5 4.2 %collective-permute-start.18 = (f32[200,128]{1,0:T(8,128)S(1)}, f32[200,128]{1,0:T(8,128)S(1)}, u32[]{:S(2)}, u32[]{:S(2)}) collective-permute-start(f32[200,128]{1,0:T(8,128)S(1)} %get-tuple-element.94), channel_id=1, source_target_pairs={{0,224},{32,0},{64,32},{96,64},{128,96},{160,128},{192,160},{224,1... | collective-permute-start | bytes 307208 | tf_op jit(solution)/shard_map/ppermute | solution.py:486
  139.8 4.1 %collective-permute-start.19 = (f32[200,128]{1,0:T(8,128)S(1)}, f32[200,128]{1,0:T(8,128)S(1)}, u32[]{:S(2)}, u32[]{:S(2)}) collective-permute-start(f32[200,128]{1,0:T(8,128)S(1)} %get-tuple-element.95), channel_id=1, source_target_pairs={{0,31},{1,0},{2,1},{3,2},{4,3},{5,4},{6,5},{7,6},{8,7},{9,8},{10,9... | collective-permute-start | bytes 307208 | tf_op jit(solution)/shard_map/ppermute | solution.py:486

commit v3 on v2

--- a/solution.py
+++ b/solution.py
@@ -261,9 +261,9 @@
     low_y[...] = faces_of(values_ref, 2, face)
 
 
-def jump_faces(values_ref, received, table_ref, face):
+def jump_faces(values_ref, received, table_ref, face, multiply=dot_columns):
     below_x, below_y, above_x, above_y = received
-    up = [wide_sum(dot_columns(table_ref[a], wide_two(ref[...]))) for a, ref in ((0, above_x), (1, above_y))]
+    up = [wide_sum(multiply(table_ref[a], wide_two(ref[...]))) for a, ref in ((0, above_x), (1, above_y))]
     own = [faces_of(values_ref, n, face) for n in range(6)]
     return [
         own[0] - below_x[...], own[1] - up[0], own[2] - below_y[...], own[3] - up[1], 0.0 * own[4], 0.0 * own[5]
@@ -293,7 +293,7 @@
 
 def corner_faces(corners, reach_ref):
     pieces = wide_two(corners)
-    return [wide_sum(dot_columns(reach_ref[n], pieces)) for n in range(4)]
+    return [wide_sum(dot(reach_ref[n], pieces)) for n in range(4)]
 
 
 def coupling_of(phi_ref, n, face):
@@ -386,6 +386,20 @@
     write_rows(sums_ref, rows)
 
 
+def first_stretch_kernel(
+    solved_ref, below_x, below_y, above_x, above_y, table_ref, matrix_ref, reach_ref, *outs
+):
+    turned_ref, spread_ref = outs[-2:]
+    face = below_x.shape[0]
+    row = lax.broadcasted_iota(jnp.int32, (face, face), 0)
+    same = jnp.where(row == lax.broadcasted_iota(jnp.int32, (face, face), 1), 1.0, 0.0).astype(BF16)
+    stretch_kernel(solved_ref, below_x, below_y, above_x, above_y, table_ref, matrix_ref, *outs[:-2])
+    for a in range(2):
+        turned_ref[a] = dot_columns(table_ref[a], same).astype(BF16)
+    for n in range(4):
+        spread_ref[n] = dot_rows(same, reach_ref[n]).astype(BF16)
+
+
 def returned(got_ref):
     corners = jnp.concatenate([got_ref[x, 0:CHUNK, :] for x in range(GX)], axis=0).T
     sums = got_ref[0, CHUNK:, :]
@@ -396,7 +410,7 @@
 
 def turn_kernel(
     got_ref, half_ref, stretched_ref, below_x, below_y, above_x, above_y, table_ref, reach_ref, matrix_ref,
-    next_ref, solved_ref, image_ref, corners_ref, scalars_ref, up_x, up_y, low_x, low_y, out_ref,
+    turned_ref, across_ref, next_ref, solved_ref, image_ref, corners_ref, scalars_ref, up_x, up_y, low_x, low_y, out_ref,
 ):
     face = below_x.shape[0]
     corners, sums = returned(got_ref)
@@ -405,8 +419,8 @@
     curvature = sums[0:1] + corners[E_LANE + 1 : E_LANE + 2]
     alpha = energy / curvature
     write_rows(scalars_ref, [energy, curvature, alpha])
-    jumped = jump_faces(stretched_ref, (below_x, below_y, above_x, above_y), table_ref, face)
-    coarse = corner_faces(corners, reach_ref)
+    jumped = jump_faces(stretched_ref, (below_x, below_y, above_x, above_y), turned_ref, face, dot)
+    coarse = corner_faces(corners, across_ref)
     for n in range(6):
         at = slice(n * face, (n + 1) * face)
         image = jumped[n] + coarse[n] if n < 4 else jumped[n]
@@ -422,7 +436,7 @@
 
 def last_kernel(
     got_ref, half_ref, upper_ref, fresh_ref, stretched_ref, below_x, below_y, above_x, above_y, image_ref,
-    corners_ref, scalars_ref, table_ref, reach_ref, matrix_ref, multipliers_ref, out_ref, held_ref,
+    corners_ref, scalars_ref, turned_ref, across_ref, matrix_ref, multipliers_ref, out_ref, held_ref,
 ):
     face = below_x.shape[0]
     corners, sums = returned(got_ref)
@@ -432,8 +446,8 @@
     mixed = sums[1:2] + 2.0 * corners[E_LANE + 2 : E_LANE + 3]
     curvature = sums[0:1] + corners[E_LANE + 1 : E_LANE + 2] + ratio * mixed + ratio * ratio * curvature
     step = energy / curvature
-    jumped = jump_faces(stretched_ref, (below_x, below_y, above_x, above_y), table_ref, face)
-    coarse = corner_faces(corners, reach_ref)
+    jumped = jump_faces(stretched_ref, (below_x, below_y, above_x, above_y), turned_ref, face, dot)
+    coarse = corner_faces(corners, across_ref)
     for n in range(6):
         at = slice(n * face, (n + 1) * face)
         image = jumped[n] + coarse[n] if n < 4 else jumped[n]
@@ -527,9 +541,11 @@
     received = passed_both_ways(*sent)
     first_rows = exchanged(message, "gx")
     (sent,) = spread(first_rows, lanes, after=received)
-    field, stretched, direction, *faces_sent, sums = call(stretch_kernel, [whole, whole, upper, *faces, ((8, 128), F32)], flops=big)(
-        solved, *received, table, stiffness
-    )
+    field, stretched, direction, *faces_sent, sums, turned, across = call(
+        first_stretch_kernel,
+        [whole, whole, upper, *faces, ((8, 128), F32), ((2, face, face), BF16), ((4, face, 128), BF16)],
+        flops=big,
+    )(solved, *received, table, stiffness, reach)
     received = passed_both_ways(*faces_sent)
     arrived = exchanged(sent, GY)
     sent, loads, energy, high, low, place = first_solve(me, arrived, first_rows, sums)
@@ -539,7 +555,7 @@
         turn_kernel,
         [whole, whole, whole, ((128, 128), F32), ((8, 128), F32), *faces, ((GX, CHUNK, 128), F32)],
         flops=big,
-    )(back, half, stretched, *received, table, reach, schur_block)
+    )(back, half, stretched, *received, table, reach, schur_block, turned, across)
 
     received = passed_both_ways(*sent)
     (sent,) = spread(exchanged(message, "gx"), lanes, after=received)
@@ -556,7 +572,7 @@
         scratch=[pltpu.VMEM((interface, 128), F32)],
         flops=big,
     )(
-        back, half, direction, fresh, fresh_stretched, *received, image, corners, scalars, table, reach, schur_block
+        back, half, direction, fresh, fresh_stretched, *received, image, corners, scalars, turned, across, schur_block
     )
     energy = jnp.sum(exchanged(jnp.broadcast_to(energy, (GX * GYN, 1, 128)), GX_GY), axis=(0, 1))
     return (multipliers[None, None, None], energy / scalars[0])

time: 186 us -> 187 us (level)
  no operation moved by 1% of the time
where the time goes in v3:
time: 187 us; the launch traced here: 186 us
  starting transfers between devices  67.4 us (36%)
  blocking collectives  47.9 us (26%)
  Pallas kernels  33.1 us (18%)
  waiting for transfers between devices  33.1 us (18%)
  local copies, waits for them, and re-layouts  2.99 us (2%)
    all_to_all x3, blocking collectives, exchanged(): return lax.all_to_all(array, axis, split_axis=0, concat_axis=0, tiled=True)  47.9 us
    all_to_all x6, starting transfers between devices, exchanged(): return lax.all_to_all(array, axis, split_axis=0, concat_axis=0, tiled=True)  37.6 us
    pallas_call x12, Pallas kernels, run(): pl.pallas_call(body, name=kernel.__name__, out_shape=[jax.ShapeDtypeStruc...  33.1 us
    ppermute x20, starting transfers between devices, passed_along(): lax.ppermute(array, axis, [(i, (i + by) % peers) for i in range(peers)])  29.8 us
    ppermute x20, waiting for transfers between devices, passed_along(): lax.ppermute(array, axis, [(i, (i + by) % peers) for i in range(peers)])  20.8 us
    all_to_all x6, waiting for transfers between devices, exchanged(): return lax.all_to_all(array, axis, split_axis=0, concat_axis=0, tiled=True)  12.3 us
  transfers between devices with their start and end apart: 26, of which 13 were waited for; matrix products, arithmetic and copies ran while one was open for 0% of the time, Pallas kernels for 5%

profile of v3, /device:TPU:1, one launch (start us, length us, event | category | flops | bytes accessed | tf_op | source)
XLA Modules:
  0.0 185.9 jit_solution(92526354919516219)
XLA Ops:
  0.6 0.0 copy-start.10
  0.6 2.0 %start_kernel.1 = (f32[248,128]{1,0:T(8,128)}, f32[248,128]{1,0:T(8,128)}, f32[24,200]{1,0:T(8,128)}, f32[24,200]{1,0:T(8,128)}, bf16[2,200,200]{2,1,0:T(8,128)(2,1)}) custom-call(f32[3,200,128]{2,1,0:T(8,128)} %bitcast.18, s32[3,1,200]{2,1,0:T(1,128)} %bitcast.23, bf16[24,1200]{1,0:T(8,128)(2,1)} %bitcast.21), custom_call_target="tpu_custom_call" | custom-call | flops 2000000 | bytes 1000000 | tf_op jit(solution)/shard_map/start_kernel/pallas_call | solution.py:472
  2.6 2.5 %collective-permute-start = (f32[248,128]{1,0:T(8,128)}, f32[248,128]{1,0:T(8,128)S(1)}, u32[]{:S(2)}, u32[]{:S(2)}) collective-permute-start(f32[248,128]{1,0:T(8,128)} %get-tuple-element.56), channel_id=1, source_target_pairs={{0,32},{32,64},{64,96},{96,128},{128,160},{160,192},{192,224},{224... | collective-permute-start | bytes 380936 | tf_op jit(solution)/shard_map/ppermute | solution.py:500
  5.1 2.1 %collective-permute-start.1 = (f32[248,128]{1,0:T(8,128)}, f32[248,128]{1,0:T(8,128)S(1)}, u32[]{:S(2)}, u32[]{:S(2)}) collective-permute-start(f32[248,128]{1,0:T(8,128)} %get-tuple-element.57), channel_id=1, source_target_pairs={{0,1},{1,2},{2,3},{3,4},{4,5},{5,6},{6,7},{7,8},{8,9},{9,10},{10,1... | collective-permute-start | bytes 380936 | tf_op jit(solution)/shard_map/ppermute | solution.py:500
  7.1 3.7 %collective-permute-start.2 = (f32[24,200]{1,0:T(8,128)}, f32[24,200]{1,0:T(8,128)S(1)}, u32[]{:S(2)}, u32[]{:S(2)}) collective-permute-start(f32[24,200]{1,0:T(8,128)} %get-tuple-element.58), channel_id=1, source_target_pairs={{0,224},{32,0},{64,32},{96,64},{128,96},{160,128},{192,160},{224,1... | collective-permute-start | bytes 57608 | tf_op jit(solution)/shard_map/ppermute | solution.py:500
  10.8 0.0 collective-permute-start.3
  10.8 1.2 collective-permute-done.2.refs_4_
  11.9 2.3 %collective-permute-done.3.refs_5_ = f32[24,200]{1,0:T(8,128)S(1)} collective-permute-done((f32[24,200]{1,0:T(8,128)}, f32[24,200]{1,0:T(8,128)S(1)}, u32[]{:S(2)}, u32[]{:S(2)}) %collective-permute-start.3) | collective-permute-done | bytes 19232 | tf_op jit(solution)/shard_map/ppermute | solution.py:500
  14.3 0.6 copy-done.9
  14.8 0.0 copy-done.6
  14.9 0.1 copy-done.7
  14.9 4.8 %first_kernel.1 = (f32[1200,128]{1,0:T(8,128)}, f32[1200,128]{1,0:T(8,128)}, bf16[4,128,200]{2,1,0:T(8,128)(2,1)}, f32[200,128]{1,0:T(8,128)}, f32[200,128]{1,0:...) custom-call(s32[8]{0:T(128)} %bitcast.24, f32[3,200,128]{2,1,0:T(8,128)} %bitcast.19, ...), custom_call_target="tpu_custom_call" | custom-call | flops 368640000 | bytes 1000000 | tf_op jit(solution)/shard_map/first_kernel/pallas_call | solution.py:472
  19.8 5.9 %all-to-all-start = ((f32[8,88,128]{2,1,0:T(8,128)}), f32[8,88,128]{2,1,0:T(8,128)S(1)}, u32[]{:S(2)}, u32[]{:S(2)}) async-start(f32[8,88,128]{2,1,0:T(8,128)} %get-tuple-element.61), calls=%async_computation | async-start | bytes 720896 | tf_op jit(solution)/shard_map/all_to_all | solution.py:513
  25.6 1.5 collective-permute-start.4
  27.1 0.7 collective-permute-start.5
  27.8 1.0 collective-permute-start.6
  28.7 2.4 %collective-permute-start.7 = (f32[200,128]{1,0:T(8,128)}, f32[200,128]{1,0:T(8,128)S(1)}, u32[]{:S(2)}, u32[]{:S(2)}) collective-permute-start(f32[200,128]{1,0:T(8,128)} %get-tuple-element.65), channel_id=1, source_target_pairs={{0,31},{1,0},{2,1},{3,2},{4,3},{5,4},{6,5},{7,6},{8,7},{9,8},{10,9... | collective-permute-start | bytes 307208 | tf_op jit(solution)/shard_map/ppermute | solution.py:500
  31.2 0.1 fusion.refs_1_.refs_4_
  31.3 6.2 %collective-permute-done.4.refs_2_.refs_1_ = f32[200,128]{1,0:T(8,128)S(1)} collective-permute-done((f32[200,128]{1,0:T(8,128)}, f32[200,128]{1,0:T(8,128)S(1)}, u32[]{:S(2)}, u32[]{:S(2)}) %collective-permute-start.4) | collective-permute-done | bytes 102432 | tf_op jit(solution)/shard_map/ppermute | solution.py:500
  37.5 1.1 spread_kernel.2
  38.6 9.9 %all-to-all-start.1 = ((f32[32,16,256]{2,1,0:T(8,128)}), f32[32,16,256]{2,1,0:T(8,128)S(1)}, u32[]{:S(2)}, u32[]{:S(2)}) async-start(f32[32,16,256]{2,1,0:T(8,128)} %spread_kernel.2), calls=%async_computation.1 | async-start | bytes 1048576 | tf_op jit(solution)/shard_map/all_to_all | solution.py:513
  48.6 4.5 %first_stretch_kernel.1 = (f32[1200,128]{1,0:T(8,128)}, f32[1200,128]{1,0:T(8,128)}, f32[3,200,128]{2,1,0:T(8,128)}, f32[200,128]{1,0:T(8,128)S(1)}, f32[200,128...) custom-call(f32[1200,128]{1,0:T(8,128)} %get-tuple-element.66.refs_0, ...), custom_call_target="tpu_custom_call" | custom-call | flops 368640000 | bytes 1000000 | tf_op jit(solution)/shard_map/first_stretch_kernel/pallas_call | solution.py:472
  53.0 0.7 copy-done.1
  53.7 6.2 %all-to-all-done.1.refs_1_ = f32[32,16,256]{2,1,0:T(8,128)S(1)} async-done(((f32[32,16,256]{2,1,0:T(8,128)}), f32[32,16,256]{2,1,0:T(8,128)S(1)}, u32[]{:S(2)}, u32[]{:S(2)}) %all-to-all-start.1) | async-done | bytes 524320 | tf_op jit(solution)/shard_map/all_to_all | solution.py:513
  60.0 0.8 copy-done.5
  60.8 2.8 %first_solve_kernel.1 = (f32[32,8,128]{2,1,0:T(8,128)}, f32[16,1536]{1,0:T(8,128)S(1)}, f32[16,128]{1,0:T(8,128)S(1)}, bf16[144,512]{1,0:T(8,128)(2,1)S(1)}, bf1...) custom-call(s32[1]{0:T(128)} %bitcast.refs_0_, f32[32,16,256]{2,1,0:T(8,128)} %copy-done.5, ...), custom_call_target="tpu_custom_call" | custom-call | flops 2000000 | bytes 1000000 | tf_op jit(solution)/shard_map/first_solve_kernel/pallas_call | solution.py:472
  63.5 3.9 %all-to-all-start.2 = ((f32[32,8,128]{2,1,0:T(8,128)}), f32[32,8,128]{2,1,0:T(8,128)S(1)}, u32[]{:S(2)}, u32[]{:S(2)}) async-start(f32[32,8,128]{2,1,0:T(8,128)} %get-tuple-element.69), calls=%async_computation.2 | async-start | bytes 262144 | tf_op jit(solution)/shard_map/all_to_all | solution.py:513
  67.5 0.6 collective-permute-start.8
  68.0 1.9 %collective-permute-start.9 = (f32[200,128]{1,0:T(8,128)S(1)}, f32[200,128]{1,0:T(8,128)S(1)}, u32[]{:S(2)}, u32[]{:S(2)}) collective-permute-start(f32[200,128]{1,0:T(8,128)S(1)} %get-tuple-element.74), channel_id=1, source_target_pairs={{0,1},{1,2},{2,3},{3,4},{4,5},{5,6},{6,7},{7,8},{8,9},{9,10},{10,1... | collective-permute-start | bytes 307208 | tf_op jit(solution)/shard_map/ppermute | solution.py:500
  69.9 2.4 %collective-permute-start.10 = (f32[200,128]{1,0:T(8,128)S(1)}, f32[200,128]{1,0:T(8,128)S(1)}, u32[]{:S(2)}, u32[]{:S(2)}) collective-permute-start(f32[200,128]{1,0:T(8,128)S(1)} %get-tuple-element.75), channel_id=1, source_target_pairs={{0,224},{32,0},{64,32},{96,64},{128,96},{160,128},{192,160},{224,1... | collective-permute-start | bytes 307208 | tf_op jit(solution)/shard_map/ppermute | solution.py:500
  72.3 0.7 collective-permute-done.8.refs_5_.refs_3_
  73.0 1.2 collective-permute-done.10.refs_7_.refs_5_
  74.2 2.2 %collective-permute-done.11.refs_8_.refs_6_ = f32[200,128]{1,0:T(8,128)S(1)} collective-permute-done((f32[200,128]{1,0:T(8,128)S(1)}, f32[200,128]{1,0:T(8,128)S(1)}, u32[]{:S(2)}, u32[]{:S(2)}) %collective-permute-start.11) | collective-permute-done | bytes 102432 | tf_op jit(solution)/shard_map/ppermute | solution.py:500
  76.4 0.8 pick_kernel.2
  77.2 11.9 %all_to_all.45.refs_0_ = f32[8,24,128]{2,1,0:T(8,128)S(1)} all-to-all(f32[8,24,128]{2,1,0:T(8,128)S(1)} %get-tuple-element.77), channel_id=1, replica_groups=mesh['gx'=8,'gy_0'=4,'gy_1'=4,'gy_2'=2] {'gx'}, dimensions={0} | all-to-all | bytes 196608 | tf_op jit(solution)/shard_map/all_to_all | solution.py:513
  89.1 5.0 %turn_kernel.1 = (f32[1200,128]{1,0:T(8,128)}, f32[1200,128]{1,0:T(8,128)}, f32[1200,128]{1,0:T(8,128)}, f32[128,128]{1,0:T(8,128)S(1)}, f32[8,128]{1,0:T(8,128)...) custom-call(f32[8,24,128]{2,1,0:T(8,128)S(1)} %all_to_all.45.refs_0_, ...), custom_call_target="tpu_custom_call" | custom-call | flops 368640000 | bytes 1000000 | tf_op jit(solution)/shard_map/turn_kernel/pallas_call | solution.py:472
  94.1 3.3 %all-to-all-start.4 = ((f32[8,16,128]{2,1,0:T(8,128)}), f32[8,16,128]{2,1,0:T(8,128)S(1)}, u32[]{:S(2)}, u32[]{:S(2)}) async-start(f32[8,16,128]{2,1,0:T(8,128)} %get-tuple-element.82), calls=%async_computation.4 | async-start | bytes 131072 | tf_op jit(solution)/shard_map/all_to_all | solution.py:513
  97.5 1.4 collective-permute-start.12
  98.8 2.7 %collective-permute-start.13 = (f32[200,128]{1,0:T(8,128)S(1)}, f32[200,128]{1,0:T(8,128)S(1)}, u32[]{:S(2)}, u32[]{:S(2)}) collective-permute-start(f32[200,128]{1,0:T(8,128)S(1)} %get-tuple-element.84), channel_id=1, source_target_pairs={{0,1},{1,2},{2,3},{3,4},{4,5},{5,6},{6,7},{7,8},{8,9},{9,10},{10,1... | collective-permute-start | bytes 307208 | tf_op jit(solution)/shard_map/ppermute | solution.py:500
  101.5 1.1 collective-permute-start.14
  102.6 1.4 collective-permute-start.15
  104.1 1.6 collective-permute-done.14.refs_4_.refs_3_
  105.6 1.4 collective-permute-done.15.refs_5_.refs_4_
  107.0 1.1 spread_kernel.3
  108.2 10.7 %all-to-all-start.5 = ((f32[32,16,256]{2,1,0:T(8,128)}), f32[32,16,256]{2,1,0:T(8,128)S(1)}, u32[]{:S(2)}, u32[]{:S(2)}) async-start(f32[32,16,256]{2,1,0:T(8,128)} %spread_kernel.3), calls=%async_computation.5 | async-start | bytes 1048576 | tf_op jit(solution)/shard_map/all_to_all | solution.py:513
  118.8 0.0 copy-start.3
  118.8 4.6 %stretch_kernel.1 = (f32[1200,128]{1,0:T(8,128)}, f32[1200,128]{1,0:T(8,128)}, f32[3,200,128]{2,1,0:T(8,128)S(1)}, f32[200,128]{1,0:T(8,128)S(1)}, f32[200,128]{...) custom-call(f32[1200,128]{1,0:T(8,128)} %get-tuple-element.89.refs_0_, ...), custom_call_target="tpu_custom_call" | custom-call | flops 368640000 | bytes 1000000 | tf_op jit(solution)/shard_map/stretch_kernel/pallas_call | solution.py:472
  123.5 0.7 copy-done.4
  124.2 6.1 %all-to-all-done.5.refs_1_ = f32[32,16,256]{2,1,0:T(8,128)S(1)} async-done(((f32[32,16,256]{2,1,0:T(8,128)}), f32[32,16,256]{2,1,0:T(8,128)S(1)}, u32[]{:S(2)}, u32[]{:S(2)}) %all-to-all-start.5) | async-done | bytes 524320 | tf_op jit(solution)/shard_map/all_to_all | solution.py:513
  130.2 1.2 next_solve_kernel.1
  131.5 3.9 %all-to-all-start.6 = ((f32[32,8,128]{2,1,0:T(8,128)}), f32[32,8,128]{2,1,0:T(8,128)S(1)}, u32[]{:S(2)}, u32[]{:S(2)}) async-start(f32[32,8,128]{2,1,0:T(8,128)} %get-tuple-element.92), calls=%async_computation.6 | async-start | bytes 262144 | tf_op jit(solution)/shard_map/all_to_all | solution.py:513
  135.4 0.4 collective-permute-start.16
  135.8 1.9 %collective-permute-start.17 = (f32[200,128]{1,0:T(8,128)S(1)}, f32[200,128]{1,0:T(8,128)S(1)}, u32[]{:S(2)}, u32[]{:S(2)}) collective-permute-start(f32[200,128]{1,0:T(8,128)S(1)} %get-tuple-element.97), channel_id=1, source_target_pairs={{0,1},{1,2},{2,3},{3,4},{4,5},{5,6},{6,7},{7,8},{8,9},{9,10},{10,1... | collective-permute-start | bytes 307208 | tf_op jit(solution)/shard_map/ppermute | solution.py:500
  137.7 2.3 %collective-permute-start.18 = (f32[200,128]{1,0:T(8,128)S(1)}, f32[200,128]{1,0:T(8,128)S(1)}, u32[]{:S(2)}, u32[]{:S(2)}) collective-permute-start(f32[200,128]{1,0:T(8,128)S(1)} %get-tuple-element.98), channel_id=1, source_target_pairs={{0,224},{32,0},{64,32},{96,64},{128,96},{160,128},{192,160},{224,1... | collective-permute-start | bytes 307208 | tf_op jit(solution)/shard_map/ppermute | solution.py:500
  140.1 0.0 collective-permute-start.19
  140.1 0.7 collective-permute-done.16.refs_6_.refs_5_
  140.8 1.2 collective-permute-done.18.refs_8_.refs_7_
  142.0 2.2 %collective-permute-done.19.refs_9_.refs_8_ = f32[200,128]{1,0:T(8,128)S(1)} collective-permute-done((f32[200,128]{1,0:T(8,128)S(1)}, f32[200,128]{1,0:T(8,128)S(1)}, u32[]{:S(2)}, u32[]{:S(2)}) %collective-permute-start.19) | collective-permute-done | bytes 102432 | tf_op jit(solution)/shard_map/ppermute | solution.py:500
  144.2 1.2 pick_kernel.3
  145.4 14.2 %all_to_all.46.refs_0_ = f32[8,24,128]{2,1,0:T(8,128)S(1)} all-to-all(f32[8,24,128]{2,1,0:T(8,128)S(1)} %get-tuple-element.100), channel_id=1, replica_groups=mesh['gx'=8,'gy_0'=4,'gy_1'=4,'gy_2'=2] {'gx'}, dimensions={0} | all-to-all | bytes 196608 | tf_op jit(solution)/shard_map/all_to_all | solution.py:513
  159.6 3.9 %last_kernel.1 = (f32[3,200,128]{2,1,0:T(8,128)}, f32[1,128]{1,0:T(1,128)S(1)}) custom-call(f32[8,24,128]{2,1,0:T(8,128)S(1)} %all_to_all.46.refs_0_, f32[1200,128]{1,0:T(8,128)} %get-tuple-element.101.refs_1_, f32[3,200,128]{2,1,0:T(8,128)S(1)} %copy-done.3, f32[3,200,128]{2,1,0:T(8,128)} %copy-done.4, f32[1200,128]{1,0:T(8,128)} %get-tuple-element.104.refs_4_, ...), custom_call_target="tpu_custom_call" | custom-call | flops 368640000 | bytes 1000000 | tf_op jit(solution)/shard_map/last_kernel/pallas_call | solution.py:472
  163.5 0.1 broadcast_in_dim.9
  163.6 21.7 %all_to_all.47 = f32[256,1,128]{2,1,0:T(1,128)S(1)} all-to-all(f32[256,1,128]{2,1,0:T(1,128)S(1)} %broadcast_in_dim.9), channel_id=1, replica_groups=mesh['gx'=8,'gy_0'=4,'gy_1'=4,'gy_2'=2] {'gx','gy_0','gy_1','gy_2'}, dimensions={0} | all-to-all | bytes 262144 | tf_op jit(solution)/shard_map/all_to_all | solution.py:513
  185.4 0.5 bitcast_divide_fusion
  (29 shorter events, 0.1 us)
Async XLA Ops:
  0.6 30.6 %copy-start.10 = (s32[128]{0:T(128)S(1)}, s32[128]{0:T(128)}, u32[]{:S(2)}) copy-start(s32[128]{0:T(128)} %constant.19.clone) | copy-start | bytes 1540
  2.6 11.6 %collective-permute-start = (f32[248,128]{1,0:T(8,128)}, f32[248,128]{1,0:T(8,128)S(1)}, u32[]{:S(2)}, u32[]{:S(2)}) collective-permute-start(f32[248,128]{1,0:T(8,128)} %get-tuple-element.56), channel_id=1, source_target_pairs={{0,32},{32,64},{64,96},{96,128},{128,160},{160,192},{192,224},{224... | collective-permute-start | bytes 380936 | tf_op jit(solution)/shard_map/ppermute | solution.py:500
  5.1 9.2 %collective-permute-start.1 = (f32[248,128]{1,0:T(8,128)}, f32[248,128]{1,0:T(8,128)S(1)}, u32[]{:S(2)}, u32[]{:S(2)}) collective-permute-start(f32[248,128]{1,0:T(8,128)} %get-tuple-element.57), channel_id=1, source_target_pairs={{0,1},{1,2},{2,3},{3,4},{4,5},{5,6},{6,7},{7,8},{8,9},{9,10},{10,1... | collective-permute-start | bytes 380936 | tf_op jit(solution)/shard_map/ppermute | solution.py:500
  7.1 4.8 %collective-permute-start.2 = (f32[24,200]{1,0:T(8,128)}, f32[24,200]{1,0:T(8,128)S(1)}, u32[]{:S(2)}, u32[]{:S(2)}) collective-permute-start(f32[24,200]{1,0:T(8,128)} %get-tuple-element.58), channel_id=1, source_target_pairs={{0,224},{32,0},{64,32},{96,64},{128,96},{160,128},{192,160},{224,1... | collective-permute-start | bytes 57608 | tf_op jit(solution)/shard_map/ppermute | solution.py:500
  10.8 3.5 %collective-permute-start.3 = (f32[24,200]{1,0:T(8,128)}, f32[24,200]{1,0:T(8,128)S(1)}, u32[]{:S(2)}, u32[]{:S(2)}) collective-permute-start(f32[24,200]{1,0:T(8,128)} %get-tuple-element.59), channel_id=1, source_target_pairs={{0,31},{1,0},{2,1},{3,2},{4,3},{5,4},{6,5},{7,6},{8,7},{9,8},{10,9... | collective-permute-start | bytes 57608 | tf_op jit(solution)/shard_map/ppermute | solution.py:500
  11.9 2.3 %copy-start.8 = (f32[24,200]{1,0:T(8,128)}, f32[24,200]{1,0:T(8,128)S(1)}, u32[]{:S(2)}) copy-start(f32[24,200]{1,0:T(8,128)S(1)} %collective-permute-done.2.refs_4_) | copy-start | bytes 57604
  14.2 0.6 copy-start.9
  14.2 0.6 copy-start.6
  14.2 0.7 copy-start.7
  14.9 33.6 %copy-start = (bf16[2,200,200]{2,1,0:T(8,128)(2,1)S(1)}, bf16[2,200,200]{2,1,0:T(8,128)(2,1)}, u32[]{:S(2)}) copy-start(bf16[2,200,200]{2,1,0:T(8,128)(2,1)} %get-tuple-element.60.refs_7_.refs_5_) | copy-start | bytes 480004
  19.8 17.7 %all-to-all-start = ((f32[8,88,128]{2,1,0:T(8,128)}), f32[8,88,128]{2,1,0:T(8,128)S(1)}, u32[]{:S(2)}, u32[]{:S(2)}) async-start(f32[8,88,128]{2,1,0:T(8,128)} %get-tuple-element.61), calls=%async_computation | async-start | bytes 720896 | tf_op jit(solution)/shard_map/all_to_all | solution.py:513
  25.6 11.8 %collective-permute-start.4 = (f32[200,128]{1,0:T(8,128)}, f32[200,128]{1,0:T(8,128)S(1)}, u32[]{:S(2)}, u32[]{:S(2)}) collective-permute-start(f32[200,128]{1,0:T(8,128)} %get-tuple-element.62), channel_id=1, source_target_pairs={{0,32},{32,64},{64,96},{96,128},{128,160},{160,192},{192,224},{224... | collective-permute-start | bytes 307208 | tf_op jit(solution)/shard_map/ppermute | solution.py:500
  27.1 10.4 %collective-permute-start.5 = (f32[200,128]{1,0:T(8,128)}, f32[200,128]{1,0:T(8,128)S(1)}, u32[]{:S(2)}, u32[]{:S(2)}) collective-permute-start(f32[200,128]{1,0:T(8,128)} %get-tuple-element.63), channel_id=1, source_target_pairs={{0,1},{1,2},{2,3},{3,4},{4,5},{5,6},{6,7},{7,8},{8,9},{9,10},{10,1... | collective-permute-start | bytes 307208 | tf_op jit(solution)/shard_map/ppermute | solution.py:500
  27.8 9.7 %collective-permute-start.6 = (f32[200,128]{1,0:T(8,128)}, f32[200,128]{1,0:T(8,128)S(1)}, u32[]{:S(2)}, u32[]{:S(2)}) collective-permute-start(f32[200,128]{1,0:T(8,128)} %get-tuple-element.64), channel_id=1, source_target_pairs={{0,224},{32,0},{64,32},{96,64},{128,96},{160,128},{192,160},{224,1... | collective-permute-start | bytes 307208 | tf_op jit(solution)/shard_map/ppermute | solution.py:500
  28.7 8.7 %collective-permute-start.7 = (f32[200,128]{1,0:T(8,128)}, f32[200,128]{1,0:T(8,128)S(1)}, u32[]{:S(2)}, u32[]{:S(2)}) collective-permute-start(f32[200,128]{1,0:T(8,128)} %get-tuple-element.65), channel_id=1, source_target_pairs={{0,31},{1,0},{2,1},{3,2},{4,3},{5,4},{6,5},{7,6},{8,7},{9,8},{10,9... | collective-permute-start | bytes 307208 | tf_op jit(solution)/shard_map/ppermute | solution.py:500
  38.6 21.4 %all-to-all-start.1 = ((f32[32,16,256]{2,1,0:T(8,128)}), f32[32,16,256]{2,1,0:T(8,128)S(1)}, u32[]{:S(2)}, u32[]{:S(2)}) async-start(f32[32,16,256]{2,1,0:T(8,128)} %spread_kernel.2), calls=%async_computation.1 | async-start | bytes 1048576 | tf_op jit(solution)/shard_map/all_to_all | solution.py:513
  53.0 0.7 copy-start.1
  60.0 0.8 copy-start.5
  63.5 12.9 %all-to-all-start.2 = ((f32[32,8,128]{2,1,0:T(8,128)}), f32[32,8,128]{2,1,0:T(8,128)S(1)}, u32[]{:S(2)}, u32[]{:S(2)}) async-start(f32[32,8,128]{2,1,0:T(8,128)} %get-tuple-element.69), calls=%async_computation.2 | async-start | bytes 262144 | tf_op jit(solution)/shard_map/all_to_all | solution.py:513
  67.5 5.6 %collective-permute-start.8 = (f32[200,128]{1,0:T(8,128)S(1)}, f32[200,128]{1,0:T(8,128)S(1)}, u32[]{:S(2)}, u32[]{:S(2)}) collective-permute-start(f32[200,128]{1,0:T(8,128)S(1)} %get-tuple-element.73), channel_id=1, source_target_pairs={{0,32},{32,64},{64,96},{96,128},{128,160},{160,192},{192,224},{224... | collective-permute-start | bytes 307208 | tf_op jit(solution)/shard_map/ppermute | solution.py:500
  68.0 5.0 %collective-permute-start.9 = (f32[200,128]{1,0:T(8,128)S(1)}, f32[200,128]{1,0:T(8,128)S(1)}, u32[]{:S(2)}, u32[]{:S(2)}) collective-permute-start(f32[200,128]{1,0:T(8,128)S(1)} %get-tuple-element.74), channel_id=1, source_target_pairs={{0,1},{1,2},{2,3},{3,4},{4,5},{5,6},{6,7},{7,8},{8,9},{9,10},{10,1... | collective-permute-start | bytes 307208 | tf_op jit(solution)/shard_map/ppermute | solution.py:500
  69.9 4.3 %collective-permute-start.10 = (f32[200,128]{1,0:T(8,128)S(1)}, f32[200,128]{1,0:T(8,128)S(1)}, u32[]{:S(2)}, u32[]{:S(2)}) collective-permute-start(f32[200,128]{1,0:T(8,128)S(1)} %get-tuple-element.75), channel_id=1, source_target_pairs={{0,224},{32,0},{64,32},{96,64},{128,96},{160,128},{192,160},{224,1... | collective-permute-start | bytes 307208 | tf_op jit(solution)/shard_map/ppermute | solution.py:500
  72.3 4.1 %collective-permute-start.11 = (f32[200,128]{1,0:T(8,128)S(1)}, f32[200,128]{1,0:T(8,128)S(1)}, u32[]{:S(2)}, u32[]{:S(2)}) collective-permute-start(f32[200,128]{1,0:T(8,128)S(1)} %get-tuple-element.76), channel_id=1, source_target_pairs={{0,31},{1,0},{2,1},{3,2},{4,3},{5,4},{6,5},{7,6},{8,7},{9,8},{10,9... | collective-permute-start | bytes 307208 | tf_op jit(solution)/shard_map/ppermute | solution.py:500
  94.1 12.9 %all-to-all-start.4 = ((f32[8,16,128]{2,1,0:T(8,128)}), f32[8,16,128]{2,1,0:T(8,128)S(1)}, u32[]{:S(2)}, u32[]{:S(2)}) async-start(f32[8,16,128]{2,1,0:T(8,128)} %get-tuple-element.82), calls=%async_computation.4 | async-start | bytes 131072 | tf_op jit(solution)/shard_map/all_to_all | solution.py:513
  97.5 6.6 %collective-permute-start.12 = (f32[200,128]{1,0:T(8,128)S(1)}, f32[200,128]{1,0:T(8,128)S(1)}, u32[]{:S(2)}, u32[]{:S(2)}) collective-permute-start(f32[200,128]{1,0:T(8,128)S(1)} %get-tuple-element.83), channel_id=1, source_target_pairs={{0,32},{32,64},{64,96},{96,128},{128,160},{160,192},{192,224},{224... | collective-permute-start | bytes 307208 | tf_op jit(solution)/shard_map/ppermute | solution.py:500
  98.8 5.2 %collective-permute-start.13 = (f32[200,128]{1,0:T(8,128)S(1)}, f32[200,128]{1,0:T(8,128)S(1)}, u32[]{:S(2)}, u32[]{:S(2)}) collective-permute-start(f32[200,128]{1,0:T(8,128)S(1)} %get-tuple-element.84), channel_id=1, source_target_pairs={{0,1},{1,2},{2,3},{3,4},{4,5},{5,6},{6,7},{7,8},{8,9},{9,10},{10,1... | collective-permute-start | bytes 307208 | tf_op jit(solution)/shard_map/ppermute | solution.py:500
  101.5 4.1 %collective-permute-start.14 = (f32[200,128]{1,0:T(8,128)S(1)}, f32[200,128]{1,0:T(8,128)S(1)}, u32[]{:S(2)}, u32[]{:S(2)}) collective-permute-start(f32[200,128]{1,0:T(8,128)S(1)} %get-tuple-element.85), channel_id=1, source_target_pairs={{0,224},{32,0},{64,32},{96,64},{128,96},{160,128},{192,160},{224,1... | collective-permute-start | bytes 307208 | tf_op jit(solution)/shard_map/ppermute | solution.py:500
  102.6 4.4 %collective-permute-start.15 = (f32[200,128]{1,0:T(8,128)S(1)}, f32[200,128]{1,0:T(8,128)S(1)}, u32[]{:S(2)}, u32[]{:S(2)}) collective-permute-start(f32[200,128]{1,0:T(8,128)S(1)} %get-tuple-element.86), channel_id=1, source_target_pairs={{0,31},{1,0},{2,1},{3,2},{4,3},{5,4},{6,5},{7,6},{8,7},{9,8},{10,9... | collective-permute-start | bytes 307208 | tf_op jit(solution)/shard_map/ppermute | solution.py:500
  108.2 22.1 %all-to-all-start.5 = ((f32[32,16,256]{2,1,0:T(8,128)}), f32[32,16,256]{2,1,0:T(8,128)S(1)}, u32[]{:S(2)}, u32[]{:S(2)}) async-start(f32[32,16,256]{2,1,0:T(8,128)} %spread_kernel.3), calls=%async_computation.5 | async-start | bytes 1048576 | tf_op jit(solution)/shard_map/all_to_all | solution.py:513
  118.8 40.8 %copy-start.2 = (bf16[4,200,128]{2,1,0:T(8,128)(2,1)S(1)}, bf16[4,200,128]{2,1,0:T(8,128)(2,1)}, u32[]{:S(2)}) copy-start(bf16[4,200,128]{2,1,0:T(8,128)(2,1)} %copy-done.1) | copy-start | bytes 614404
  118.8 40.8 %copy-start.3 = (f32[3,200,128]{2,1,0:T(8,128)S(1)}, f32[3,200,128]{2,1,0:T(8,128)}, u32[]{:S(2)}) copy-start(f32[3,200,128]{2,1,0:T(8,128)} %get-tuple-element.102.refs_2_) | copy-start | bytes 921604
  123.5 0.7 copy-start.4
  131.5 12.7 %all-to-all-start.6 = ((f32[32,8,128]{2,1,0:T(8,128)}), f32[32,8,128]{2,1,0:T(8,128)S(1)}, u32[]{:S(2)}, u32[]{:S(2)}) async-start(f32[32,8,128]{2,1,0:T(8,128)} %get-tuple-element.92), calls=%async_computation.6 | async-start | bytes 262144 | tf_op jit(solution)/shard_map/all_to_all | solution.py:513
  135.4 5.4 %collective-permute-start.16 = (f32[200,128]{1,0:T(8,128)S(1)}, f32[200,128]{1,0:T(8,128)S(1)}, u32[]{:S(2)}, u32[]{:S(2)}) collective-permute-start(f32[200,128]{1,0:T(8,128)S(1)} %get-tuple-element.96), channel_id=1, source_target_pairs={{0,32},{32,64},{64,96},{96,128},{128,160},{160,192},{192,224},{224... | collective-permute-start | bytes 307208 | tf_op jit(solution)/shard_map/ppermute | solution.py:500
  135.8 5.0 %collective-permute-start.17 = (f32[200,128]{1,0:T(8,128)S(1)}, f32[200,128]{1,0:T(8,128)S(1)}, u32[]{:S(2)}, u32[]{:S(2)}) collective-permute-start(f32[200,128]{1,0:T(8,128)S(1)} %get-tuple-element.97), channel_id=1, source_target_pairs={{0,1},{1,2},{2,3},{3,4},{4,5},{5,6},{6,7},{7,8},{8,9},{9,10},{10,1... | collective-permute-start | bytes 307208 | tf_op jit(solution)/shard_map/ppermute | solution.py:500
  137.7 4.2 %collective-permute-start.18 = (f32[200,128]{1,0:T(8,128)S(1)}, f32[200,128]{1,0:T(8,128)S(1)}, u32[]{:S(2)}, u32[]{:S(2)}) collective-permute-start(f32[200,128]{1,0:T(8,128)S(1)} %get-tuple-element.98), channel_id=1, source_target_pairs={{0,224},{32,0},{64,32},{96,64},{128,96},{160,128},{192,160},{224,1... | collective-permute-start | bytes 307208 | tf_op jit(solution)/shard_map/ppermute | solution.py:500
  140.1 4.1 %collective-permute-start.19 = (f32[200,128]{1,0:T(8,128)S(1)}, f32[200,128]{1,0:T(8,128)S(1)}, u32[]{:S(2)}, u32[]{:S(2)}) collective-permute-start(f32[200,128]{1,0:T(8,128)S(1)} %get-tuple-element.99), channel_id=1, source_target_pairs={{0,31},{1,0},{2,1},{3,2},{4,3},{5,4},{6,5},{7,6},{8,7},{9,8},{10,9... | collective-permute-start | bytes 307208 | tf_op jit(solution)/shard_map/ppermute | solution.py:500
